TPU v7x, 32 devices: a whole 2x2x4 slice. The times are simulated.
32 devices in a mesh: dp: 32 (over z, y, x, core).
Axes of the slice: x: 2, y: 2, z: 4, core: 2. Of those that a mesh axis runs over, the one named last changes fastest.
Arguments:
- tokens: bfloat16 [65536, 768], P('dp'), may hold values from -6 to 6
- teacher: bfloat16 [65536, 768], P('dp'), may hold values from -6 to 6
- route_to: int32 [65536], P('dp'), may hold values from 0 to 65535, as said below
- anchor: int32 [65536], P('dp'), may hold values from 0 to 65535, as said below
- seq_lengths: int32 [512], P('dp'), may hold values from 0 to 1024, as said below
- query_weight: bfloat16 [768, 768], P('dp'), may hold values from -0.21875 to 0.21875
- query_bias: bfloat16 [768], P('dp'), may hold values from -3 to 3
- key_weight: bfloat16 [768, 768], P('dp'), may hold values from -0.21875 to 0.21875
- value_weight: bfloat16 [768, 768], P('dp'), may hold values from -0.21875 to 0.21875
- value_bias: bfloat16 [768], P('dp'), may hold values from -3 to 3
- out_weight: bfloat16 [768, 768], P('dp'), may hold values from -1.75 to 1.75
- out_bias: bfloat16 [768], P('dp'), may hold values from -3 to 3
- first_gain: bfloat16 [768], P('dp'), may hold values from 0.5 to 1.5
- first_shift: bfloat16 [768], P('dp'), may hold values from -3 to 3
- up_weight: bfloat16 [768, 3072], P('dp'), may hold values from -0.21875 to 0.21875
- up_bias: bfloat16 [3072], P('dp'), may hold values from -3 to 3
- down_weight: bfloat16 [3072, 768], P('dp'), may hold values from -0.109375 to 0.109375
- down_bias: bfloat16 [768], P('dp'), may hold values from -3 to 3
- second_gain: bfloat16 [768], P('dp'), may hold values from 0.5 to 1.5
- second_shift: bfloat16 [768], P('dp'), may hold values from -3 to 3
Outputs:
- states: bfloat16 [65536, 768], P('dp')
- mse_loss: float32 [], replicated
- token_grad: bfloat16 [65536, 768], P('dp')
- grad_query_weight: float32 [768, 768], P('dp')
- grad_query_bias: float32 [768], P('dp')
- grad_key_weight: float32 [768, 768], P('dp')
- grad_value_weight: float32 [768, 768], P('dp')
- grad_value_bias: float32 [768], P('dp')
- grad_out_weight: float32 [768, 768], P('dp')
- grad_out_bias: float32 [768], P('dp')
- grad_first_gain: float32 [768], P('dp')
- grad_first_shift: float32 [768], P('dp')
- grad_up_weight: float32 [768, 3072], P('dp')
- grad_up_bias: float32 [3072], P('dp')
- grad_down_weight: float32 [3072, 768], P('dp')
- grad_down_bias: float32 [768], P('dp')
- grad_second_gain: float32 [768], P('dp')
- grad_second_shift: float32 [768], P('dp')
Inputs may be any that keep to these rules, and one draw needn't show every extreme that they name: route_to is a permutation of the rows. Rows k * 2048 to (k + 1) * 2048 - 1 of either order belong to device k; the input rows of each device go to exactly 64 routed rows of every device, and the rows that go from one device to another keep their order. anchor is the inverse of route_to: anchor[route_to[i]] = i. `seq_lengths`: in each aligned group of 8 entries (one micro-batch of one device, in order) the lengths of that micro-batch's sequences come first, zeros follow, and the block counts (L + 127) // 128 of the nonzero lengths L sum to 8; some group holds a single sequence of 1024 rows.
All inputs are finite; a program needn't handle non-finite values.
Results may differ from a plain program's by a relative error of at most 0.013.
Values may be sent and summed in bfloat16 or wider, within the bound.
A program may use at most 256 MiB of HBM per device.

v0:
```python
import jax
import jax.numpy as jnp
from jax import lax
from jax.sharding import PartitionSpec as P

HEADS = 12
HEAD_DIM = 64
BLOCK = 128
MB_TOK = 1024


EPSILON = 1e-12


def layer_norm(value, gain, shift):
    center = value - jnp.mean(value, axis=-1, keepdims=True)
    spread = jnp.mean(center * center, axis=-1, keepdims=True)
    return center * lax.rsqrt(spread + EPSILON) * gain + shift


def gelu_exact(value):
    return jax.nn.gelu(value, approximate=False)


def matmul(left, right):
    return jnp.dot(left, right, preferred_element_type=jnp.float32)


def contract_last(left, right):
    return lax.dot_general(
        left, right, (((1,), (1,)), ((), ())), preferred_element_type=jnp.float32
    )


def cross_rows(left, right):
    return lax.dot_general(
        left, right, (((0,), (0,)), ((), ())), preferred_element_type=jnp.float32
    )


def column_sum(value):
    return jnp.sum(value, axis=0, dtype=jnp.float32)


def head_major(rows):
    return rows.reshape(rows.shape[0], HEADS, HEAD_DIM).transpose(1, 0, 2)


def row_major(heads):
    return heads.transpose(1, 0, 2).reshape(heads.shape[1], HEADS * HEAD_DIM)


def sequence_masks(lengths_flat, groups):
    length_grid = lengths_flat.reshape(groups, MB_TOK // BLOCK)
    blocks = (length_grid + BLOCK - 1) // BLOCK
    starts = jnp.cumsum(blocks, axis=1) - blocks
    places = jnp.arange(MB_TOK, dtype=jnp.int32)
    inside = (places[None, :, None] // BLOCK >= starts[:, None, :]) & (blocks[:, None, :] > 0)
    segment = jnp.sum(inside.astype(jnp.int32), axis=2) - 1
    chosen = segment[:, :, None] == jnp.arange(MB_TOK // BLOCK, dtype=jnp.int32)[None, None, :]
    first_row = jnp.sum(jnp.where(chosen, starts[:, None, :], 0), axis=2) * BLOCK
    seq_limit = jnp.sum(jnp.where(chosen, length_grid[:, None, :], 0), axis=2)
    usable = places[None, :] - first_row < seq_limit
    return (segment, usable)


def slot_positions(targets, rows_dev, slot_rows, device_count):
    owner_dev = targets // rows_dev
    onehot = (owner_dev[:, None] == jnp.arange(device_count, dtype=jnp.int32)[None, :]).astype(
        jnp.int32
    )
    ranking = jnp.sum(jnp.cumsum(onehot, axis=0) * onehot, axis=1) - 1
    return owner_dev * slot_rows + ranking


def invert(positions):
    return (
        jnp.zeros_like(positions).at[positions].set(jnp.arange(positions.shape[0], dtype=jnp.int32))
    )


def forward(weights, rows_in, teacher_rows, segment, usable):
    (
        query_weight,
        query_bias,
        key_weight,
        value_weight,
        value_bias,
        out_weight,
        out_bias,
        first_gain,
        first_shift,
        up_weight,
        up_bias,
        down_weight,
        down_bias,
        second_gain,
        second_shift,
    ) = weights
    queries = ((matmul(rows_in, query_weight) + query_bias) * 0.125).astype(jnp.bfloat16)
    key_rows = matmul(rows_in, key_weight).astype(jnp.bfloat16)
    value_rows = (matmul(rows_in, value_weight) + value_bias).astype(jnp.bfloat16)
    allowed = (segment[:, None] == segment[None, :]) & usable[None, :]

    def head_forward(head_inputs):
        head_query, head_key, head_value = head_inputs
        scores = jnp.where(allowed, contract_last(head_query, head_key), -1e30)
        row_max = jnp.max(scores, axis=1, keepdims=True)
        exp_scores = jnp.exp(scores - row_max)
        row_total = jnp.sum(exp_scores, axis=1, keepdims=True)
        attn_probs = exp_scores / row_total
        log_total = (row_max + jnp.log(row_total))[:, 0]
        head_out = matmul(attn_probs.astype(jnp.bfloat16), head_value).astype(jnp.bfloat16)
        return (head_out, log_total)

    head_out, log_total = lax.map(
        head_forward, (head_major(queries), head_major(key_rows), head_major(value_rows))
    )
    attended = row_major(head_out)
    pre_first = rows_in + (matmul(attended, out_weight) + out_bias)
    hidden, pull_first = jax.vjp(
        layer_norm, pre_first, first_gain.astype(jnp.float32), first_shift.astype(jnp.float32)
    )
    hidden_low = hidden.astype(jnp.bfloat16)
    pre_act = matmul(hidden_low, up_weight) + up_bias
    activated, pull_gelu = jax.vjp(gelu_exact, pre_act)
    act_low = activated.astype(jnp.bfloat16)
    pre_second = hidden + (matmul(act_low, down_weight) + down_bias)
    layer_out, pull_second = jax.vjp(
        layer_norm, pre_second, second_gain.astype(jnp.float32), second_shift.astype(jnp.float32)
    )
    misfit = jnp.where(usable[:, None], layer_out - teacher_rows.astype(jnp.float32), 0.0)
    kept = (
        queries,
        key_rows,
        value_rows,
        log_total,
        attended,
        hidden_low,
        act_low,
        pull_first,
        pull_gelu,
        pull_second,
        allowed,
    )
    return (layer_out, misfit, kept)


def backward(weights, kept, rows_in, grad_out):
    query_weight = weights[0]
    key_weight = weights[2]
    value_weight = weights[3]
    out_weight = weights[5]
    up_weight = weights[9]
    down_weight = weights[11]
    (
        queries,
        key_rows,
        value_rows,
        log_total,
        attended,
        hidden_low,
        act_low,
        pull_first,
        pull_gelu,
        pull_second,
        allowed,
    ) = kept
    grad_pre_second, grad_second_gain, grad_second_shift = pull_second(grad_out)
    down_grad = grad_pre_second.astype(jnp.bfloat16)
    grad_down_weight = cross_rows(act_low, down_grad)
    grad_down_bias = column_sum(down_grad)
    grad_activated = contract_last(down_grad, down_weight)
    up_grad = pull_gelu(grad_activated)[0].astype(jnp.bfloat16)
    grad_up_weight = cross_rows(hidden_low, up_grad)
    grad_up_bias = column_sum(up_grad)
    grad_hidden = grad_pre_second + contract_last(up_grad, up_weight)
    grad_pre_first, grad_first_gain, grad_first_shift = pull_first(grad_hidden)
    out_grad = grad_pre_first.astype(jnp.bfloat16)
    grad_out_weight = cross_rows(attended, out_grad)
    grad_out_bias = column_sum(out_grad)
    attended_grad = contract_last(out_grad, out_weight).astype(jnp.bfloat16)

    def head_backward(head_inputs):
        head_query, head_key, head_value, head_grad, head_log = head_inputs
        scores = contract_last(head_query, head_key)
        attn_probs = jnp.where(allowed, jnp.exp(scores - head_log[:, None]), 0.0)
        grad_probs = contract_last(head_grad, head_value)
        centre = jnp.sum(attn_probs * grad_probs, axis=1, keepdims=True)
        grad_scores = (attn_probs * (grad_probs - centre)).astype(jnp.bfloat16)
        query_part = matmul(grad_scores, head_key).astype(jnp.bfloat16)
        key_part = cross_rows(grad_scores, head_query).astype(jnp.bfloat16)
        value_part = cross_rows(attn_probs.astype(jnp.bfloat16), head_grad).astype(jnp.bfloat16)
        return (query_part, key_part, value_part)

    query_heads, key_heads, value_heads = lax.map(
        head_backward,
        (
            head_major(queries),
            head_major(key_rows),
            head_major(value_rows),
            head_major(attended_grad),
            log_total,
        ),
    )
    query_grad = row_major(query_heads) * 0.125
    key_grad = row_major(key_heads)
    value_grad = row_major(value_heads)
    grad_query_weight = cross_rows(rows_in, query_grad)
    grad_query_bias = column_sum(query_grad)
    grad_key_weight = cross_rows(rows_in, key_grad)
    grad_value_weight = cross_rows(rows_in, value_grad)
    grad_value_bias = column_sum(value_grad)
    rows_grad = (
        grad_pre_first
        + contract_last(query_grad, query_weight)
        + contract_last(key_grad, key_weight)
        + contract_last(value_grad, value_weight)
    )
    grads = (
        grad_query_weight,
        grad_query_bias,
        grad_key_weight,
        grad_value_weight,
        grad_value_bias,
        grad_out_weight,
        grad_out_bias,
        grad_first_gain,
        grad_first_shift,
        grad_up_weight,
        grad_up_bias,
        grad_down_weight,
        grad_down_bias,
        grad_second_gain,
        grad_second_shift,
    )
    return (rows_grad.astype(jnp.bfloat16), grads)


def on_device(
    tokens,
    teacher,
    route_to,
    anchor,
    seq_lengths,
    query_weight,
    query_bias,
    key_weight,
    value_weight,
    value_bias,
    out_weight,
    out_bias,
    first_gain,
    first_shift,
    up_weight,
    up_bias,
    down_weight,
    down_bias,
    second_gain,
    second_shift,
):
    rows_dev, model_width = tokens.shape
    device_count = lax.axis_size("dp")
    slot_rows = rows_dev // device_count
    micro_count = rows_dev // MB_TOK
    outgoing = slot_positions(route_to, rows_dev, slot_rows, device_count)
    incoming = slot_positions(anchor, rows_dev, slot_rows, device_count)
    send_order = invert(outgoing)
    arrived_rows, arrived_teacher = (
        lax.all_to_all(
            tokens[send_order].reshape(device_count, slot_rows, model_width),
            "dp",
            split_axis=0,
            concat_axis=0,
            tiled=True,
        ),
        lax.all_to_all(
            teacher[send_order].reshape(device_count, slot_rows, model_width),
            "dp",
            split_axis=0,
            concat_axis=0,
            tiled=True,
        ),
    )
    routed_rows = arrived_rows.reshape(rows_dev, model_width)[incoming]
    routed_teacher = arrived_teacher.reshape(rows_dev, model_width)[incoming]
    segment, usable = sequence_masks(seq_lengths, micro_count)
    valid_count = lax.psum(jnp.sum(usable.astype(jnp.float32)), "dp")
    loss_scale = rows_dev * device_count * 2.0 / valid_count
    squares = jnp.zeros((), jnp.float32)
    state_pieces = []
    grad_pieces = []
    totals = None
    for micro_index in range(micro_count):
        rows_in = routed_rows[micro_index * MB_TOK : (micro_index + 1) * MB_TOK]
        teacher_rows = routed_teacher[micro_index * MB_TOK : (micro_index + 1) * MB_TOK]
        gathered = (
            lax.all_gather(query_weight, "dp", axis=0, tiled=True),
            lax.all_gather(query_bias, "dp", axis=0, tiled=True),
            lax.all_gather(key_weight, "dp", axis=0, tiled=True),
            lax.all_gather(value_weight, "dp", axis=0, tiled=True),
            lax.all_gather(value_bias, "dp", axis=0, tiled=True),
            lax.all_gather(out_weight, "dp", axis=0, tiled=True),
            lax.all_gather(out_bias, "dp", axis=0, tiled=True),
            lax.all_gather(first_gain, "dp", axis=0, tiled=True),
            lax.all_gather(first_shift, "dp", axis=0, tiled=True),
            lax.all_gather(up_weight, "dp", axis=0, tiled=True),
            lax.all_gather(up_bias, "dp", axis=0, tiled=True),
            lax.all_gather(down_weight, "dp", axis=0, tiled=True),
            lax.all_gather(down_bias, "dp", axis=0, tiled=True),
            lax.all_gather(second_gain, "dp", axis=0, tiled=True),
            lax.all_gather(second_shift, "dp", axis=0, tiled=True),
        )
        layer_out, misfit, kept = forward(
            gathered, rows_in, teacher_rows, segment[micro_index], usable[micro_index]
        )
        squares = squares + jnp.sum(misfit * misfit)
        back_weights = (
            lax.all_gather(query_weight, "dp", axis=0, tiled=True),
            lax.all_gather(query_bias, "dp", axis=0, tiled=True),
            lax.all_gather(key_weight, "dp", axis=0, tiled=True),
            lax.all_gather(value_weight, "dp", axis=0, tiled=True),
            lax.all_gather(value_bias, "dp", axis=0, tiled=True),
            lax.all_gather(out_weight, "dp", axis=0, tiled=True),
            lax.all_gather(out_bias, "dp", axis=0, tiled=True),
            lax.all_gather(first_gain, "dp", axis=0, tiled=True),
            lax.all_gather(first_shift, "dp", axis=0, tiled=True),
            lax.all_gather(up_weight, "dp", axis=0, tiled=True),
            lax.all_gather(up_bias, "dp", axis=0, tiled=True),
            lax.all_gather(down_weight, "dp", axis=0, tiled=True),
            lax.all_gather(down_bias, "dp", axis=0, tiled=True),
            lax.all_gather(second_gain, "dp", axis=0, tiled=True),
            lax.all_gather(second_shift, "dp", axis=0, tiled=True),
        )
        rows_grad, grads = backward(back_weights, kept, rows_in, misfit * loss_scale)
        if micro_index == 0:
            totals = grads
        else:
            totals = jax.tree.map(jnp.add, totals, grads)
        state_pieces.append(layer_out.astype(jnp.bfloat16))
        grad_pieces.append(rows_grad)
    shares = (
        lax.psum_scatter(totals[0], "dp", scatter_dimension=0, tiled=True),
        lax.psum_scatter(totals[1], "dp", scatter_dimension=0, tiled=True),
        lax.psum_scatter(totals[2], "dp", scatter_dimension=0, tiled=True),
        lax.psum_scatter(totals[3], "dp", scatter_dimension=0, tiled=True),
        lax.psum_scatter(totals[4], "dp", scatter_dimension=0, tiled=True),
        lax.psum_scatter(totals[5], "dp", scatter_dimension=0, tiled=True),
        lax.psum_scatter(totals[6], "dp", scatter_dimension=0, tiled=True),
        lax.psum_scatter(totals[7], "dp", scatter_dimension=0, tiled=True),
        lax.psum_scatter(totals[8], "dp", scatter_dimension=0, tiled=True),
        lax.psum_scatter(totals[9], "dp", scatter_dimension=0, tiled=True),
        lax.psum_scatter(totals[10], "dp", scatter_dimension=0, tiled=True),
        lax.psum_scatter(totals[11], "dp", scatter_dimension=0, tiled=True),
        lax.psum_scatter(totals[12], "dp", scatter_dimension=0, tiled=True),
        lax.psum_scatter(totals[13], "dp", scatter_dimension=0, tiled=True),
        lax.psum_scatter(totals[14], "dp", scatter_dimension=0, tiled=True),
    )
    mse_loss = lax.psum(squares, "dp") / valid_count
    routed_states = jnp.concatenate(state_pieces, axis=0)
    routed_grad = jnp.concatenate(grad_pieces, axis=0)
    back_order = invert(incoming)
    sent_states, sent_grads = (
        lax.all_to_all(
            routed_states[back_order].reshape(device_count, slot_rows, model_width),
            "dp",
            split_axis=0,
            concat_axis=0,
            tiled=True,
        ),
        lax.all_to_all(
            routed_grad[back_order].reshape(device_count, slot_rows, model_width),
            "dp",
            split_axis=0,
            concat_axis=0,
            tiled=True,
        ),
    )
    states = sent_states.reshape(rows_dev, model_width)[outgoing]
    token_grad = sent_grads.reshape(rows_dev, model_width)[outgoing]
    return (
        states,
        mse_loss,
        token_grad,
        shares[0],
        shares[1],
        shares[2],
        shares[3],
        shares[4],
        shares[5],
        shares[6],
        shares[7],
        shares[8],
        shares[9],
        shares[10],
        shares[11],
        shares[12],
        shares[13],
        shares[14],
    )


def solution(mesh):
    placed = (
        P("dp", None),
        P("dp", None),
        P("dp"),
        P("dp"),
        P("dp"),
        P("dp", None),
        P("dp"),
        P("dp", None),
        P("dp", None),
        P("dp"),
        P("dp", None),
        P("dp"),
        P("dp"),
        P("dp"),
        P("dp", None),
        P("dp"),
        P("dp", None),
        P("dp"),
        P("dp"),
        P("dp"),
    )
    return jax.shard_map(
        on_device,
        mesh=mesh,
        in_specs=placed,
        out_specs=(
            P("dp", None),
            P(),
            P("dp", None),
            P("dp", None),
            P("dp"),
            P("dp", None),
            P("dp", None),
            P("dp"),
            P("dp", None),
            P("dp"),
            P("dp"),
            P("dp"),
            P("dp", None),
            P("dp"),
            P("dp", None),
            P("dp"),
            P("dp"),
            P("dp"),
        ),
        check_vma=False,
    )
```

profile of v0, /device:TPU:0, one launch (start us, length us, event | category | flops | bytes accessed | tf_op | source)
XLA Modules:
  0.0 1741.7 jit_solution(3361099373734668195)
XLA Ops:
  12.0 15.9 reduce-window.14
  58.4 97.2 %psum.15 = f32[]{:T(128)} all-reduce(f32[]{:T(128)} %get-tuple-element.435), channel_id=1, replica_groups=mesh['dp'=32] {'dp'}, use_global_device_ids=true, to_apply=%region_32.33 | all-reduce | flops 1 | bytes 8 | tf_op jit(solution)/shard_map/psum | solution.py:288
  157.7 38.8 %all-reduce.19 = (bf16[768]{0:T(1024)(128)(2,1)S(1)}, bf16[768]{0:T(1024)(128)(2,1)S(1)}, bf16[768]{0:T(1024)(128)(2,1)S(1)}, bf16[768]{0:T(1024)(128)(2,1)S(1)}...) all-reduce(bf16[768]{0:T(1024)(128)(2,1)S(1)} %dynamic-update-slice, ...), channel_id=1, replica_groups=mesh['dp'=32] {'dp'}, use_global_device_ids=true, to_apply=%add | all-reduce | flops 9216 | bytes 36864
  197.2 15.9 reduce-window.16
  217.8 12.4 gather_fusion.4
  239.3 12.8 gather_fusion.1
  278.8 126.2 %while.56 = (s32[]{:T(128)}, bf16[12,1024,64]{1,2,0:T(8,128)(2,1)}, f32[12,1024]{1,0:T(8,128)S(1)}, bf16[12,1024,64]{2,1,0:T(8,128)(2,1)}, bf16[12,1024,64]{2,1,...) while((s32[]{:T(128)}, bf16[12,1024,64]{1,2,0:T(8,128)(2,1)}, ...), condition=%wide.region_14.15_spmd.clone, body=%wide.region_11.14_spmd.clone.sunk | while | flops 284228608 | bytes 30344324 | solution.py:116
  432.1 126.0 %while.57 = (s32[]{:T(128)}, bf16[12,1024,64]{1,2,0:T(8,128)(2,1)}, f32[12,1024]{1,0:T(8,128)S(1)}, bf16[12,1024,64]{2,1,0:T(8,128)(2,1)}, bf16[12,1024,64]{2,1,...) while((s32[]{:T(128)}, bf16[12,1024,64]{1,2,0:T(8,128)(2,1)}, ...), condition=%wide.region_22.23_spmd.clone, body=%wide.region_19.22_spmd.clone.sunk | while | flops 284228608 | bytes 30344324 | solution.py:116
  591.1 63.4 %multiply_convert_fusion.3 = (bf16[1024,3072]{1,0:T(8,128)(2,1)}, f32[1024,3072]{1,0:T(8,128)}, bf16[1024,3072]{1,0:T(8,128)(2,1)}, f32[1024,3072]{1,0:T(8,128)}, f32[1024,3072]{1,0:T(8,128)}) fusion(f32[3072]{0:T(1024)S(1)} %copy-done.88, f32[1024,3072]{1,0:T(8,128)S(1)} %fusion.167, bf16[768,3072]{1,0:T(8,128)(2,1)S(1)} %copy-done.96, ...), kind=kOutput, calls=%fused_computation.145 | convolution fusion | flops 5251006464 | bytes 70805504 | tf_op jit(solution)/shard_map/dot_general | solution.py:26
  688.0 18.7 %convert_reduce_fusion.1 = (f32[3072]{0:T(1024)}, bf16[1024,3072]{1,0:T(8,128)(2,1)}) fusion(f32[1024,3072]{1,0:T(8,128)} %get-tuple-element.440, bf16[1024,768]{1,0:T(8,128)(2,1)} %get-tuple-element.420, bf16[3072,768]{1,0:T(8,128)(2,1)} %all-gather.17.cloned.1.call-done, f32[1024,3072]{1,0:T(8,128)} %get-tuple-element.482, f32[3072]{0:T(1024)S(1)} %copy-done.88), kind=kOutput, calls=%fused_computation.129 | convolution fusion | flops 4885312512 | bytes 37773312 | tf_op jit(solution)/shard_map/dot_general | solution.py:30
  706.7 10.4 add_add_fusion.9
  717.1 18.8 %convert_reduce_fusion = (f32[3072]{0:T(1024)}, bf16[1024,3072]{1,0:T(8,128)(2,1)}) fusion(f32[1024,3072]{1,0:T(8,128)} %get-tuple-element.464, bf16[1024,768]{1,0:T(8,128)(2,1)} %get-tuple-element.418, bf16[3072,768]{1,0:T(8,128)(2,1)} %all-gather.17.cloned.1.call-done, f32[1024,3072]{1,0:T(8,128)} %copy-done.110, f32[3072]{0:T(1024)S(1)} %copy-done.88), kind=kOutput, calls=%fused_computation.128 | convolution fusion | flops 4885312512 | bytes 37773312 | tf_op jit(solution)/shard_map/dot_general | solution.py:30
  735.9 12.1 multiply_reduce_fusion.4
  770.2 164.7 %while.59 = (s32[]{:T(128)}, bf16[12,1024,64]{1,2,0:T(8,128)(2,1)}, bf16[12,1024,64]{1,2,0:T(8,128)(2,1)}, bf16[12,1024,64]{1,2,0:T(8,128)(2,1)}, bf16[12,1024,6...) while((s32[]{:T(128)}, bf16[12,1024,64]{1,2,0:T(8,128)(2,1)}, ...), condition=%wide.region_46.47_spmd.clone, body=%wide.region_44.46_spmd.clone.sunk | while | flops 681769984 | bytes 46303408 | solution.py:196
  946.5 165.1 %while.58 = (s32[]{:T(128)}, bf16[12,1024,64]{1,2,0:T(8,128)(2,1)}, bf16[12,1024,64]{1,2,0:T(8,128)(2,1)}, bf16[12,1024,64]{1,2,0:T(8,128)(2,1)}, bf16[12,1024,6...) while((s32[]{:T(128)}, bf16[12,1024,64]{1,2,0:T(8,128)(2,1)}, ...), condition=%wide.region_39.40_spmd.clone, body=%wide.region_37.39_spmd.clone.sunk | while | flops 681769984 | bytes 46303408 | solution.py:196
  1140.7 10.7 convolution_add_fusion
  1168.2 11.5 convolution_add_fusion.1
  1216.0 12.4 gather_fusion.2
  1228.4 58.9 %all-to-all-done.3 = bf16[32,64,768]{2,1,0:T(8,128)(2,1)S(1)} async-done(((bf16[32,64,768]{2,1,0:T(8,128)(2,1)}), bf16[32,64,768]{2,1,0:T(8,128)(2,1)S(1)}, u32[]{:S(2)}, u32[]{:S(2)}) %all-to-all-start.3) | async-done | bytes 3145760 | tf_op jit(solution)/shard_map/all_to_all | solution.py:371
  1301.2 87.7 %all-reduce.18 = (f32[]{:T(128)}, f32[768]{0:T(1024)S(1)}, f32[768]{0:T(1024)S(1)}, f32[768]{0:T(1024)S(1)}, f32[768]{0:T(1024)S(1)}, /*index=5*/f32[768]{0:T(10...) all-reduce(f32[]{:T(128)S(6)} %add.409, ...), channel_id=1, replica_groups=mesh['dp'=32] {'dp'}, use_global_device_ids=true, to_apply=%region_30.31 | all-reduce | flops 9217 | bytes 73736 | tf_op jit(solution)/shard_map/psum | solution.py:359
  1404.9 12.5 gather_fusion.3
  1417.4 32.7 %reduce-scatter.7.cloned.1.call-done = f32[24,768]{1,0:T(8,128)} async-done(((f32[768,768]{1,0:T(8,128)}), f32[24,768]{1,0:T(8,128)}) %reduce-scatter.7.cloned.1.call-update) | async-done | bytes 73744 | tf_op jit(solution)/shard_map/reduce_scatter | solution.py:343
  1450.1 141.7 %reduce-scatter.17.cloned.1.call-done = f32[96,768]{1,0:T(8,128)} async-done(((f32[3072,768]{1,0:T(8,128)}), f32[96,768]{1,0:T(8,128)}) %reduce-scatter.17.cloned.1.call-update) | async-done | bytes 294928 | tf_op jit(solution)/shard_map/reduce_scatter | solution.py:354
  1591.8 141.4 %reduce-scatter.15.cloned.1.call-done = f32[24,3072]{1,0:T(8,128)} async-done(((f32[768,3072]{1,0:T(8,128)}), f32[24,3072]{1,0:T(8,128)}) %reduce-scatter.15.cloned.1.call-update) | async-done | bytes 294928 | tf_op jit(solution)/shard_map/reduce_scatter | solution.py:352
  (857 shorter events, 892.8 us)
Async XLA Ops:
  7.2 245.0 %all-gather.7.cloned.1.call-start = ((), (), s32[]{:S(2)}) async-start(), calls=%async_computation.10 | async-start | bytes 1216512 | tf_op jit(solution)/shard_map/all_gather | solution.py:298
  7.9 252.7 %all-gather.11.cloned.1.call-start = ((), (), s32[]{:S(2)}) async-start(), calls=%async_computation.12 | async-start | bytes 1216512 | tf_op jit(solution)/shard_map/all_gather | solution.py:301
  8.7 260.3 %all-gather.9.cloned.1.call-start = ((), (), s32[]{:S(2)}) async-start(), calls=%async_computation.11 | async-start | bytes 1216512 | tf_op jit(solution)/shard_map/all_gather | solution.py:300
  9.4 548.7 %all-gather.13.cloned.1.call-start = ((), (), s32[]{:S(2)}) async-start(), calls=%async_computation.13 | async-start | bytes 1216512 | tf_op jit(solution)/shard_map/all_gather | solution.py:303
  10.0 568.1 %all-gather.15.cloned.1.call-start = ((), (), s32[]{:S(2)}) async-start(), calls=%async_computation.14 | async-start | bytes 4866048 | tf_op jit(solution)/shard_map/all_gather | solution.py:307
  49.3 107.9 %copy-start.108 = (bf16[24]{0:T(256)(128)(2,1)S(1)}, bf16[24]{0:T(256)(128)(2,1)}, u32[]{:S(2)}) copy-start(bf16[24]{0:T(256)(128)(2,1)} %param.47) | copy-start | bytes 148
  49.3 108.1 %copy-start.109 = (bf16[96]{0:T(256)(128)(2,1)S(1)}, bf16[96]{0:T(256)(128)(2,1)}, u32[]{:S(2)}) copy-start(bf16[96]{0:T(256)(128)(2,1)} %param.43) | copy-start | bytes 580
  49.3 147.2 %copy-start.78 = (s32[2048]{0:T(1024)S(1)}, s32[2048]{0:T(1024)}, u32[]{:S(2)}) copy-start(s32[2048]{0:T(1024)} %param.31) | copy-start | bytes 24580
  49.3 182.5 %all-to-all-start = ((bf16[32,64,768]{2,1,0:T(8,128)(2,1)}), bf16[32,64,768]{2,1,0:T(8,128)(2,1)S(1)}, u32[]{:S(2)}, u32[]{:S(2)}) async-start(bf16[32,64,768]{2,1,0:T(8,128)(2,1)} %bitcast.331), calls=%async_computation | async-start | bytes 6291456 | tf_op jit(solution)/shard_map/all_to_all | solution.py:270
  56.6 597.8 %all-gather.17.cloned.1.call-start = ((), (), s32[]{:S(2)}) async-start(), calls=%async_computation.15 | async-start | bytes 4866048 | tf_op jit(solution)/shard_map/all_gather | solution.py:309
  215.4 532.6 %copy-start.47 = (f32[768]{0:T(1024)}, f32[768]{0:T(1024)S(1)}, u32[]{:S(2)}) copy-start(f32[768]{0:T(1024)S(1)} %convert_element_type.218) | copy-start | bytes 9220
  215.4 449.6 %copy-start.49 = (f32[768]{0:T(1024)}, f32[768]{0:T(1024)S(1)}, u32[]{:S(2)}) copy-start(f32[768]{0:T(1024)S(1)} %convert_element_type.219) | copy-start | bytes 9220
  233.5 335.1 %all-to-all-start.2 = ((bf16[32,64,768]{2,1,0:T(8,128)(2,1)}), bf16[32,64,768]{2,1,0:T(8,128)(2,1)S(1)}, u32[]{:S(2)}, u32[]{:S(2)}) async-start(bf16[32,64,768]{2,1,0:T(8,128)(2,1)} %bitcast.330), calls=%async_computation.2 | async-start | bytes 6291456 | tf_op jit(solution)/shard_map/all_to_all | solution.py:277
  239.3 1178.1 %reduce-scatter.13.cloned.1.call-start = ((), (), s32[]{:S(2)}) async-start(), calls=%async_computation.19 | async-start | bytes 2433024 | tf_op jit(solution)/shard_map/reduce_scatter | solution.py:348
  562.3 185.8 %copy-start.51 = (f32[1024]{0:T(1024)}, f32[1024]{0:T(1024)S(1)}, u32[]{:S(2)}) copy-start(f32[1024]{0:T(1024)S(1)} %broadcast_multiply_fusion.5) | copy-start | bytes 12292
  562.8 185.2 %copy-start.56 = (f32[1024]{0:T(1024)}, f32[1024]{0:T(1024)S(1)}, u32[]{:S(2)}) copy-start(f32[1024]{0:T(1024)S(1)} %fusion.160) | copy-start | bytes 12292
  758.9 658.5 %reduce-scatter.11.cloned.1.call-start = ((), (), s32[]{:S(2)}) async-start(), calls=%async_computation.18 | async-start | bytes 2433024 | tf_op jit(solution)/shard_map/reduce_scatter | solution.py:346
  1119.5 298.0 %reduce-scatter.9.cloned.1.call-start = ((), (), s32[]{:S(2)}) async-start(), calls=%async_computation.17 | async-start | bytes 2433024 | tf_op jit(solution)/shard_map/reduce_scatter | solution.py:345
  1125.5 324.6 %reduce-scatter.7.cloned.1.call-start = ((), (), s32[]{:S(2)}) async-start(), calls=%async_computation.16 | async-start | bytes 2433024 | tf_op jit(solution)/shard_map/reduce_scatter | solution.py:343
  1132.9 459.0 %reduce-scatter.17.cloned.1.call-start = ((), (), s32[]{:S(2)}) async-start(), calls=%async_computation.21 | async-start | bytes 9732096 | tf_op jit(solution)/shard_map/reduce_scatter | solution.py:354
  1151.5 581.8 %reduce-scatter.15.cloned.1.call-start = ((), (), s32[]{:S(2)}) async-start(), calls=%async_computation.20 | async-start | bytes 9732096 | tf_op jit(solution)/shard_map/reduce_scatter | solution.py:352
  1206.4 80.8 %all-to-all-start.3 = ((bf16[32,64,768]{2,1,0:T(8,128)(2,1)}), bf16[32,64,768]{2,1,0:T(8,128)(2,1)S(1)}, u32[]{:S(2)}, u32[]{:S(2)}) async-start(bf16[32,64,768]{2,1,0:T(8,128)(2,1)} %bitcast.333), calls=%async_computation.3 | async-start | bytes 6291456 | tf_op jit(solution)/shard_map/all_to_all | solution.py:371
  1287.3 117.6 %all-to-all-start.1 = ((bf16[32,64,768]{2,1,0:T(8,128)(2,1)}), bf16[32,64,768]{2,1,0:T(8,128)(2,1)}, u32[]{:S(2)}, u32[]{:S(2)}) async-start(bf16[32,64,768]{2,1,0:T(8,128)(2,1)} %bitcast.332), calls=%async_computation.1 | async-start | bytes 6291456 | tf_op jit(solution)/shard_map/all_to_all | solution.py:364
  1404.9 328.4 %copy-start.1 = (bf16[2048,768]{1,0:T(8,128)(2,1)S(1)}, bf16[2048,768]{1,0:T(8,128)(2,1)}, u32[]{:S(2)}) copy-start(bf16[2048,768]{1,0:T(8,128)(2,1)} %param.28) | copy-start | bytes 9437188
  (173 other events, 1685.4 us)
Sparse Core Ops, SparseCore 0:
  10.9 57.8 all-gather.6
  71.7 66.3 all-gather.10
  141.0 53.7 all-gather.8
  197.6 53.9 all-gather.12
  254.3 81.6 all-gather.14
  338.8 62.7 all-gather.16
  759.1 100.8 reduce-scatter.12
  1119.6 101.0 reduce-scatter.10
  1226.6 116.6 reduce-scatter.8
  1349.0 101.0 reduce-scatter.6
  1456.6 135.1 reduce-scatter.16
  1598.1 135.0 reduce-scatter.14
where the time goes:
time: 1760 us; the launch traced here: 1740 us
  matrix products  710 us (40%)
  waiting for transfers between devices  379 us (22%)
  local copies, waits for them, and re-layouts  245 us (14%)
  blocking collectives  224 us (13%)
  other arithmetic  137 us (8%)
  starting transfers between devices  24.5 us (1%)
  between operations  20.8 us (1%)
    dot_general x60, matrix products, matmul(): return jnp.dot(left, right, preferred_element_type=jnp.float32)  278 us
    dot_general x84, matrix products, contract_last(): lax.dot_general(left, right, (((1,), (1,)), ((), ())), preferred_element_...  253 us
    dot_general x60, matrix products, cross_rows(): lax.dot_general(left, right, (((0,), (0,)), ((), ())), preferred_element_...  178 us
    reduce_scatter x1, waiting for transfers between devices, on_device(): lax.psum_scatter(totals[11], 'dp', scatter_dimension=0, tiled=True)  142 us
    reduce_scatter x1, waiting for transfers between devices, on_device(): lax.psum_scatter(totals[9], 'dp', scatter_dimension=0, tiled=True)  141 us
    psum x1, blocking collectives, on_device(): valid_count = lax.psum(jnp.sum(usable.astype(jnp.float32)), 'dp')  97.2 us
    psum x1, blocking collectives, on_device(): mse_loss = lax.psum(squares, 'dp') / valid_count  87.7 us
    all_to_all x1, waiting for transfers between devices, on_device(): lax.all_to_all(routed_grad[back_order].reshape(device_count, slot_rows, m...  58.9 us
  transfers between devices with their start and end apart: 16, of which 4 were waited for; matrix products, arithmetic and copies ran while one was open for 53% of the time, Pallas kernels for 0%

commit v1 on v0

v1 whole, which is shorter than its diff:
```python
import functools

import jax
import jax.numpy as jnp
from jax import lax
from jax.experimental import pallas as pl
from jax.experimental.pallas import tpu as pltpu
from jax.sharding import PartitionSpec as P

HEADS = 12
HEAD_DIM = 64
PAIRS = HEADS // 2
LANES = 2 * HEAD_DIM
BLOCK = 128
MB_TOK = 1024
SEQS = MB_TOK // BLOCK
TILE = 256
EPSILON = 1e-12
NEG = -1e30
F32 = jnp.float32
BF16 = jnp.bfloat16


def matmul(left, right):
    return jnp.dot(left, right, preferred_element_type=F32)


def contract_last(left, right):
    return lax.dot_general(left, right, (((1,), (1,)), ((), ())), preferred_element_type=F32)


def cross_rows(left, right):
    return lax.dot_general(left, right, (((0,), (0,)), ((), ())), preferred_element_type=F32)


def column_sum(value):
    return jnp.sum(value, axis=0, dtype=F32)


def sequence_tables(lengths_flat, groups):
    length_grid = lengths_flat.reshape(groups, SEQS)
    blocks = (length_grid + BLOCK - 1) // BLOCK
    before = jnp.arange(SEQS)[:, None] > jnp.arange(SEQS)[None, :]
    starts = jnp.sum(jnp.where(before[None], blocks[:, None, :], 0), axis=2)
    places = jnp.arange(MB_TOK, dtype=jnp.int32)[None, :, None]
    first = (starts * BLOCK)[:, None, :]
    member = (places >= first) & (places < ((starts + blocks) * BLOCK)[:, None, :])
    live = (places >= first) & (places < first + length_grid[:, None, :])
    usable = jnp.any(live, axis=2)
    pad = ((0, 0), (0, 0), (0, HEAD_DIM - SEQS))
    asked = jnp.pad(member.astype(BF16), pad)
    barred = jnp.pad(jnp.where(live, 0.0, NEG).astype(BF16), pad)
    asked = jnp.concatenate([asked, asked], axis=2)
    barred = jnp.concatenate([barred, barred], axis=2)
    rows = groups * MB_TOK
    return asked.reshape(rows, LANES), barred.reshape(rows, LANES), usable.reshape(rows)


def low_half(shape):
    return lax.broadcasted_iota(jnp.int32, shape, 1) < HEAD_DIM


def attend_kernel(q_ref, k_ref, v_ref, asked_ref, barred_ref, out_ref, lse_ref):
    full = low_half((MB_TOK, LANES))
    tile_half = low_half((TILE, LANES))
    ones = jnp.ones((MB_TOK, LANES), BF16)
    keys = k_ref[...]
    barred = barred_ref[...]
    values = v_ref[...]
    keys_of = (jnp.where(full, keys, barred), jnp.where(full, barred, keys))
    values_of = (jnp.where(full, values, ones), jnp.where(full, ones, values))
    for step in range(MB_TOK // TILE):
        rows = pl.ds(step * TILE, TILE)
        queries = q_ref[rows, :]
        asked = asked_ref[rows, :]
        outs = []
        logs = []
        for side in range(2):
            if side == 0:
                query = jnp.where(tile_half, queries, asked)
            else:
                query = jnp.where(tile_half, asked, queries)
            scores = contract_last(query, keys_of[side])
            peak = jnp.max(scores, axis=1, keepdims=True)
            probs = jnp.exp(scores - peak).astype(BF16)
            mixed = matmul(probs, values_of[side])
            total = pltpu.roll(mixed, HEAD_DIM, 1)
            outs.append(mixed / total)
            both = jnp.where(tile_half, total, mixed) if side == 0 else jnp.where(tile_half, mixed, total)
            logs.append(peak + jnp.log(both))
        out_ref[rows, :] = jnp.where(tile_half, outs[0], outs[1]).astype(BF16)
        logs = jnp.where(tile_half, logs[0], logs[1]).T
        lse_ref[0, 0, 0:8, rows] = logs[0:8, :]
        lse_ref[0, 0, 8:16, rows] = logs[HEAD_DIM:HEAD_DIM + 8, :]


def attend(queries, keys, values, asked, barred):
    rows = queries.shape[0]
    micro = rows // MB_TOK
    wide = pl.BlockSpec((MB_TOK, LANES), lambda m, p: (m, p))
    side = pl.BlockSpec((MB_TOK, LANES), lambda m, p: (m, 0))
    return pl.pallas_call(
        attend_kernel,
        grid=(micro, PAIRS),
        in_specs=[wide, wide, wide, side, side],
        out_specs=[wide, pl.BlockSpec((1, 1, 16, MB_TOK), lambda m, p: (m, p, 0, 0))],
        out_shape=(
            jax.ShapeDtypeStruct(queries.shape, BF16),
            jax.ShapeDtypeStruct((micro, PAIRS, 16, MB_TOK), F32),
        ),
        compiler_params=pltpu.CompilerParams(vmem_limit_bytes=56 << 20),
        cost_estimate=pl.CostEstimate(
            flops=4 * rows * MB_TOK * HEADS * HEAD_DIM,
            transcendentals=rows * MB_TOK * HEADS,
            bytes_accessed=rows * 768 * 8,
        ),
        name="attend",
    )(queries, keys, values, asked, barred)


def attend_back_kernel(q_ref, k_ref, v_ref, g_ref, lse_ref, asked_ref, barred_ref, dq_ref, dk_ref, dv_ref, acc_k, acc_v):
    full = low_half((MB_TOK, LANES))
    tile_half = low_half((TILE, LANES))
    keys = k_ref[...]
    barred = barred_ref[...]
    values = v_ref[...]
    zero = jnp.zeros_like(values)
    keys_of = (jnp.where(full, keys, barred), jnp.where(full, barred, keys))
    values_of = (jnp.where(full, values, zero), jnp.where(full, zero, values))
    keys_turned = keys.astype(F32).T.astype(BF16)
    for step in range(MB_TOK // TILE):
        rows = pl.ds(step * TILE, TILE)
        queries = q_ref[rows, :]
        asked = asked_ref[rows, :]
        grads = g_ref[rows, :]
        turned = []
        for side in range(2):
            if side == 0:
                query = jnp.where(tile_half, queries, asked)
            else:
                query = jnp.where(tile_half, asked, queries)
            scores = contract_last(keys_of[side], query)
            probs = jnp.exp(scores - lse_ref[0, 0, 8 * side:8 * side + 1, rows])
            grad_probs = contract_last(values_of[side], grads)
            product = probs * grad_probs
            centre = jnp.sum(product, axis=0, keepdims=True)
            grad_scores = (product - probs * centre).astype(BF16)
            part_v = matmul(probs.astype(BF16), grads)
            part_k = matmul(grad_scores, queries)
            if step == 0:
                acc_v[side] = part_v
                acc_k[side] = part_k
            else:
                acc_v[side] += part_v
                acc_k[side] += part_k
            turned.append(matmul(keys_turned[side * HEAD_DIM:(side + 1) * HEAD_DIM, :], grad_scores))
        dq_ref[rows, :] = jnp.concatenate(turned, axis=0).T.astype(BF16)
    dk_ref[...] = jnp.where(full, acc_k[0], acc_k[1]).astype(BF16)
    dv_ref[...] = jnp.where(full, acc_v[0], acc_v[1]).astype(BF16)


def attend_back(queries, keys, values, grads, lse, asked, barred):
    rows = queries.shape[0]
    micro = rows // MB_TOK
    wide = pl.BlockSpec((MB_TOK, LANES), lambda m, p: (m, p))
    side = pl.BlockSpec((MB_TOK, LANES), lambda m, p: (m, 0))
    return pl.pallas_call(
        attend_back_kernel,
        grid=(micro, PAIRS),
        in_specs=[wide, wide, wide, wide, pl.BlockSpec((1, 1, 16, MB_TOK), lambda m, p: (m, p, 0, 0)), side, side],
        out_specs=[wide, wide, wide],
        out_shape=(jax.ShapeDtypeStruct(queries.shape, BF16),) * 3,
        scratch_shapes=[pltpu.VMEM((2, MB_TOK, LANES), F32), pltpu.VMEM((2, MB_TOK, LANES), F32)],
        compiler_params=pltpu.CompilerParams(vmem_limit_bytes=56 << 20),
        cost_estimate=pl.CostEstimate(
            flops=10 * rows * MB_TOK * HEADS * HEAD_DIM,
            transcendentals=rows * MB_TOK * HEADS,
            bytes_accessed=rows * 768 * 14,
        ),
        name="attend_back",
    )(queries, keys, values, grads, lse, asked, barred)


def norm_stats(value):
    center = value - jnp.mean(value, axis=-1, keepdims=True)
    spread = jnp.mean(center * center, axis=-1, keepdims=True)
    scale = lax.rsqrt(spread + EPSILON)
    return center * scale, scale


def norm_back(grad, normed, scale, gain):
    u = grad * gain
    return scale * (
        u
        - jnp.mean(u, axis=-1, keepdims=True)
        - normed * jnp.mean(u * normed, axis=-1, keepdims=True)
    )


def slot_positions(targets, rows_dev, slot_rows, device_count):
    owner_dev = targets // rows_dev
    onehot = (owner_dev[:, None] == jnp.arange(device_count, dtype=jnp.int32)[None, :]).astype(
        jnp.int32
    )
    ranking = jnp.sum(jnp.cumsum(onehot, axis=0) * onehot, axis=1) - 1
    return owner_dev * slot_rows + ranking


def invert(positions):
    return (
        jnp.zeros_like(positions).at[positions].set(jnp.arange(positions.shape[0], dtype=jnp.int32))
    )


def exchange(rows, device_count):
    count, width = rows.shape
    return lax.all_to_all(
        rows.reshape(device_count, count // device_count, width), "dp", split_axis=0, concat_axis=0, tiled=True
    ).reshape(count, width)


def on_device(
    tokens,
    teacher,
    route_to,
    anchor,
    seq_lengths,
    query_weight,
    query_bias,
    key_weight,
    value_weight,
    value_bias,
    out_weight,
    out_bias,
    first_gain,
    first_shift,
    up_weight,
    up_bias,
    down_weight,
    down_bias,
    second_gain,
    second_shift,
):
    rows_dev, width = tokens.shape
    device_count = lax.axis_size("dp")
    slot_rows = rows_dev // device_count
    micro_count = rows_dev // MB_TOK
    asked, barred, usable = sequence_tables(seq_lengths, micro_count)

    count = jnp.sum(seq_lengths)
    pieces = jnp.stack([count // 64, count % 64]).astype(BF16)
    vectors = (query_bias, value_bias, out_bias, first_gain, first_shift, down_bias, second_gain, second_shift, up_bias)
    sizes = [v.shape[0] for v in vectors]
    used = sum(sizes) + 2
    padded = -(-used // 128) * 128
    packed = jnp.concatenate(list(vectors) + [pieces, jnp.zeros((padded - used,), BF16)])
    gathered = lax.all_gather(packed, "dp", axis=0, tiled=False).astype(F32)
    full_vectors = []
    place = 0
    for size in sizes:
        full_vectors.append(gathered[:, place:place + size].reshape(-1))
        place += size
    q_b, v_b, o_b, g1, s1, d_b, g2, s2, u_b = full_vectors
    valid_count = jnp.sum(gathered[:, place] * 64.0 + gathered[:, place + 1])

    w_qkv = lax.all_gather(
        jnp.concatenate([query_weight, key_weight, value_weight], axis=1), "dp", axis=0, tiled=True
    )
    w_out = lax.all_gather(out_weight, "dp", axis=0, tiled=True)
    w_up = lax.all_gather(up_weight, "dp", axis=0, tiled=True)
    w_down = lax.all_gather(down_weight, "dp", axis=0, tiled=True)

    outgoing = slot_positions(route_to, rows_dev, slot_rows, device_count)
    incoming = slot_positions(anchor, rows_dev, slot_rows, device_count)
    send_order = invert(outgoing)
    back_order = invert(incoming)
    x = exchange(tokens[send_order], device_count)[incoming]
    target = exchange(teacher[send_order], device_count)[incoming]

    w_q = w_qkv[:, :width]
    w_k = w_qkv[:, width:2 * width]
    w_v = w_qkv[:, 2 * width:]
    queries = ((matmul(x, w_q) + q_b) * 0.125).astype(BF16)
    keys = matmul(x, w_k).astype(BF16)
    values = (matmul(x, w_v) + v_b).astype(BF16)
    attended, lse = attend(queries, keys, values, asked, barred)
    pre_first = x + (matmul(attended, w_out) + o_b)
    n1, r1 = norm_stats(pre_first)
    hidden = n1 * g1 + s1
    hidden_low = hidden.astype(BF16)
    pre_act = matmul(hidden_low, w_up) + u_b
    cdf = 0.5 * (1.0 + lax.erf(pre_act * (2.0 ** -0.5)))
    act_low = (pre_act * cdf).astype(BF16)
    slope = (cdf + pre_act * (jnp.exp(-0.5 * pre_act * pre_act) * 0.3989422804014327)).astype(BF16)
    pre_second = hidden + (matmul(act_low, w_down) + d_b)
    n2, r2 = norm_stats(pre_second)
    layer_out = n2 * g2 + s2
    misfit = jnp.where(usable[:, None], layer_out - target.astype(F32), 0.0)
    states_routed = layer_out.astype(BF16)
    squares = jnp.sum(misfit * misfit)
    states = exchange(states_routed[back_order], device_count)[outgoing]

    grad_out = misfit * (rows_dev * device_count * 2.0 / valid_count)
    grad_s2 = column_sum(grad_out)
    grad_g2 = column_sum(grad_out * n2)
    grad_pre_second = norm_back(grad_out, n2, r2, g2)
    down_grad = grad_pre_second.astype(BF16)
    grad_w_down = cross_rows(act_low, down_grad).astype(BF16)
    grad_d_b = column_sum(down_grad)
    up_grad = (slope * contract_last(down_grad, w_down)).astype(BF16)
    grad_w_up = cross_rows(hidden_low, up_grad).astype(BF16)
    grad_u_b = column_sum(up_grad)
    share_down = lax.psum_scatter(grad_w_down, "dp", scatter_dimension=0, tiled=True)
    share_up = lax.psum_scatter(grad_w_up, "dp", scatter_dimension=0, tiled=True)
    grad_hidden = grad_pre_second + contract_last(up_grad, w_up)
    grad_s1 = column_sum(grad_hidden)
    grad_g1 = column_sum(grad_hidden * n1)
    grad_pre_first = norm_back(grad_hidden, n1, r1, g1)
    out_grad = grad_pre_first.astype(BF16)
    grad_w_out = cross_rows(attended, out_grad).astype(BF16)
    grad_o_b = column_sum(out_grad)
    share_out = lax.psum_scatter(grad_w_out, "dp", scatter_dimension=0, tiled=True)
    attended_grad = contract_last(out_grad, w_out).astype(BF16)
    dq, dk, dv = attend_back(queries, keys, values, attended_grad, lse, asked, barred)
    dq = dq * jnp.asarray(0.125, BF16)
    rows_grad = (
        grad_pre_first + contract_last(dq, w_q) + contract_last(dk, w_k) + contract_last(dv, w_v)
    ).astype(BF16)
    token_grad = exchange(rows_grad[back_order], device_count)[outgoing]
    grad_q_b = column_sum(dq)
    grad_v_b = column_sum(dv)
    grad_w_qkv = jnp.concatenate(
        [cross_rows(x, dq).astype(BF16), cross_rows(x, dk).astype(BF16), cross_rows(x, dv).astype(BF16)], axis=1
    )
    share_qkv = lax.psum_scatter(grad_w_qkv, "dp", scatter_dimension=0, tiled=True).astype(F32)

    grad_vectors = (grad_q_b, grad_v_b, grad_o_b, grad_g1, grad_s1, grad_d_b, grad_g2, grad_s2, grad_u_b)
    total_block = jnp.broadcast_to(squares.reshape(1, 1), (device_count, 1))
    grad_used = sum(sizes) + 1
    fill = jnp.zeros((device_count, -(-grad_used // 128) * 128 - grad_used), F32)
    grad_packed = jnp.concatenate(
        [g.reshape(device_count, -1) for g in grad_vectors] + [total_block, fill], axis=1
    )
    summed = lax.psum_scatter(grad_packed, "dp", scatter_dimension=0, tiled=True).reshape(-1)
    parts = []
    place = 0
    for size in sizes:
        parts.append(summed[place:place + size])
        place += size
    h_q_b, h_v_b, h_o_b, h_g1, h_s1, h_d_b, h_g2, h_s2, h_u_b = parts
    mse_loss = summed[place] / valid_count
    return (
        states,
        mse_loss,
        token_grad,
        share_qkv[:, :width],
        h_q_b,
        share_qkv[:, width:2 * width],
        share_qkv[:, 2 * width:],
        h_v_b,
        share_out.astype(F32),
        h_o_b,
        h_g1,
        h_s1,
        share_up.astype(F32),
        h_u_b,
        share_down.astype(F32),
        h_d_b,
        h_g2,
        h_s2,
    )


def solution(mesh):
    row = P("dp", None)
    vec = P("dp")
    placed = (row, row, vec, vec, vec, row, vec, row, row, vec, row, vec, vec, vec, row, vec, row, vec, vec, vec)
    return jax.shard_map(
        on_device,
        mesh=mesh,
        in_specs=placed,
        out_specs=(row, P(), row, row, vec, row, row, vec, row, vec, vec, vec, row, vec, row, vec, vec, vec),
        check_vma=False,
    )
```

time: 1760 us -> 1080 us (0.61)
  matrix products: 710 us -> 176 us
  Pallas kernels: 0 us -> 132 us
  waiting for transfers between devices: 379 us -> 271 us
  local copies, waits for them, and re-layouts: 245 us -> 157 us
  other arithmetic: 137 us -> 82.9 us
  blocking collectives: 224 us -> 190 us
    dot_general x60 -> x6, matrix products: 278 us -> 60.8 us  [matmul(): return jnp.dot(left, right, preferred_element_type=F32)]
    dot_general x84 -> x6, matrix products: 253 us -> 66 us  [contract_last(): lax.dot_general(left, right, (((1,), (1,)), ((), ())), preferred_element_...]
    psum x2 -> x0, blocking collectives: 185 us -> none  [the longest x1 97.2 us: on_device(): valid_count = lax.psum(jnp.sum(usable.astype(jnp.float32)), 'dp')]
    reduce_scatter x6 -> x3, waiting for transfers between devices: 316 us -> 177 us  [the longest x1 111 us: on_device(): lax.psum_scatter(grad_w_down, 'dp', scatter_dimension=0, tiled=True)]
    pallas_call x0 -> x2, Pallas kernels: none -> 132 us  [the longest x1 79.2 us: attend_back(): pl.pallas_call(attend_back_kernel, grid=(micro, PAIRS), in_specs=[wide, w...]
    dot_general x60 -> x6, matrix products: 178 us -> 49.4 us  [cross_rows(): lax.dot_general(left, right, (((0,), (0,)), ((), ())), preferred_element_...]
    all_gather x0 -> x1, blocking collectives: none -> 89.4 us  [on_device(): gathered = lax.all_gather(packed, 'dp', axis=0, tiled=False).astype(F32)]
    unnamed x1, blocking collectives: 38.8 us -> 100 us
  transfers between devices with their start and end apart: 16 -> 12, of which waited for: 4 -> 4; matrix products, arithmetic and copies ran while one was open for 53% -> 29% of each run, Pallas kernels for 0% -> 5%
where the time goes in v1:
time: 1080 us; the launch traced here: 1070 us
  waiting for transfers between devices  271 us (25%)
  blocking collectives  190 us (18%)
  matrix products  176 us (16%)
  local copies, waits for them, and re-layouts  157 us (15%)
  Pallas kernels  132 us (12%)
  other arithmetic  82.9 us (8%)
  starting transfers between devices  41.8 us (4%)
  between operations  20.9 us (2%)
    reduce_scatter x1, waiting for transfers between devices, on_device(): lax.psum_scatter(grad_w_down, 'dp', scatter_dimension=0, tiled=True)  111 us
    unnamed x1, blocking collectives  100 us
    all_to_all x4, waiting for transfers between devices, exchange(): lax.all_to_all(rows.reshape(device_count, count // device_count, width),...  91.9 us
    all_gather x1, blocking collectives, on_device(): gathered = lax.all_gather(packed, 'dp', axis=0, tiled=False).astype(F32)  89.4 us
    pallas_call x1, Pallas kernels, attend_back(): pl.pallas_call(attend_back_kernel, grid=(micro, PAIRS), in_specs=[wide, w...  79.2 us
    reduce_scatter x1, waiting for transfers between devices, on_device(): lax.psum_scatter(grad_w_up, 'dp', scatter_dimension=0, tiled=True)  66.3 us
    dot_general x6, matrix products, contract_last(): lax.dot_general(left, right, (((1,), (1,)), ((), ())), preferred_element_...  66 us
    dot_general x6, matrix products, matmul(): return jnp.dot(left, right, preferred_element_type=F32)  60.8 us
  transfers between devices with their start and end apart: 12, of which 4 were waited for; matrix products, arithmetic and copies ran while one was open for 29% of the time, Pallas kernels for 5%

profile of v1, /device:TPU:0, one launch (start us, length us, event | category | flops | bytes accessed | tf_op | source)
XLA Modules:
  0.0 1070.7 jit_solution(14539642811200029769)
XLA Ops:
  11.1 15.9 %reduce-window.14 = s32[32,16,128]{2,1,0:T(8,128)S(1)} reduce-window(s32[32,16,128]{2,1,0:T(8,128)} %fusion.30, s32[]{:T(128)} %constant.92.clone.1), window={size=1x1x128 pad=0_0x0_0x127_0}, to_apply=%region_0.1 | reduce-window | flops 8323072 | bytes 524292 | tf_op jit(solution)/shard_map/reduce-window
  38.8 9.4 gather_fusion.4
  56.3 12.4 %gather_fusion = bf16[2048,768]{1,0:T(8,128)(2,1)} fusion(bf16[2048,768]{1,0:T(8,128)(2,1)} %param.20, s32[2048]{0:T(1024)S(1)} %fusion.35), kind=kCustom, calls=%fused_computation | custom fusion | bytes 6299648 | tf_op jit(solution)/shard_map/gather | solution.py:277
  68.8 69.8 %all-to-all-done.2 = bf16[32,64,768]{2,1,0:T(8,128)(2,1)S(1)} async-done(((bf16[32,64,768]{2,1,0:T(8,128)(2,1)}), bf16[32,64,768]{2,1,0:T(8,128)(2,1)S(1)}, u32[]{:S(2)}, u32[]{:S(2)}) %all-to-all-start.2) | async-done | bytes 3145760 | tf_op jit(solution)/shard_map/all_to_all | solution.py:217
  146.5 89.4 %all-gather.1 = bf16[32,1,384]{2,1,0:T(2,128)(2,1)S(1)} all-gather(bf16[1,1,384]{2,1,0:T(2,128)(2,1)S(1)} %reshape.367), channel_id=2, replica_groups=mesh['dp'=32] {'dp'}, dimensions={0}, use_global_device_ids=true | all-gather | bytes 25344 | tf_op jit(solution)/shard_map/all_gather | solution.py:257
  239.3 15.9 %reduce-window.16 = s32[32,16,128]{2,1,0:T(8,128)S(1)} reduce-window(s32[32,16,128]{2,1,0:T(8,128)} %fusion.31, s32[]{:T(128)} %constant.92.clone.1), window={size=1x1x128 pad=0_0x0_0x127_0}, to_apply=%region_4.5 | reduce-window | flops 8323072 | bytes 524292 | tf_op jit(solution)/shard_map/reduce-window.2
  290.3 12.4 %gather_fusion.1 = bf16[2048,768]{1,0:T(8,128)(2,1)} fusion(bf16[2048,768]{1,0:T(8,128)(2,1)} %bitcast.5, s32[2048]{0:T(1024)S(1)} %get-tuple-element.115), kind=kCustom, calls=%fused_computation.1 | custom fusion | bytes 6299648 | tf_op jit(solution)/shard_map/gather | solution.py:277
  322.1 52.6 %attend.1 = (bf16[2048,768]{1,0:T(8,128)(2,1)}, f32[2,6,16,1024]{3,2,1,0:T(8,128)}) custom-call(bf16[2048,768]{1,0:T(8,128)(2,1)} %multiply_convert_fusion.2.q_ref, bf16[2048,768]{1,0:T(8,128)(2,1)} %convolution_convert_fusion.3.k_ref, bf16[2048,768]{1,0:T(8,128)(2,1)} %add_convert_fusion.1.v_ref, bf16[2048,128]{1,0:T(8,128)(2,1)} %bitcast.108, ...), custom_call_target="tpu_custom_call" | custom-call | flops 6442450944 | bytes 12582912 | tf_op jit(solution)/shard_map/attend/pallas_call | solution.py:102
  384.4 21.3 %multiply_convert_fusion.1 = (bf16[2048,3072]{1,0:T(8,128)(2,1)}, f32[2048,3072]{1,0:T(8,128)}) fusion(f32[3072]{0:T(1024)S(1)} %add.220, bf16[768,3072]{1,0:T(8,128)(2,1)} %all-gather.11.cloned.1.call-done, f32[2048,768]{0,1:T(8,128)} %copy-done.3, f32[768]{0:T(1024)S(1)} %add.217, f32[768]{0:T(1024)S(1)} %mul.198, f32[2048]{0:T(1024)S(1)} %add_rsqrt_fusion.1, ...), kind=kOutput, calls=%fused_computation.18 | convolution fusion | flops 9709289472 | bytes 48793600 | tf_op jit(solution)/shard_map/dot_general | solution.py:25
  405.8 18.4 %fusion.58 = (f32[2048]{0:T(1024)S(1)}, f32[2048,768]{0,1:T(8,128)}) fusion(f32[768]{0:T(1024)S(1)} %copy-done.21, bf16[2048,3072]{1,0:T(8,128)(2,1)} %get-tuple-element.148, bf16[3072,768]{1,0:T(8,128)(2,1)} %all-gather.13.cloned.1.call-done, f32[768]{0:T(1024)S(1)} %add.217, f32[768]{0:T(1024)S(1)} %mul.198, f32[2048]{0:T(1024)S(1)} %add_rsqrt_fusion.1, ...), kind=kOutput, calls=%fused_computation.163 | convolution fusion | flops 9674684416 | bytes 29918208 | tf_op jit(solution)/shard_map/dot_general | solution.py:25
  440.2 24.2 %convert_reduce_fusion = (f32[3072]{0:T(1024)}, bf16[2048,3072]{1,0:T(8,128)(2,1)}) fusion(bf16[3072,768]{1,0:T(8,128)(2,1)S(1)} %bitcast.119, f32[2048,768]{0,1:T(8,128)S(1)} %get-tuple-element.110, f32[2048,3072]{1,0:T(8,128)} %get-tuple-element.149, f32[3072]{0:T(1024)S(1)} %add.220), kind=kOutput, calls=%fused_computation.16 | convolution fusion | flops 9759618048 | bytes 48783360 | tf_op jit(solution)/shard_map/dot_general | solution.py:29
  464.4 16.9 %multiply_reduce_fusion.2 = (f32[768]{0:T(1024)S(1)}, f32[2048]{0:T(1024)S(1)}, f32[2048]{0:T(1024)S(1)}, f32[768]{0:T(1024)S(1)}, f32[2048,768]{0,1:T(8,128)}) fusion(f32[2048,768]{0,1:T(8,128)S(1)} %bitcast.96, f32[2048]{0:T(1024)S(1)} %add_rsqrt_fusion.1, f32[2048]{0:T(1024)S(1)} %broadcast_multiply_fusion.5, f32[768]{0:T(1024)S(1)} %mul.198, ...), kind=kOutput, calls=%fused_computation.24 | convolution fusion | flops 9679398912 | bytes 36217856 | tf_op jit(solution)/shard_map/dot_general | solution.py:29
  499.2 79.2 %attend_back.1 = (bf16[2048,768]{1,0:T(8,128)(2,1)}, bf16[2048,768]{1,0:T(8,128)(2,1)}, bf16[2048,768]{1,0:T(8,128)(2,1)}) custom-call(bf16[2048,768]{1,0:T(8,128)(2,1)} %multiply_convert_fusion.2.q_ref, bf16[2048,768]{1,0:T(8,128)(2,1)} %convolution_convert_fusion.3.k_ref, bf16[2048,768]{1,0:T(8,128)(2,1)} %add_convert_fusion.1.v_ref, ...), custom_call_target="tpu_custom_call" | custom-call | flops 16106127360 | bytes 22020096 | tf_op jit(solution)/shard_map/attend_back/pallas_call | solution.py:167
  599.8 16.3 %convolution_convert_fusion.1 = bf16[768,3072]{1,0:T(8,128)(2,1)} fusion(bf16[2048,3072]{1,0:T(8,128)(2,1)} %get-tuple-element.154, f32[2048,768]{0,1:T(8,128)} %copy-done.3, f32[768]{0:T(1024)S(1)} %add.217, f32[768]{0:T(1024)S(1)} %mul.198, f32[2048]{0:T(1024)S(1)} %add_rsqrt_fusion.1, f32[2048]{0:T(1024)S(1)} %broadcast_multiply_fusion.5), kind=kOutput, calls=%fused_computation.48 | convolution fusion | flops 9673900032 | bytes 23615488 | tf_op jit(solution)/shard_map/dot_general | solution.py:33
  627.6 9.4 gather_fusion.2
  637.0 25.8 %all-to-all-start.1 = ((bf16[32,64,768]{2,1,0:T(8,128)(2,1)}), bf16[32,64,768]{2,1,0:T(8,128)(2,1)S(1)}, u32[]{:S(2)}, u32[]{:S(2)}) async-start(bf16[32,64,768]{2,1,0:T(8,128)(2,1)} %bitcast.101), calls=%async_computation.1 | async-start | bytes 6291456 | tf_op jit(solution)/shard_map/all_to_all | solution.py:217
  663.0 16.4 %convolution_convert_fusion = bf16[3072,768]{1,0:T(8,128)(2,1)} fusion(bf16[2048,3072]{1,0:T(8,128)(2,1)} %get-tuple-element.148, f32[2048,768]{0,1:T(8,128)} %copy-done.8), kind=kOutput, calls=%fused_computation.47 | convolution fusion | flops 9667608576 | bytes 23592960 | tf_op jit(solution)/shard_map/dot_general | solution.py:33
  702.0 12.5 %gather_fusion.6 = bf16[2048,768]{1,0:T(8,128)(2,1)} fusion(bf16[2048,768]{1,0:T(8,128)(2,1)} %copy.94, s32[2048]{0:T(1024)S(1)} %fusion.36), kind=kCustom, calls=%fused_computation.6 | custom fusion | bytes 6299648 | tf_op jit(solution)/shard_map/gather | solution.py:329
  714.4 22.1 %all-to-all-done.1 = bf16[32,64,768]{2,1,0:T(8,128)(2,1)S(1)} async-done(((bf16[32,64,768]{2,1,0:T(8,128)(2,1)}), bf16[32,64,768]{2,1,0:T(8,128)(2,1)S(1)}, u32[]{:S(2)}, u32[]{:S(2)}) %all-to-all-start.1) | async-done | bytes 3145760 | tf_op jit(solution)/shard_map/all_to_all | solution.py:217
  747.3 100.2 %all-reduce.2 = f32[32,384]{1,0:T(8,128)S(1)} all-reduce(f32[32,384]{1,0:T(8,128)S(1)} %concatenate.24), channel_id=3, replica_groups=mesh['dp'=32] {'dp'}, use_global_device_ids=true, to_apply=%region_30.31.clone | all-reduce | flops 12288 | bytes 98304
  860.5 9.4 gather_fusion.3
  869.9 12.6 %gather_fusion.7 = bf16[2048,768]{1,0:T(8,128)(2,1)} fusion(bf16[2048,768]{1,0:T(8,128)(2,1)} %bitcast.20, s32[2048]{0:T(1024)S(1)} %copy-done.13), kind=kCustom, calls=%fused_computation.7 | custom fusion | bytes 6299648 | tf_op jit(solution)/shard_map/gather | solution.py:329
  882.4 66.3 %reduce-scatter.9.cloned.1.call-done = bf16[24,3072]{1,0:T(8,128)(2,1)} async-done(((bf16[768,3072]{1,0:T(8,128)(2,1)}), bf16[24,3072]{1,0:T(8,128)(2,1)}) %reduce-scatter.9.cloned.1.call-update) | async-done | bytes 147472 | tf_op jit(solution)/shard_map/reduce_scatter | solution.py:314
  950.4 110.5 %reduce-scatter.11.cloned.1.call-done = bf16[96,768]{1,0:T(8,128)(2,1)} async-done(((bf16[3072,768]{1,0:T(8,128)(2,1)}), bf16[96,768]{1,0:T(8,128)(2,1)}) %reduce-scatter.11.cloned.1.call-update) | async-done | bytes 147472 | tf_op jit(solution)/shard_map/reduce_scatter | solution.py:313
  (225 shorter events, 210.6 us)
Async XLA Ops:
  7.2 300.2 %all-gather.7.cloned.1.call-start = ((), (), s32[]{:S(2)}) async-start(), calls=%async_computation.8 | async-start | bytes 3649536 | tf_op jit(solution)/shard_map/all_gather | solution.py:266
  8.9 365.8 %all-gather.9.cloned.1.call-start = ((), (), s32[]{:S(2)}) async-start(), calls=%async_computation.9 | async-start | bytes 1216512 | tf_op jit(solution)/shard_map/all_gather | solution.py:269
  48.2 90.4 %all-to-all-start.2 = ((bf16[32,64,768]{2,1,0:T(8,128)(2,1)}), bf16[32,64,768]{2,1,0:T(8,128)(2,1)S(1)}, u32[]{:S(2)}, u32[]{:S(2)}) async-start(bf16[32,64,768]{2,1,0:T(8,128)(2,1)} %bitcast.102), calls=%async_computation.2 | async-start | bytes 6291456 | tf_op jit(solution)/shard_map/all_to_all | solution.py:217
  55.6 328.9 %all-gather.11.cloned.1.call-start = ((), (), s32[]{:S(2)}) async-start(), calls=%async_computation.10 | async-start | bytes 4866048 | tf_op jit(solution)/shard_map/all_gather | solution.py:270
  68.7 77.6 %copy-start.24 = (bf16[24]{0:T(256)(128)(2,1)S(1)}, bf16[24]{0:T(256)(128)(2,1)}, u32[]{:S(2)}) copy-start(bf16[24]{0:T(256)(128)(2,1)} %param.29) | copy-start | bytes 148
  68.7 77.6 %copy-start.25 = (bf16[24]{0:T(256)(128)(2,1)S(1)}, bf16[24]{0:T(256)(128)(2,1)}, u32[]{:S(2)}) copy-start(bf16[24]{0:T(256)(128)(2,1)} %param.31) | copy-start | bytes 148
  68.7 77.6 %copy-start.26 = (bf16[24]{0:T(256)(128)(2,1)S(1)}, bf16[24]{0:T(256)(128)(2,1)}, u32[]{:S(2)}) copy-start(bf16[24]{0:T(256)(128)(2,1)} %param.32) | copy-start | bytes 148
  68.7 77.6 %copy-start.27 = (bf16[24]{0:T(256)(128)(2,1)S(1)}, bf16[24]{0:T(256)(128)(2,1)}, u32[]{:S(2)}) copy-start(bf16[24]{0:T(256)(128)(2,1)} %param.33) | copy-start | bytes 148
  68.7 77.6 %copy-start.28 = (bf16[24]{0:T(256)(128)(2,1)S(1)}, bf16[24]{0:T(256)(128)(2,1)}, u32[]{:S(2)}) copy-start(bf16[24]{0:T(256)(128)(2,1)} %param.37) | copy-start | bytes 148
  68.7 77.6 %copy-start.29 = (bf16[24]{0:T(256)(128)(2,1)S(1)}, bf16[24]{0:T(256)(128)(2,1)}, u32[]{:S(2)}) copy-start(bf16[24]{0:T(256)(128)(2,1)} %param.38) | copy-start | bytes 148
  68.7 77.6 %copy-start.30 = (bf16[24]{0:T(256)(128)(2,1)S(1)}, bf16[24]{0:T(256)(128)(2,1)}, u32[]{:S(2)}) copy-start(bf16[24]{0:T(256)(128)(2,1)} %param.39) | copy-start | bytes 148
  68.7 167.1 %copy-start.16 = (s32[2048]{0:T(1024)S(1)}, s32[2048]{0:T(1024)}, u32[]{:S(2)}) copy-start(s32[2048]{0:T(1024)} %param.23) | copy-start | bytes 24580
  138.6 151.7 %all-to-all-start = ((bf16[32,64,768]{2,1,0:T(8,128)(2,1)}), bf16[32,64,768]{2,1,0:T(8,128)(2,1)}, u32[]{:S(2)}, u32[]{:S(2)}) async-start(bf16[32,64,768]{2,1,0:T(8,128)(2,1)} %bitcast.99), calls=%async_computation | async-start | bytes 6291456 | tf_op jit(solution)/shard_map/all_to_all | solution.py:217
  142.3 263.5 %all-gather.13.cloned.1.call-start = ((), (), s32[]{:S(2)}) async-start(), calls=%async_computation.11 | async-start | bytes 4866048 | tf_op jit(solution)/shard_map/all_gather | solution.py:271
  142.9 707.8 %reduce-scatter.7.cloned.1.call-start = ((), (), s32[]{:S(2)}) async-start(), calls=%async_computation.12 | async-start | bytes 1216512 | tf_op jit(solution)/shard_map/reduce_scatter | solution.py:322
  146.3 92.3 %copy-start.22 = (s32[2,8]{1,0:T(2,128)}, s32[2,8]{1,0:T(2,128)S(1)}, u32[]{:S(2)}) copy-start(s32[2,8]{1,0:T(2,128)S(1)} %reshape.254) | copy-start | bytes 196
  499.2 79.2 %copy-start.7 = (bf16[2048,768]{1,0:T(8,128)(2,1)S(1)}, bf16[2048,768]{1,0:T(8,128)(2,1)}, u32[]{:S(2)}) copy-start(bf16[2048,768]{1,0:T(8,128)(2,1)} %gather_fusion.1) | copy-start | bytes 9437188
  584.0 268.1 %reduce-scatter.13.cloned.1.call-start = ((), (), s32[]{:S(2)}) async-start(), calls=%async_computation.15 | async-start | bytes 3649536
  599.8 349.0 %reduce-scatter.9.cloned.1.call-start = ((), (), s32[]{:S(2)}) async-start(), calls=%async_computation.13 | async-start | bytes 4866048 | tf_op jit(solution)/shard_map/reduce_scatter | solution.py:314
  637.0 99.5 %all-to-all-start.1 = ((bf16[32,64,768]{2,1,0:T(8,128)(2,1)}), bf16[32,64,768]{2,1,0:T(8,128)(2,1)S(1)}, u32[]{:S(2)}, u32[]{:S(2)}) async-start(bf16[32,64,768]{2,1,0:T(8,128)(2,1)} %bitcast.101), calls=%async_computation.1 | async-start | bytes 6291456 | tf_op jit(solution)/shard_map/all_to_all | solution.py:217
  662.8 398.1 %reduce-scatter.11.cloned.1.call-start = ((), (), s32[]{:S(2)}) async-start(), calls=%async_computation.14 | async-start | bytes 4866048 | tf_op jit(solution)/shard_map/reduce_scatter | solution.py:313
  736.5 133.3 %all-to-all-start.3 = ((bf16[32,64,768]{2,1,0:T(8,128)(2,1)}), bf16[32,64,768]{2,1,0:T(8,128)(2,1)}, u32[]{:S(2)}, u32[]{:S(2)}) async-start(bf16[32,64,768]{2,1,0:T(8,128)(2,1)} %bitcast.100), calls=%async_computation.3 | async-start | bytes 6291456 | tf_op jit(solution)/shard_map/all_to_all | solution.py:217
  740.6 119.9 %copy-start.13 = (s32[2048]{0:T(1024)S(1)}, s32[2048]{0:T(1024)}, u32[]{:S(2)}) copy-start(s32[2048]{0:T(1024)} %get-tuple-element.113) | copy-start | bytes 24580
  869.9 192.7 %copy-start.1 = (bf16[2048,768]{1,0:T(8,128)(2,1)S(1)}, bf16[2048,768]{1,0:T(8,128)(2,1)}, u32[]{:S(2)}) copy-start(bf16[2048,768]{1,0:T(8,128)(2,1)} %param.21) | copy-start | bytes 9437188
  (31 other events, 549.3 us)
Sparse Core Ops, SparseCore 0:
  10.9 80.8 all-gather.6
  94.7 68.2 all-gather.8
  165.9 74.9 all-gather.10
  243.7 62.2 all-gather.12
  584.1 128.9 reduce-scatter.6
  718.4 118.0 reduce-scatter.12
  842.0 106.6 reduce-scatter.8
  954.2 106.6 reduce-scatter.10

commit v2 on v1

--- a/solution.py
+++ b/solution.py
@@ -1,11 +1,10 @@
-import functools
-
 import jax
 import jax.numpy as jnp
 from jax import lax
 from jax.experimental import pallas as pl
 from jax.experimental.pallas import tpu as pltpu
 from jax.sharding import PartitionSpec as P
+
 
 HEADS = 12
 HEAD_DIM = 64
@@ -199,11 +198,17 @@
 
 def slot_positions(targets, rows_dev, slot_rows, device_count):
     owner_dev = targets // rows_dev
-    onehot = (owner_dev[:, None] == jnp.arange(device_count, dtype=jnp.int32)[None, :]).astype(
-        jnp.int32
-    )
-    ranking = jnp.sum(jnp.cumsum(onehot, axis=0) * onehot, axis=1) - 1
-    return owner_dev * slot_rows + ranking
+    chunks = rows_dev // BLOCK
+    onehot = (owner_dev[:, None] == jnp.arange(device_count, dtype=jnp.int32)[None, :]).astype(BF16)
+    onehot = onehot.reshape(chunks, BLOCK, device_count)
+    steps = jnp.arange(BLOCK)
+    earlier = (steps[:, None] > steps[None, :]).astype(BF16)
+    inner = jnp.einsum("ij,cjd->cid", earlier, onehot, preferred_element_type=F32)
+    sums = jnp.sum(onehot.astype(F32), axis=1)
+    places = jnp.arange(chunks)
+    outer = jnp.sum(jnp.where((places[:, None] > places[None, :])[:, :, None], sums[None], 0.0), axis=1)
+    rank = jnp.sum((inner + outer[:, None, :]) * onehot.astype(F32), axis=2)
+    return owner_dev * slot_rows + rank.reshape(rows_dev).astype(jnp.int32)
 
 
 def invert(positions):
@@ -212,14 +217,22 @@
     )
 
 
+def gather(value, tiled=True):
+    return lax.all_gather(value, "dp", axis=0, tiled=tiled)
+
+
+def scatter_sum(value):
+    return lax.psum_scatter(value, "dp", scatter_dimension=0, tiled=True)
+
+
 def exchange(rows, device_count):
     count, width = rows.shape
-    return lax.all_to_all(
-        rows.reshape(device_count, count // device_count, width), "dp", split_axis=0, concat_axis=0, tiled=True
-    ).reshape(count, width)
-
-
-def on_device(
+    slots = rows.reshape(device_count, count // device_count, width)
+    slots = lax.all_to_all(slots, "dp", split_axis=0, concat_axis=0, tiled=True)
+    return slots.reshape(count, width)
+
+
+def layer_step(
     tokens,
     teacher,
     route_to,
@@ -252,9 +265,15 @@
     vectors = (query_bias, value_bias, out_bias, first_gain, first_shift, down_bias, second_gain, second_shift, up_bias)
     sizes = [v.shape[0] for v in vectors]
     used = sum(sizes) + 2
-    padded = -(-used // 128) * 128
-    packed = jnp.concatenate(list(vectors) + [pieces, jnp.zeros((padded - used,), BF16)])
-    gathered = lax.all_gather(packed, "dp", axis=0, tiled=False).astype(F32)
+    extra = -(-used // width)
+    packed = jnp.concatenate(list(vectors) + [pieces, jnp.zeros((extra * width - used,), BF16)])
+    own_out = out_weight.shape[0]
+    w_qkv = gather(jnp.concatenate([query_weight, key_weight, value_weight], axis=1))
+    with_out = gather(jnp.concatenate([out_weight, packed.reshape(extra, width)], axis=0), False)
+    w_out = with_out[:, :own_out].reshape(device_count * own_out, width)
+    gathered = with_out[:, own_out:].reshape(device_count, extra * width).astype(F32)
+    w_up = gather(up_weight)
+    w_down = gather(down_weight)
     full_vectors = []
     place = 0
     for size in sizes:
@@ -263,18 +282,12 @@
     q_b, v_b, o_b, g1, s1, d_b, g2, s2, u_b = full_vectors
     valid_count = jnp.sum(gathered[:, place] * 64.0 + gathered[:, place + 1])
 
-    w_qkv = lax.all_gather(
-        jnp.concatenate([query_weight, key_weight, value_weight], axis=1), "dp", axis=0, tiled=True
-    )
-    w_out = lax.all_gather(out_weight, "dp", axis=0, tiled=True)
-    w_up = lax.all_gather(up_weight, "dp", axis=0, tiled=True)
-    w_down = lax.all_gather(down_weight, "dp", axis=0, tiled=True)
-
     outgoing = slot_positions(route_to, rows_dev, slot_rows, device_count)
     incoming = slot_positions(anchor, rows_dev, slot_rows, device_count)
     send_order = invert(outgoing)
     back_order = invert(incoming)
-    x = exchange(tokens[send_order], device_count)[incoming]
+    tokens_out, incoming, back_order = lax.optimization_barrier((tokens[send_order], incoming, back_order))
+    x = exchange(tokens_out, device_count)[incoming]
     target = exchange(teacher[send_order], device_count)[incoming]
 
     w_q = w_qkv[:, :width]
@@ -298,20 +311,19 @@
     misfit = jnp.where(usable[:, None], layer_out - target.astype(F32), 0.0)
     states_routed = layer_out.astype(BF16)
     squares = jnp.sum(misfit * misfit)
-    states = exchange(states_routed[back_order], device_count)[outgoing]
+    states_out = states_routed[back_order]
 
     grad_out = misfit * (rows_dev * device_count * 2.0 / valid_count)
     grad_s2 = column_sum(grad_out)
     grad_g2 = column_sum(grad_out * n2)
     grad_pre_second = norm_back(grad_out, n2, r2, g2)
-    down_grad = grad_pre_second.astype(BF16)
+    down_grad, states_out = lax.optimization_barrier((grad_pre_second.astype(BF16), states_out))
+    states = exchange(states_out, device_count)[outgoing]
     grad_w_down = cross_rows(act_low, down_grad).astype(BF16)
     grad_d_b = column_sum(down_grad)
     up_grad = (slope * contract_last(down_grad, w_down)).astype(BF16)
     grad_w_up = cross_rows(hidden_low, up_grad).astype(BF16)
     grad_u_b = column_sum(up_grad)
-    share_down = lax.psum_scatter(grad_w_down, "dp", scatter_dimension=0, tiled=True)
-    share_up = lax.psum_scatter(grad_w_up, "dp", scatter_dimension=0, tiled=True)
     grad_hidden = grad_pre_second + contract_last(up_grad, w_up)
     grad_s1 = column_sum(grad_hidden)
     grad_g1 = column_sum(grad_hidden * n1)
@@ -319,8 +331,13 @@
     out_grad = grad_pre_first.astype(BF16)
     grad_w_out = cross_rows(attended, out_grad).astype(BF16)
     grad_o_b = column_sum(out_grad)
-    share_out = lax.psum_scatter(grad_w_out, "dp", scatter_dimension=0, tiled=True)
     attended_grad = contract_last(out_grad, w_out).astype(BF16)
+    attended_grad, grad_w_down, grad_w_up, grad_w_out = lax.optimization_barrier(
+        (attended_grad, grad_w_down, grad_w_up, grad_w_out)
+    )
+    share_down = scatter_sum(grad_w_down)
+    share_up = scatter_sum(grad_w_up)
+    share_out = scatter_sum(grad_w_out)
     dq, dk, dv = attend_back(queries, keys, values, attended_grad, lse, asked, barred)
     dq = dq * jnp.asarray(0.125, BF16)
     rows_grad = (
@@ -332,7 +349,7 @@
     grad_w_qkv = jnp.concatenate(
         [cross_rows(x, dq).astype(BF16), cross_rows(x, dk).astype(BF16), cross_rows(x, dv).astype(BF16)], axis=1
     )
-    share_qkv = lax.psum_scatter(grad_w_qkv, "dp", scatter_dimension=0, tiled=True).astype(F32)
+    share_qkv = scatter_sum(grad_w_qkv).astype(F32)
 
     grad_vectors = (grad_q_b, grad_v_b, grad_o_b, grad_g1, grad_s1, grad_d_b, grad_g2, grad_s2, grad_u_b)
     total_block = jnp.broadcast_to(squares.reshape(1, 1), (device_count, 1))
@@ -341,7 +358,8 @@
     grad_packed = jnp.concatenate(
         [g.reshape(device_count, -1) for g in grad_vectors] + [total_block, fill], axis=1
     )
-    summed = lax.psum_scatter(grad_packed, "dp", scatter_dimension=0, tiled=True).reshape(-1)
+    shares = lax.all_to_all(grad_packed, "dp", split_axis=0, concat_axis=0, tiled=True)
+    summed = jnp.sum(shares, axis=0)
     parts = []
     place = 0
     for size in sizes:
@@ -376,7 +394,7 @@
     vec = P("dp")
     placed = (row, row, vec, vec, vec, row, vec, row, row, vec, row, vec, vec, vec, row, vec, row, vec, vec, vec)
     return jax.shard_map(
-        on_device,
+        layer_step,
         mesh=mesh,
         in_specs=placed,
         out_specs=(row, P(), row, row, vec, row, row, vec, row, vec, vec, vec, row, vec, row, vec, vec, vec),

time: 1080 us -> 1040 us (0.963)
  waiting for transfers between devices: 271 us -> 478 us
  blocking collectives: 190 us -> 10.5 us
  other arithmetic: 82.9 us -> 46.2 us
  starting transfers between devices: 41.8 us -> 18.3 us
    unnamed x9, waiting for transfers between devices: 1.98 us -> 106 us
    unnamed x1 -> x0, blocking collectives: 100 us -> none
    all_gather x1 -> x0, blocking collectives: 89.4 us -> none  [on_device(): gathered = lax.all_gather(packed, 'dp', axis=0, tiled=False).astype(F32)]
    all_to_all x4, waiting for transfers between devices: 91.9 us -> 180 us  [exchange(): slots = lax.all_to_all(slots, 'dp', split_axis=0, concat_axis=0, tiled=True)]
    another operation x6 -> x0, other arithmetic: 34.5 us -> none
    all_to_all x4, starting transfers between devices: 40.9 us -> 17.7 us  [exchange(): slots = lax.all_to_all(slots, 'dp', split_axis=0, concat_axis=0, tiled=True)]
    reduce_scatter x3, waiting for transfers between devices: 177 us -> 192 us  [scatter_sum(): return lax.psum_scatter(value, 'dp', scatter_dimension=0, tiled=True)]
  transfers between devices with their start and end apart: 12 -> 12, of which waited for: 4 -> 6; matrix products, arithmetic and copies ran while one was open for 29% -> 21% of each run, Pallas kernels for 5% -> 5%
where the time goes in v2:
time: 1040 us
  waiting for transfers between devices  478 us (46%)
  matrix products  175 us (17%)
  local copies, waits for them, and re-layouts  156 us (15%)
  Pallas kernels  132 us (13%)
  other arithmetic  46.2 us (4%)
  between operations  20.9 us (2%)
  starting transfers between devices  18.3 us (2%)
  blocking collectives  10.5 us (1%)
    reduce_scatter x3, waiting for transfers between devices, scatter_sum(): return lax.psum_scatter(value, 'dp', scatter_dimension=0, tiled=True)  192 us
    all_to_all x4, waiting for transfers between devices, exchange(): slots = lax.all_to_all(slots, 'dp', split_axis=0, concat_axis=0, tiled=True)  180 us
    unnamed x9, waiting for transfers between devices  106 us
    pallas_call x1, Pallas kernels, attend_back(): pl.pallas_call(attend_back_kernel, grid=(micro, PAIRS), in_specs=[wide, w...  79.1 us
    dot_general x6, matrix products, contract_last(): lax.dot_general(left, right, (((1,), (1,)), ((), ())), preferred_element_...  66.3 us
    dot_general x6, matrix products, matmul(): return jnp.dot(left, right, preferred_element_type=F32)  60.2 us
    pallas_call x1, Pallas kernels, attend(): pl.pallas_call(attend_kernel, grid=(micro, PAIRS), in_specs=[wide, wide,...  52.7 us
    dot_general x6, matrix products, cross_rows(): lax.dot_general(left, right, (((0,), (0,)), ((), ())), preferred_element_...  48.4 us
  transfers between devices with their start and end apart: 12, of which 6 were waited for; matrix products, arithmetic and copies ran while one was open for 21% of the time, Pallas kernels for 5%

profile of v2, /device:TPU:0, one launch (start us, length us, event | category | flops | bytes accessed | tf_op | source)
XLA Modules:
  0.0 1036.2 jit_solution(9378927362773283448)
XLA Ops:
  31.8 9.4 gather_fusion
  41.5 8.0 scatter_custom_fusion.1
  57.6 12.4 %gather_fusion.2 = bf16[2048,768]{1,0:T(8,128)(2,1)} fusion(bf16[2048,768]{1,0:T(8,128)(2,1)} %param.21, s32[2048]{0:T(1024)S(1)} %fusion.42), kind=kCustom, calls=%fused_computation.2 | custom fusion | bytes 6299648 | tf_op jit(solution)/shard_map/gather | solution.py:291
  70.0 69.4 %all-to-all-done = bf16[32,64,768]{2,1,0:T(8,128)(2,1)S(1)} async-done(((bf16[32,64,768]{2,1,0:T(8,128)(2,1)}), bf16[32,64,768]{2,1,0:T(8,128)(2,1)S(1)}, u32[]{:S(2)}, u32[]{:S(2)}) %all-to-all-start) | async-done | bytes 3145760 | tf_op jit(solution)/shard_map/all_to_all | solution.py:231
  155.3 9.6 gather_fusion.1
  169.6 69.4 %all-to-all-done.1 = bf16[32,64,768]{2,1,0:T(8,128)(2,1)} async-done(((bf16[32,64,768]{2,1,0:T(8,128)(2,1)}), bf16[32,64,768]{2,1,0:T(8,128)(2,1)}, u32[]{:S(2)}, u32[]{:S(2)}) %all-to-all-start.1) | async-done | bytes 3145760 | tf_op jit(solution)/shard_map/all_to_all | solution.py:231
  239.0 12.4 %gather_fusion.3 = bf16[2048,768]{1,0:T(8,128)(2,1)} fusion(bf16[2048,768]{1,0:T(8,128)(2,1)} %bitcast.16, s32[2048]{0:T(1024)S(1)} %fusion.43), kind=kCustom, calls=%fused_computation.3 | custom fusion | bytes 6299648 | tf_op jit(solution)/shard_map/gather | solution.py:291
  270.2 52.7 %attend.1 = (bf16[2048,768]{1,0:T(8,128)(2,1)}, f32[2,6,16,1024]{3,2,1,0:T(8,128)}) custom-call(bf16[2048,768]{1,0:T(8,128)(2,1)} %multiply_convert_fusion.2.q_ref, bf16[2048,768]{1,0:T(8,128)(2,1)} %convolution_convert_fusion.3.k_ref, bf16[2048,768]{1,0:T(8,128)(2,1)} %add_convert_fusion.1.v_ref, bf16[2048,128]{1,0:T(8,128)(2,1)} %bitcast.85, ...), custom_call_target="tpu_custom_call" | custom-call | flops 6442450944 | bytes 12582912 | tf_op jit(solution)/shard_map/attend/pallas_call | solution.py:101
  331.4 21.3 %multiply_convert_fusion.1 = (bf16[2048,3072]{1,0:T(8,128)(2,1)}, f32[2048,3072]{1,0:T(8,128)}) fusion(f32[3072]{0:T(1024)S(1)} %add.247, bf16[768,3072]{1,0:T(8,128)(2,1)} %all-gather.9.cloned.1.call-done, f32[2048,768]{0,1:T(8,128)} %copy-done.5, f32[768]{0:T(1024)S(1)} %add.244, f32[768]{0:T(1024)S(1)} %mul.198, f32[2048]{0:T(1024)S(1)} %add_rsqrt_fusion.1, ...), kind=kOutput, calls=%fused_computation.18 | convolution fusion | flops 9709289472 | bytes 48793600 | tf_op jit(solution)/shard_map/dot_general | solution.py:24
  352.8 18.2 %fusion.66 = (f32[2048]{0:T(1024)S(1)}, f32[2048,768]{0,1:T(8,128)}) fusion(f32[768]{0:T(1024)S(1)} %add.252, bf16[2048,3072]{1,0:T(8,128)(2,1)} %get-tuple-element.163, bf16[3072,768]{1,0:T(8,128)(2,1)} %all-gather.11.cloned.1.call-done, f32[768]{0:T(1024)S(1)} %add.244, f32[768]{0:T(1024)S(1)} %mul.198, f32[2048]{0:T(1024)S(1)} %add_rsqrt_fusion.1, ...), kind=kOutput, calls=%fused_computation.166 | convolution fusion | flops 9674684416 | bytes 29918208 | tf_op jit(solution)/shard_map/dot_general | solution.py:24
  390.2 9.4 gather_fusion.4
  399.6 17.3 %convolution_convert_fusion.1 = bf16[3072,768]{1,0:T(8,128)(2,1)} fusion(bf16[2048,3072]{1,0:T(8,128)(2,1)} %get-tuple-element.163, bf16[2048,768]{0,1:T(8,128)(2,1)} %get-tuple-element.37), kind=kOutput, calls=%fused_computation.48 | convolution fusion | flops 9666035712 | bytes 20447232 | tf_op jit(solution)/shard_map/dot_general | solution.py:32
  416.9 22.8 %convert_reduce_fusion = (f32[3072]{0:T(1024)S(1)}, bf16[2048,3072]{1,0:T(8,128)(2,1)S(1)}) fusion(bf16[2048,768]{0,1:T(8,128)(2,1)S(1)} %copy-done.9, bf16[3072,768]{1,0:T(8,128)(2,1)} %all-gather.11.cloned.1.call-done, f32[2048,3072]{1,0:T(8,128)} %get-tuple-element.164, f32[3072]{0:T(1024)S(1)} %add.247), kind=kOutput, calls=%fused_computation.16 | convolution fusion | flops 9758045184 | bytes 45637632 | tf_op jit(solution)/shard_map/dot_general | solution.py:28
  444.4 14.5 %convolution_convert_fusion = bf16[768,3072]{1,0:T(8,128)(2,1)} fusion(bf16[2048,3072]{1,0:T(8,128)(2,1)S(1)} %get-tuple-element.169, f32[2048,768]{0,1:T(8,128)} %copy-done.5, f32[768]{0:T(1024)S(1)} %add.244, f32[768]{0:T(1024)S(1)} %mul.198, f32[2048]{0:T(1024)S(1)} %add_rsqrt_fusion.1, f32[2048]{0:T(1024)S(1)} %broadcast_multiply_fusion.5), kind=kOutput, calls=%fused_computation.47 | convolution fusion | flops 9673900032 | bytes 23615488 | tf_op jit(solution)/shard_map/dot_general | solution.py:32
  458.8 21.1 %multiply_reduce_fusion.2 = (f32[768]{0:T(1024)S(1)}, f32[2048]{0:T(1024)S(1)}, f32[2048]{0:T(1024)S(1)}, f32[768]{0:T(1024)S(1)}, f32[2048,768]{0,1:T(8,128)S(1)}) fusion(f32[2048,768]{0,1:T(8,128)} %copy-done.5, f32[2048]{0:T(1024)S(1)} %add_rsqrt_fusion.1, f32[2048]{0:T(1024)S(1)} %broadcast_multiply_fusion.5, f32[768]{0:T(1024)S(1)} %mul.198, ...), kind=kOutput, calls=%fused_computation.24 | convolution fusion | flops 9699846144 | bytes 39404548 | tf_op jit(solution)/shard_map/dot_general | solution.py:28
  492.7 79.1 %attend_back.1 = (bf16[2048,768]{1,0:T(8,128)(2,1)}, bf16[2048,768]{1,0:T(8,128)(2,1)}, bf16[2048,768]{1,0:T(8,128)(2,1)}) custom-call(bf16[2048,768]{1,0:T(8,128)(2,1)} %multiply_convert_fusion.2.q_ref, bf16[2048,768]{1,0:T(8,128)(2,1)} %convolution_convert_fusion.3.k_ref, bf16[2048,768]{1,0:T(8,128)(2,1)} %add_convert_fusion.1.v_ref, ...), custom_call_target="tpu_custom_call" | custom-call | flops 16106127360 | bytes 22020096 | tf_op jit(solution)/shard_map/attend_back/pallas_call | solution.py:166
  601.0 10.5 %all_to_all.29 = f32[32,1,384]{2,1,0:T(1,128)S(1)} all-to-all(f32[32,1,384]{2,1,0:T(1,128)S(1)} %all_to_all.21), channel_id=1, replica_groups=mesh['dp'=32] {'dp'}, dimensions={0} | all-to-all | bytes 98304 | tf_op jit(solution)/shard_map/all_to_all | solution.py:361
  637.5 12.4 %gather_fusion.6 = bf16[2048,768]{1,0:T(8,128)(2,1)} fusion(bf16[2048,768]{1,0:T(8,128)(2,1)} %copy.78, s32[2048]{0:T(1024)S(1)} %copy-done.20), kind=kCustom, calls=%fused_computation.6 | custom fusion | bytes 6299648 | tf_op jit(solution)/shard_map/gather | solution.py:346
  649.9 41.3 %all-to-all-done.2 = bf16[32,64,768]{2,1,0:T(8,128)(2,1)S(1)} async-done(((bf16[32,64,768]{2,1,0:T(8,128)(2,1)}), bf16[32,64,768]{2,1,0:T(8,128)(2,1)S(1)}, u32[]{:S(2)}, u32[]{:S(2)}) %all-to-all-start.2) | async-done | bytes 3145760 | tf_op jit(solution)/shard_map/all_to_all | solution.py:231
  699.4 103.2 %reduce-scatter.13.cloned.1.call-done = bf16[24,2304]{1,0:T(8,128)(2,1)} async-done(((bf16[768,2304]{1,0:T(8,128)(2,1)}), bf16[24,2304]{1,0:T(8,128)(2,1)}) %reduce-scatter.13.cloned.1.call-update) | async-done | bytes 110608
  810.9 9.4 gather_fusion.5
  820.3 12.6 %gather_fusion.7 = bf16[2048,768]{1,0:T(8,128)(2,1)} fusion(bf16[2048,768]{1,0:T(8,128)(2,1)} %bitcast.21, s32[2048]{0:T(1024)S(1)} %copy-done.21), kind=kCustom, calls=%fused_computation.7 | custom fusion | bytes 6299648 | tf_op jit(solution)/shard_map/gather | solution.py:346
  832.9 81.7 %reduce-scatter.9.cloned.1.call-done = bf16[24,3072]{1,0:T(8,128)(2,1)} async-done(((bf16[768,3072]{1,0:T(8,128)(2,1)}), bf16[24,3072]{1,0:T(8,128)(2,1)}) %reduce-scatter.9.cloned.1.call-update) | async-done | bytes 147472 | tf_op jit(solution)/shard_map/reduce_scatter | solution.py:225
  916.3 110.1 %reduce-scatter.11.cloned.1.call-done = bf16[96,768]{1,0:T(8,128)(2,1)} async-done(((bf16[3072,768]{1,0:T(8,128)(2,1)}), bf16[96,768]{1,0:T(8,128)(2,1)}) %reduce-scatter.11.cloned.1.call-update) | async-done | bytes 147472 | tf_op jit(solution)/shard_map/reduce_scatter | solution.py:225
  (194 shorter events, 187.1 us)
Async XLA Ops:
  7.2 24.6 %copy-start = (bf16[2048,768]{1,0:T(8,128)(2,1)S(1)}, bf16[2048,768]{1,0:T(8,128)(2,1)}, u32[]{:S(2)}) copy-start(bf16[2048,768]{1,0:T(8,128)(2,1)} %param.20) | copy-start | bytes 9437188
  7.2 142.3 %all-gather.13.cloned.1.call-start = ((), (), s32[]{:S(2)}) async-start(), calls=%async_computation.15 | async-start | bytes 1622016 | tf_op jit(solution)/shard_map/all_gather | solution.py:221
  18.9 235.8 %all-gather.7.cloned.1.call-start = ((), (), s32[]{:S(2)}) async-start(), calls=%async_computation.9 | async-start | bytes 3649536 | tf_op jit(solution)/shard_map/all_gather | solution.py:221
  49.5 89.8 %all-to-all-start = ((bf16[32,64,768]{2,1,0:T(8,128)(2,1)}), bf16[32,64,768]{2,1,0:T(8,128)(2,1)S(1)}, u32[]{:S(2)}, u32[]{:S(2)}) async-start(bf16[32,64,768]{2,1,0:T(8,128)(2,1)} %bitcast.79), calls=%async_computation | async-start | bytes 6291456 | tf_op jit(solution)/shard_map/all_to_all | solution.py:231
  56.9 274.6 %all-gather.9.cloned.1.call-start = ((), (), s32[]{:S(2)}) async-start(), calls=%async_computation.10 | async-start | bytes 4866048 | tf_op jit(solution)/shard_map/all_gather | solution.py:221
  70.0 74.0 %copy-start.25 = (s32[16]{0:T(128)S(1)}, s32[16]{0:T(128)}, u32[]{:S(2)}) copy-start(s32[16]{0:T(128)} %param.24) | copy-start | bytes 196
  139.3 99.7 %all-to-all-start.1 = ((bf16[32,64,768]{2,1,0:T(8,128)(2,1)}), bf16[32,64,768]{2,1,0:T(8,128)(2,1)}, u32[]{:S(2)}, u32[]{:S(2)}) async-start(bf16[32,64,768]{2,1,0:T(8,128)(2,1)} %bitcast.77), calls=%async_computation.1 | async-start | bytes 6291456 | tf_op jit(solution)/shard_map/all_to_all | solution.py:231
  143.3 209.5 %all-gather.11.cloned.1.call-start = ((), (), s32[]{:S(2)}) async-start(), calls=%async_computation.11 | async-start | bytes 4866048 | tf_op jit(solution)/shard_map/all_gather | solution.py:221
  143.9 554.1 %reduce-scatter.7.cloned.1.call-start = ((), (), s32[]{:S(2)}) async-start(), calls=%async_computation.12 | async-start | bytes 1216512 | tf_op jit(solution)/shard_map/reduce_scatter | solution.py:225
  149.5 240.7 %copy-start.19 = (s32[2048]{0:T(1024)}, s32[2048]{0:T(1024)S(1)}, u32[]{:S(2)}) copy-start(s32[2048]{0:T(1024)S(1)} %fusion.44) | copy-start | bytes 24580
  254.6 126.9 %copy-start.3 = (bf16[2048,768]{0,1:T(8,128)(2,1)}, bf16[2048,768]{0,1:T(8,128)(2,1)S(1)}, u32[]{:S(2)}) copy-start(bf16[2048,768]{0,1:T(8,128)(2,1)S(1)} %copy.72) | copy-start | bytes 9437188
  270.2 52.7 %copy-start.14 = (bf16[2048,768]{0,1:T(8,128)(2,1)S(1)}, bf16[2048,768]{0,1:T(8,128)(2,1)}, u32[]{:S(2)}) copy-start(bf16[2048,768]{0,1:T(8,128)(2,1)} %copy.71) | copy-start | bytes 9437188
  270.2 52.7 %copy-start.16 = (bf16[32,24,768]{2,1,0:T(8,128)(2,1)S(1)}, bf16[32,24,768]{2,1,0:T(8,128)(2,1)}, u32[]{:S(2)}) copy-start(bf16[32,24,768]{2,1,0:T(8,128)(2,1)} %slice.138) | copy-start | bytes 3538948
  399.6 17.3 %copy-start.9 = (bf16[2048,768]{0,1:T(8,128)(2,1)S(1)}, bf16[2048,768]{0,1:T(8,128)(2,1)}, u32[]{:S(2)}) copy-start(bf16[2048,768]{0,1:T(8,128)(2,1)} %get-tuple-element.37) | copy-start | bytes 9437188
  444.4 14.5 %copy-start.4 = (bf16[2048,768]{0,1:T(8,128)(2,1)S(1)}, bf16[2048,768]{0,1:T(8,128)(2,1)}, u32[]{:S(2)}) copy-start(bf16[2048,768]{0,1:T(8,128)(2,1)} %copy-done.3) | copy-start | bytes 9437188
  492.7 79.1 %copy-start.11 = (bf16[2048,768]{1,0:T(8,128)(2,1)S(1)}, bf16[2048,768]{1,0:T(8,128)(2,1)}, u32[]{:S(2)}) copy-start(bf16[2048,768]{1,0:T(8,128)(2,1)} %gather_fusion.1) | copy-start | bytes 9437188
  577.5 225.1 %reduce-scatter.13.cloned.1.call-start = ((), (), s32[]{:S(2)}) async-start(), calls=%async_computation.16 | async-start | bytes 3649536
  592.9 321.8 %reduce-scatter.9.cloned.1.call-start = ((), (), s32[]{:S(2)}) async-start(), calls=%async_computation.13 | async-start | bytes 4866048 | tf_op jit(solution)/shard_map/reduce_scatter | solution.py:225
  611.5 79.7 %all-to-all-start.2 = ((bf16[32,64,768]{2,1,0:T(8,128)(2,1)}), bf16[32,64,768]{2,1,0:T(8,128)(2,1)S(1)}, u32[]{:S(2)}, u32[]{:S(2)}) async-start(bf16[32,64,768]{2,1,0:T(8,128)(2,1)} %bitcast.76), calls=%async_computation.2 | async-start | bytes 6291456 | tf_op jit(solution)/shard_map/all_to_all | solution.py:231
  614.3 412.1 %reduce-scatter.11.cloned.1.call-start = ((), (), s32[]{:S(2)}) async-start(), calls=%async_computation.14 | async-start | bytes 4866048 | tf_op jit(solution)/shard_map/reduce_scatter | solution.py:225
  615.0 11.1 %slice-start = ((s8[6291456]{0:T(1024)(128)(4,1)}), s8[4194304]{0:T(1024)(128)(4,1)S(1)}, s32[]{:S(2)}) async-start(s8[6291456]{0:T(1024)(128)(4,1)} %bitcast.74), calls=%async_computation.17 | async-start | bytes 8388608
  649.9 161.0 %copy-start.21 = (s32[2048]{0:T(1024)S(1)}, s32[2048]{0:T(1024)}, u32[]{:S(2)}) copy-start(s32[2048]{0:T(1024)} %get-tuple-element.131) | copy-start | bytes 24580
  691.2 129.1 %all-to-all-start.4 = ((bf16[32,64,768]{2,1,0:T(8,128)(2,1)}), bf16[32,64,768]{2,1,0:T(8,128)(2,1)}, u32[]{:S(2)}, u32[]{:S(2)}) async-start(bf16[32,64,768]{2,1,0:T(8,128)(2,1)} %bitcast.78), calls=%async_computation.4 | async-start | bytes 6291456 | tf_op jit(solution)/shard_map/all_to_all | solution.py:231
  820.3 207.7 %copy-start.1 = (bf16[2048,768]{1,0:T(8,128)(2,1)S(1)}, bf16[2048,768]{1,0:T(8,128)(2,1)}, u32[]{:S(2)}) copy-start(bf16[2048,768]{1,0:T(8,128)(2,1)} %param.20) | copy-start | bytes 9437188
  (18 other events, 97.6 us)
Sparse Core Ops, SparseCore 0:
  19.0 67.8 all-gather.12
  90.4 75.1 all-gather.6
  168.4 75.3 all-gather.8
  246.6 62.2 all-gather.10
  577.6 108.2 reduce-scatter.6
  691.2 111.3 reduce-scatter.12
  808.1 106.5 reduce-scatter.8
  920.1 106.2 reduce-scatter.10

commit v3 on v2

--- a/solution.py
+++ b/solution.py
@@ -222,7 +222,7 @@
 
 
 def scatter_sum(value):
-    return lax.psum_scatter(value, "dp", scatter_dimension=0, tiled=True)
+    return lax.psum_scatter(value, "dp", scatter_dimension=0, tiled=False)
 
 
 def exchange(rows, device_count):
@@ -267,11 +267,15 @@
     used = sum(sizes) + 2
     extra = -(-used // width)
     packed = jnp.concatenate(list(vectors) + [pieces, jnp.zeros((extra * width - used,), BF16)])
-    own_out = out_weight.shape[0]
-    w_qkv = gather(jnp.concatenate([query_weight, key_weight, value_weight], axis=1))
-    with_out = gather(jnp.concatenate([out_weight, packed.reshape(extra, width)], axis=0), False)
-    w_out = with_out[:, :own_out].reshape(device_count * own_out, width)
-    gathered = with_out[:, own_out:].reshape(device_count, extra * width).astype(F32)
+    own = out_weight.shape[0]
+    together = gather(
+        jnp.concatenate([query_weight, key_weight, value_weight, out_weight, packed.reshape(extra, width)], axis=0),
+        False,
+    )
+    w_q, w_k, w_v, w_out = (
+        together[:, i * own:(i + 1) * own].reshape(device_count * own, width) for i in range(4)
+    )
+    gathered = together[:, 4 * own:].reshape(device_count, extra * width).astype(F32)
     w_up = gather(up_weight)
     w_down = gather(down_weight)
     full_vectors = []
@@ -290,9 +294,6 @@
     x = exchange(tokens_out, device_count)[incoming]
     target = exchange(teacher[send_order], device_count)[incoming]
 
-    w_q = w_qkv[:, :width]
-    w_k = w_qkv[:, width:2 * width]
-    w_v = w_qkv[:, 2 * width:]
     queries = ((matmul(x, w_q) + q_b) * 0.125).astype(BF16)
     keys = matmul(x, w_k).astype(BF16)
     values = (matmul(x, w_v) + v_b).astype(BF16)
@@ -324,7 +325,20 @@
     up_grad = (slope * contract_last(down_grad, w_down)).astype(BF16)
     grad_w_up = cross_rows(hidden_low, up_grad).astype(BF16)
     grad_u_b = column_sum(up_grad)
-    grad_hidden = grad_pre_second + contract_last(up_grad, w_up)
+    up_own = up_weight.shape[0]
+    down_own = down_weight.shape[0]
+    chunks = up_weight.shape[1] // width
+    blocks = [grad_w_down.reshape(device_count, down_own, width)] + [
+        grad_w_up[:, c * width:(c + 1) * width].reshape(device_count, up_own, width) for c in range(chunks)
+    ]
+    up_grad, block = lax.optimization_barrier((up_grad, jnp.concatenate(blocks, axis=1)))
+    share_ffn = scatter_sum(block)
+    share_down = share_ffn[:down_own]
+    share_up = jnp.concatenate(
+        [share_ffn[down_own + c * up_own:down_own + (c + 1) * up_own] for c in range(chunks)], axis=1
+    )
+    back_up = contract_last(up_grad, w_up)
+    grad_hidden = grad_pre_second + back_up
     grad_s1 = column_sum(grad_hidden)
     grad_g1 = column_sum(grad_hidden * n1)
     grad_pre_first = norm_back(grad_hidden, n1, r1, g1)
@@ -332,25 +346,16 @@
     grad_w_out = cross_rows(attended, out_grad).astype(BF16)
     grad_o_b = column_sum(out_grad)
     attended_grad = contract_last(out_grad, w_out).astype(BF16)
-    attended_grad, grad_w_down, grad_w_up, grad_w_out = lax.optimization_barrier(
-        (attended_grad, grad_w_down, grad_w_up, grad_w_out)
-    )
-    share_down = scatter_sum(grad_w_down)
-    share_up = scatter_sum(grad_w_up)
-    share_out = scatter_sum(grad_w_out)
     dq, dk, dv = attend_back(queries, keys, values, attended_grad, lse, asked, barred)
     dq = dq * jnp.asarray(0.125, BF16)
-    rows_grad = (
-        grad_pre_first + contract_last(dq, w_q) + contract_last(dk, w_k) + contract_last(dv, w_v)
-    ).astype(BF16)
-    token_grad = exchange(rows_grad[back_order], device_count)[outgoing]
     grad_q_b = column_sum(dq)
     grad_v_b = column_sum(dv)
-    grad_w_qkv = jnp.concatenate(
-        [cross_rows(x, dq).astype(BF16), cross_rows(x, dk).astype(BF16), cross_rows(x, dv).astype(BF16)], axis=1
-    )
-    share_qkv = scatter_sum(grad_w_qkv).astype(F32)
-
+    blocks = [cross_rows(x, dq).astype(BF16), cross_rows(x, dk).astype(BF16), cross_rows(x, dv).astype(BF16), grad_w_out]
+    block = jnp.concatenate([g.reshape(device_count, own, width) for g in blocks], axis=1)
+    dq, dk, dv, block = lax.optimization_barrier((dq, dk, dv, block))
+    share_att = scatter_sum(block).astype(F32)
+    rows_grad = (grad_pre_first + contract_last(dq, w_q) + contract_last(dk, w_k) + contract_last(dv, w_v)).astype(BF16)
+    token_grad = exchange(rows_grad[back_order], device_count)[outgoing]
     grad_vectors = (grad_q_b, grad_v_b, grad_o_b, grad_g1, grad_s1, grad_d_b, grad_g2, grad_s2, grad_u_b)
     total_block = jnp.broadcast_to(squares.reshape(1, 1), (device_count, 1))
     grad_used = sum(sizes) + 1
@@ -371,12 +376,12 @@
         states,
         mse_loss,
         token_grad,
-        share_qkv[:, :width],
+        share_att[:own],
         h_q_b,
-        share_qkv[:, width:2 * width],
-        share_qkv[:, 2 * width:],
+        share_att[own:2 * own],
+        share_att[2 * own:3 * own],
         h_v_b,
-        share_out.astype(F32),
+        share_att[3 * own:],
         h_o_b,
         h_g1,
         h_s1,

time: 1040 us -> 890 us (0.86)
  waiting for transfers between devices: 478 us -> 342 us
  matrix products: 175 us -> 162 us
    reduce_scatter x3 -> x2, waiting for transfers between devices: 192 us -> 74.2 us  [scatter_sum(): return lax.psum_scatter(value, 'dp', scatter_dimension=0, tiled=False)]
    unnamed x9 -> x5, waiting for transfers between devices: 106 us -> 1.43 us
    all_to_all x4, waiting for transfers between devices: 180 us -> 266 us  [exchange(): slots = lax.all_to_all(slots, 'dp', split_axis=0, concat_axis=0, tiled=True)]
  transfers between devices with their start and end apart: 12 -> 9, of which waited for: 6 -> 5; matrix products, arithmetic and copies ran while one was open for 21% -> 21% of each run, Pallas kernels for 5% -> 6%
where the time goes in v3:
time: 890 us; the launch traced here: 884 us
  waiting for transfers between devices  342 us (38%)
  matrix products  162 us (18%)
  local copies, waits for them, and re-layouts  151 us (17%)
  Pallas kernels  132 us (15%)
  other arithmetic  47.6 us (5%)
  between operations  20.6 us (2%)
  starting transfers between devices  18.8 us (2%)
  blocking collectives  11.5 us (1%)
    all_to_all x4, waiting for transfers between devices, exchange(): slots = lax.all_to_all(slots, 'dp', split_axis=0, concat_axis=0, tiled=True)  266 us
    pallas_call x1, Pallas kernels, attend_back(): pl.pallas_call(attend_back_kernel, grid=(micro, PAIRS), in_specs=[wide, w...  79.2 us
    reduce_scatter x2, waiting for transfers between devices, scatter_sum(): return lax.psum_scatter(value, 'dp', scatter_dimension=0, tiled=False)  74.2 us
    dot_general x6, matrix products, contract_last(): lax.dot_general(left, right, (((1,), (1,)), ((), ())), preferred_element_...  66.2 us
    dot_general x6, matrix products, matmul(): return jnp.dot(left, right, preferred_element_type=F32)  56.4 us
    pallas_call x1, Pallas kernels, attend(): pl.pallas_call(attend_kernel, grid=(micro, PAIRS), in_specs=[wide, wide,...  52.6 us
    dot_general x6, matrix products, cross_rows(): lax.dot_general(left, right, (((0,), (0,)), ((), ())), preferred_element_...  38.5 us
    gather x3, local copies, waits for them, and re-layouts, layer_step(): target = exchange(teacher[send_order], device_count)[incoming]  27.9 us
  transfers between devices with their start and end apart: 9, of which 5 were waited for; matrix products, arithmetic and copies ran while one was open for 21% of the time, Pallas kernels for 6%

profile of v3, /device:TPU:0, one launch (start us, length us, event | category | flops | bytes accessed | tf_op | source)
XLA Modules:
  0.0 884.3 jit_solution(13195420390723870895)
XLA Ops:
  24.5 8.0 scatter_custom_fusion
  32.6 9.4 %gather_fusion = bf16[2048,768]{1,0:T(8,128)(2,1)} fusion(bf16[2048,768]{1,0:T(8,128)(2,1)S(1)} %copy-done, s32[2048]{0:T(1024)S(1)} %fusion.27), kind=kCustom, calls=%fused_computation | custom fusion | bytes 6299648 | tf_op jit(solution)/shard_map/gather | solution.py:293
  42.3 8.0 scatter_custom_fusion.1
  58.4 12.4 %gather_fusion.2 = bf16[2048,768]{1,0:T(8,128)(2,1)} fusion(bf16[2048,768]{1,0:T(8,128)(2,1)} %param.21, s32[2048]{0:T(1024)S(1)} %fusion.27), kind=kCustom, calls=%fused_computation.2 | custom fusion | bytes 6299648 | tf_op jit(solution)/shard_map/gather | solution.py:295
  70.8 78.2 %all-to-all-done = bf16[32,64,768]{2,1,0:T(8,128)(2,1)S(1)} async-done(((bf16[32,64,768]{2,1,0:T(8,128)(2,1)}), bf16[32,64,768]{2,1,0:T(8,128)(2,1)S(1)}, u32[]{:S(2)}, u32[]{:S(2)}) %all-to-all-start) | async-done | bytes 3145760 | tf_op jit(solution)/shard_map/all_to_all | solution.py:231
  159.4 9.4 %gather_fusion.1 = bf16[2048,768]{1,0:T(8,128)(2,1)} fusion(bf16[2048,768]{1,0:T(8,128)(2,1)S(1)} %bitcast.110, s32[2048]{0:T(1024)S(1)} %fusion.28), kind=kCustom, calls=%fused_computation.1 | custom fusion | bytes 6299648 | tf_op jit(solution)/shard_map/gather | solution.py:294
  173.5 69.2 %all-to-all-done.1 = bf16[32,64,768]{2,1,0:T(8,128)(2,1)} async-done(((bf16[32,64,768]{2,1,0:T(8,128)(2,1)}), bf16[32,64,768]{2,1,0:T(8,128)(2,1)}, u32[]{:S(2)}, u32[]{:S(2)}) %all-to-all-start.1) | async-done | bytes 3145760 | tf_op jit(solution)/shard_map/all_to_all | solution.py:231
  242.7 12.4 %gather_fusion.3 = bf16[2048,768]{1,0:T(8,128)(2,1)} fusion(bf16[2048,768]{1,0:T(8,128)(2,1)} %bitcast.19, s32[2048]{0:T(1024)S(1)} %fusion.28), kind=kCustom, calls=%fused_computation.3 | custom fusion | bytes 6299648 | tf_op jit(solution)/shard_map/gather | solution.py:295
  276.2 52.6 %attend.1 = (bf16[2048,768]{1,0:T(8,128)(2,1)}, f32[2,6,16,1024]{3,2,1,0:T(8,128)}) custom-call(bf16[2048,768]{1,0:T(8,128)(2,1)} %multiply_convert_fusion.2.q_ref, bf16[2048,768]{1,0:T(8,128)(2,1)} %convolution_convert_fusion.3.k_ref, bf16[2048,768]{1,0:T(8,128)(2,1)} %add_convert_fusion.1.v_ref, bf16[2048,128]{1,0:T(8,128)(2,1)} %bitcast.140, ...), custom_call_target="tpu_custom_call" | custom-call | flops 6442450944 | bytes 12582912 | tf_op jit(solution)/shard_map/attend/pallas_call | solution.py:101
  337.2 21.4 %multiply_convert_fusion.1 = (bf16[2048,3072]{1,0:T(8,128)(2,1)}, f32[2048,3072]{1,0:T(8,128)}) fusion(f32[3072]{0:T(1024)S(1)} %add.243, bf16[768,3072]{1,0:T(8,128)(2,1)} %all-gather.6.cloned.1.call-done, f32[2048,768]{0,1:T(8,128)} %copy-done.4, f32[768]{0:T(1024)S(1)} %add.240, f32[768]{0:T(1024)S(1)} %mul.198, f32[2048]{0:T(1024)S(1)} %add_rsqrt_fusion.1, ...), kind=kOutput, calls=%fused_computation.18 | convolution fusion | flops 9709289472 | bytes 48793600 | tf_op jit(solution)/shard_map/dot_general | solution.py:24
  358.6 18.1 %fusion.50 = (f32[2048]{0:T(1024)S(1)}, f32[2048,768]{0,1:T(8,128)}) fusion(f32[768]{0:T(1024)S(1)} %add.248, bf16[2048,3072]{1,0:T(8,128)(2,1)} %get-tuple-element.108, bf16[3072,768]{1,0:T(8,128)(2,1)} %all-gather.8.cloned.1.call-done, f32[768]{0:T(1024)S(1)} %add.240, f32[768]{0:T(1024)S(1)} %mul.198, f32[2048]{0:T(1024)S(1)} %add_rsqrt_fusion.1, ...), kind=kOutput, calls=%fused_computation.172 | convolution fusion | flops 9674684416 | bytes 29918208 | tf_op jit(solution)/shard_map/dot_general | solution.py:24
  398.7 9.4 %gather_fusion.4 = bf16[2048,768]{1,0:T(8,128)(2,1)} fusion(bf16[2048,768]{1,0:T(8,128)(2,1)S(1)} %copy.64, s32[2048]{0:T(1024)S(1)} %fusion.29), kind=kCustom, calls=%fused_computation.4 | custom fusion | bytes 6299648 | tf_op jit(solution)/shard_map/gather | solution.py:315
  408.1 14.4 %convolution_convert_fusion.1 = bf16[3072,768]{1,0:T(8,128)(2,1)S(1)} fusion(bf16[2048,3072]{1,0:T(8,128)(2,1)} %get-tuple-element.108, bf16[2048,768]{0,1:T(8,128)(2,1)} %get-tuple-element.39), kind=kOutput, calls=%fused_computation.48 | convolution fusion | flops 9666035712 | bytes 20447232 | tf_op jit(solution)/shard_map/dot_general | solution.py:32
  425.9 24.7 %convert_reduce_fusion = (f32[3072]{0:T(1024)S(1)}, bf16[2048,3072]{1,0:T(8,128)(2,1)}) fusion(bf16[2048,768]{0,1:T(8,128)(2,1)S(1)} %copy-done.9, bf16[3072,768]{1,0:T(8,128)(2,1)} %all-gather.8.cloned.1.call-done, f32[2048,3072]{1,0:T(8,128)} %get-tuple-element.109, f32[3072]{0:T(1024)S(1)} %add.243), kind=kOutput, calls=%fused_computation.16 | convolution fusion | flops 9758045184 | bytes 45637632 | tf_op jit(solution)/shard_map/dot_general | solution.py:28
  450.6 13.4 %convolution_convert_fusion = bf16[768,3072]{1,0:T(8,128)(2,1)S(1)} fusion(bf16[2048,3072]{1,0:T(8,128)(2,1)} %get-tuple-element.40, f32[2048,768]{0,1:T(8,128)S(1)} %bitcast.113, f32[768]{0:T(1024)S(1)} %add.240, f32[768]{0:T(1024)S(1)} %mul.198, f32[2048]{0:T(1024)S(1)} %add_rsqrt_fusion.1, f32[2048]{0:T(1024)S(1)} %broadcast_multiply_fusion.6), kind=kOutput, calls=%fused_computation.47 | convolution fusion | flops 9673900032 | bytes 23615488 | tf_op jit(solution)/shard_map/dot_general | solution.py:32
  468.8 21.1 %multiply_reduce_fusion.2 = (f32[768]{0:T(1024)S(1)}, f32[2048]{0:T(1024)S(1)}, f32[2048]{0:T(1024)S(1)}, f32[768]{0:T(1024)S(1)}, f32[2048,768]{0,1:T(8,128)S(1)}) fusion(f32[2048,768]{0,1:T(8,128)} %copy-done.4, f32[2048]{0:T(1024)S(1)} %add_rsqrt_fusion.1, f32[2048]{0:T(1024)S(1)} %broadcast_multiply_fusion.6, f32[768]{0:T(1024)S(1)} %mul.198, ...), kind=kOutput, calls=%fused_computation.24 | convolution fusion | flops 9699846144 | bytes 39404548 | tf_op jit(solution)/shard_map/dot_general | solution.py:28
  501.6 79.2 %attend_back.1 = (bf16[2048,768]{1,0:T(8,128)(2,1)}, bf16[2048,768]{1,0:T(8,128)(2,1)}, bf16[2048,768]{1,0:T(8,128)(2,1)}) custom-call(bf16[2048,768]{1,0:T(8,128)(2,1)} %multiply_convert_fusion.2.q_ref, bf16[2048,768]{1,0:T(8,128)(2,1)} %convolution_convert_fusion.3.k_ref, bf16[2048,768]{1,0:T(8,128)(2,1)} %add_convert_fusion.1.v_ref, ...), custom_call_target="tpu_custom_call" | custom-call | flops 16106127360 | bytes 22020096 | tf_op jit(solution)/shard_map/attend_back/pallas_call | solution.py:166
  601.6 11.5 %all_to_all.29 = f32[32,1,384]{2,1,0:T(1,128)S(1)} all-to-all(f32[32,1,384]{2,1,0:T(1,128)S(1)} %all_to_all.21), channel_id=1, replica_groups=mesh['dp'=32] {'dp'}, dimensions={0} | all-to-all | bytes 98304 | tf_op jit(solution)/shard_map/all_to_all | solution.py:366
  637.1 12.4 %gather_fusion.6 = bf16[2048,768]{1,0:T(8,128)(2,1)} fusion(bf16[2048,768]{1,0:T(8,128)(2,1)} %copy.69, s32[2048]{0:T(1024)S(1)} %copy-done.24), kind=kCustom, calls=%fused_computation.6 | custom fusion | bytes 6299648 | tf_op jit(solution)/shard_map/gather | solution.py:358
  649.4 56.9 %all-to-all-done.2 = bf16[32,64,768]{2,1,0:T(8,128)(2,1)S(1)} async-done(((bf16[32,64,768]{2,1,0:T(8,128)(2,1)}), bf16[32,64,768]{2,1,0:T(8,128)(2,1)S(1)}, u32[]{:S(2)}, u32[]{:S(2)}) %all-to-all-start.2) | async-done | bytes 3145760 | tf_op jit(solution)/shard_map/all_to_all | solution.py:231
  713.7 9.4 %gather_fusion.5 = bf16[2048,768]{1,0:T(8,128)(2,1)} fusion(bf16[2048,768]{1,0:T(8,128)(2,1)S(1)} %bitcast.111, s32[2048]{0:T(1024)S(1)} %copy-done.25), kind=kCustom, calls=%fused_computation.5 | custom fusion | bytes 6299648 | tf_op jit(solution)/shard_map/gather | solution.py:322
  723.1 61.8 %all-to-all-done.4 = bf16[32,64,768]{2,1,0:T(8,128)(2,1)} async-done(((bf16[32,64,768]{2,1,0:T(8,128)(2,1)}), bf16[32,64,768]{2,1,0:T(8,128)(2,1)}, u32[]{:S(2)}, u32[]{:S(2)}) %all-to-all-start.4) | async-done | bytes 3145760 | tf_op jit(solution)/shard_map/all_to_all | solution.py:231
  784.9 12.5 %gather_fusion.7 = bf16[2048,768]{1,0:T(8,128)(2,1)} fusion(bf16[2048,768]{1,0:T(8,128)(2,1)} %bitcast.33, s32[2048]{0:T(1024)S(1)} %copy-done.25), kind=kCustom, calls=%fused_computation.7 | custom fusion | bytes 6299648 | tf_op jit(solution)/shard_map/gather | solution.py:358
  799.0 74.2 %reduce-scatter.5.cloned.1.call-done = bf16[1,192,768]{2,1,0:T(8,128)(2,1)} async-done(((bf16[32,192,768]{2,1,0:T(8,128)(2,1)}), bf16[1,192,768]{2,1,0:T(8,128)(2,1)}) %reduce-scatter.5.cloned.1.call-update) | async-done | bytes 294928 | tf_op jit(solution)/shard_map/reduce_scatter | solution.py:225
  (203 shorter events, 163.7 us)
Async XLA Ops:
  7.2 25.4 %copy-start = (bf16[2048,768]{1,0:T(8,128)(2,1)S(1)}, bf16[2048,768]{1,0:T(8,128)(2,1)}, u32[]{:S(2)}) copy-start(bf16[2048,768]{1,0:T(8,128)(2,1)} %param.20) | copy-start | bytes 9437188
  7.2 251.1 %all-gather.10.cloned.1.call-start = ((), (), s32[]{:S(2)}) async-start(), calls=%async_computation.11 | async-start | bytes 5271552 | tf_op jit(solution)/shard_map/all_gather | solution.py:221
  32.6 9.6 %copy-start.26 = (s32[2048]{0:T(1024)S(1)}, s32[2048]{0:T(1024)}, u32[]{:S(2)}) copy-start(s32[2048]{0:T(1024)} %param.23) | copy-start | bytes 24580
  50.3 98.7 %all-to-all-start = ((bf16[32,64,768]{2,1,0:T(8,128)(2,1)}), bf16[32,64,768]{2,1,0:T(8,128)(2,1)S(1)}, u32[]{:S(2)}, u32[]{:S(2)}) async-start(bf16[32,64,768]{2,1,0:T(8,128)(2,1)} %bitcast.119), calls=%async_computation | async-start | bytes 6291456 | tf_op jit(solution)/shard_map/all_to_all | solution.py:231
  57.6 279.6 %all-gather.6.cloned.1.call-start = ((), (), s32[]{:S(2)}) async-start(), calls=%async_computation.7 | async-start | bytes 4866048 | tf_op jit(solution)/shard_map/all_gather | solution.py:221
  70.8 83.1 %copy-start.29 = (s32[16]{0:T(128)S(1)}, s32[16]{0:T(128)}, u32[]{:S(2)}) copy-start(s32[16]{0:T(128)} %param.24) | copy-start | bytes 196
  149.0 93.8 %all-to-all-start.1 = ((bf16[32,64,768]{2,1,0:T(8,128)(2,1)}), bf16[32,64,768]{2,1,0:T(8,128)(2,1)}, u32[]{:S(2)}, u32[]{:S(2)}) async-start(bf16[32,64,768]{2,1,0:T(8,128)(2,1)} %bitcast.117), calls=%async_computation.1 | async-start | bytes 6291456 | tf_op jit(solution)/shard_map/all_to_all | solution.py:231
  152.5 206.1 %all-gather.8.cloned.1.call-start = ((), (), s32[]{:S(2)}) async-start(), calls=%async_computation.8 | async-start | bytes 4866048 | tf_op jit(solution)/shard_map/all_gather | solution.py:221
  153.3 644.1 %reduce-scatter.3.cloned.1.call-start = ((), (), s32[]{:S(2)}) async-start(), calls=%async_computation.9 | async-start | bytes 4866048 | tf_op jit(solution)/shard_map/reduce_scatter | solution.py:225
  159.4 239.3 %copy-start.23 = (s32[2048]{0:T(1024)}, s32[2048]{0:T(1024)S(1)}, u32[]{:S(2)}) copy-start(s32[2048]{0:T(1024)S(1)} %fusion.29) | copy-start | bytes 24580
  258.3 130.1 %copy-start.2 = (bf16[2048,768]{0,1:T(8,128)(2,1)}, bf16[2048,768]{0,1:T(8,128)(2,1)S(1)}, u32[]{:S(2)}) copy-start(bf16[2048,768]{0,1:T(8,128)(2,1)S(1)} %copy.63) | copy-start | bytes 9437188
  264.3 7.9 copy-start.13
  264.3 64.5 %copy-start.20 = (bf16[32,24,768]{2,1,0:T(8,128)(2,1)}, bf16[32,24,768]{2,1,0:T(8,128)(2,1)S(1)}, u32[]{:S(2)}) copy-start(bf16[32,24,768]{2,1,0:T(8,128)(2,1)S(1)} %get-tuple-element.69) | copy-start | bytes 3538948
  276.2 52.7 %copy-start.16 = (bf16[2048,768]{0,1:T(8,128)(2,1)S(1)}, bf16[2048,768]{0,1:T(8,128)(2,1)}, u32[]{:S(2)}) copy-start(bf16[2048,768]{0,1:T(8,128)(2,1)} %copy.62) | copy-start | bytes 9437188
  422.5 28.1 %slice-start = ((s8[6291456]{0:T(1024)(128)(4,1)}), s8[4194304]{0:T(1024)(128)(4,1)S(1)}, s32[]{:S(2)}) async-start(s8[6291456]{0:T(1024)(128)(4,1)} %bitcast.112), calls=%async_computation.12 | async-start | bytes 8388608
  425.9 24.7 %slice-start.1 = ((s8[6291456]{0:T(1024)(128)(4,1)}), s8[2097152]{0:T(1024)(128)(4,1)S(1)}, s32[]{:S(2)}) async-start(s8[6291456]{0:T(1024)(128)(4,1)} %bitcast.112), calls=%async_computation.13 | async-start | bytes 4194304
  580.8 7.5 copy-start.6
  596.1 277.1 %reduce-scatter.5.cloned.1.call-start = ((), (), s32[]{:S(2)}) async-start(), calls=%async_computation.10 | async-start | bytes 9732096 | tf_op jit(solution)/shard_map/reduce_scatter | solution.py:225
  613.2 93.1 %all-to-all-start.2 = ((bf16[32,64,768]{2,1,0:T(8,128)(2,1)}), bf16[32,64,768]{2,1,0:T(8,128)(2,1)S(1)}, u32[]{:S(2)}, u32[]{:S(2)}) async-start(bf16[32,64,768]{2,1,0:T(8,128)(2,1)} %bitcast.116), calls=%async_computation.2 | async-start | bytes 6291456 | tf_op jit(solution)/shard_map/all_to_all | solution.py:231
  616.2 5.2 copy-start.15
  616.2 9.8 %slice-start.2 = ((s8[6291456]{0:T(1024)(128)(4,1)}), s8[4194304]{0:T(1024)(128)(4,1)S(1)}, s32[]{:S(2)}) async-start(s8[6291456]{0:T(1024)(128)(4,1)} %bitcast.114), calls=%async_computation.14 | async-start | bytes 8388608
  649.4 64.3 %copy-start.25 = (s32[2048]{0:T(1024)S(1)}, s32[2048]{0:T(1024)}, u32[]{:S(2)}) copy-start(s32[2048]{0:T(1024)} %get-tuple-element.63) | copy-start | bytes 24580
  706.3 78.6 %all-to-all-start.4 = ((bf16[32,64,768]{2,1,0:T(8,128)(2,1)}), bf16[32,64,768]{2,1,0:T(8,128)(2,1)}, u32[]{:S(2)}, u32[]{:S(2)}) async-start(bf16[32,64,768]{2,1,0:T(8,128)(2,1)} %bitcast.118), calls=%async_computation.4 | async-start | bytes 6291456 | tf_op jit(solution)/shard_map/all_to_all | solution.py:231
  784.9 91.5 %copy-start.1 = (bf16[2048,768]{1,0:T(8,128)(2,1)S(1)}, bf16[2048,768]{1,0:T(8,128)(2,1)}, u32[]{:S(2)}) copy-start(bf16[2048,768]{1,0:T(8,128)(2,1)} %param.20) | copy-start | bytes 9437188
  (21 other events, 76.6 us)
Sparse Core Ops, SparseCore 0:
  21.3 90.3 all-gather.9
  114.6 88.5 all-gather.5
  206.1 66.8 all-gather.7
  596.3 134.6 reduce-scatter.2
  736.7 136.4 reduce-scatter.4

commit v4 on v3

--- a/solution.py
+++ b/solution.py
@@ -180,20 +180,105 @@
     )(queries, keys, values, grads, lse, asked, barred)
 
 
-def norm_stats(value):
-    center = value - jnp.mean(value, axis=-1, keepdims=True)
-    spread = jnp.mean(center * center, axis=-1, keepdims=True)
-    scale = lax.rsqrt(spread + EPSILON)
-    return center * scale, scale
-
-
-def norm_back(grad, normed, scale, gain):
-    u = grad * gain
-    return scale * (
-        u
-        - jnp.mean(u, axis=-1, keepdims=True)
-        - normed * jnp.mean(u * normed, axis=-1, keepdims=True)
-    )
+def row_mean(value):
+    return jnp.sum(value, axis=-1, keepdims=True) * (1.0 / value.shape[-1])
+
+
+def middle_kernel(
+    att_ref, x_ref, target_ref, usable_ref, w_out_ref, w_up_ref, w_down_ref, vec_ref, ub_ref,
+    states_ref, hidden_ref, act_ref, down_ref, up_ref, first_ref, out_ref, attg_ref, sums_ref, ubsum_ref,
+    slope_ref,
+):
+    width = x_ref.shape[1]
+    chunks = w_up_ref.shape[1] // width
+    o_b, g1, s1, d_b, g2, s2, scale = (vec_ref[i:i + 1, :] for i in range(7))
+
+    @pl.when(pl.program_id(0) == 0)
+    def _():
+        sums_ref[...] = jnp.zeros_like(sums_ref)
+        ubsum_ref[...] = jnp.zeros_like(ubsum_ref)
+
+    pre_first = x_ref[...].astype(F32) + (matmul(att_ref[...], w_out_ref[...]) + o_b)
+    center = pre_first - row_mean(pre_first)
+    r1 = lax.rsqrt(row_mean(center * center) + EPSILON)
+    n1 = center * r1
+    hidden = n1 * g1 + s1
+    hidden_low = hidden.astype(BF16)
+    hidden_ref[...] = hidden_low
+    total = hidden + d_b
+    for c in range(chunks):
+        cols = slice(c * width, (c + 1) * width)
+        pre_act = matmul(hidden_low, w_up_ref[:, cols]) + ub_ref[0:1, cols]
+        cdf = 0.5 * (1.0 + lax.erf(pre_act * (2.0 ** -0.5)))
+        act_low = (pre_act * cdf).astype(BF16)
+        slope = cdf + pre_act * (jnp.exp(-0.5 * pre_act * pre_act) * 0.3989422804014327)
+        act_ref[:, cols] = act_low
+        slope_ref[:, cols] = slope.astype(BF16)
+        total += matmul(act_low, w_down_ref[cols, :])
+    center = total - row_mean(total)
+    r2 = lax.rsqrt(row_mean(center * center) + EPSILON)
+    n2 = center * r2
+    layer_out = n2 * g2 + s2
+    states_ref[...] = layer_out.astype(BF16)
+    misfit = jnp.where(usable_ref[...] > 0.5, layer_out - target_ref[...].astype(F32), 0.0)
+    grad_out = misfit * scale
+    u = grad_out * g2
+    grad_second = r2 * (u - row_mean(u) - n2 * row_mean(u * n2))
+    down_grad = grad_second.astype(BF16)
+    down_ref[...] = down_grad
+    sums_ref[0:1, :] += jnp.sum(grad_out, axis=0, keepdims=True)
+    sums_ref[1:2, :] += jnp.sum(grad_out * n2, axis=0, keepdims=True)
+    sums_ref[2:3, :] += jnp.sum(down_grad.astype(F32), axis=0, keepdims=True)
+    sums_ref[6:7, :] += jnp.sum(misfit * misfit, axis=0, keepdims=True)
+    grad_hidden = grad_second
+    for c in range(chunks):
+        cols = slice(c * width, (c + 1) * width)
+        grad_act = contract_last(down_grad, w_down_ref[cols, :])
+        up_grad = (slope_ref[:, cols].astype(F32) * grad_act).astype(BF16)
+        up_ref[:, cols] = up_grad
+        ubsum_ref[0:1, cols] += jnp.sum(up_grad.astype(F32), axis=0, keepdims=True)
+        grad_hidden += contract_last(up_grad, w_up_ref[:, cols])
+    u = grad_hidden * g1
+    grad_first = r1 * (u - row_mean(u) - n1 * row_mean(u * n1))
+    first_ref[...] = grad_first
+    out_grad = grad_first.astype(BF16)
+    out_ref[...] = out_grad
+    sums_ref[3:4, :] += jnp.sum(grad_hidden, axis=0, keepdims=True)
+    sums_ref[4:5, :] += jnp.sum(grad_hidden * n1, axis=0, keepdims=True)
+    sums_ref[5:6, :] += jnp.sum(out_grad.astype(F32), axis=0, keepdims=True)
+    attg_ref[...] = contract_last(out_grad, w_out_ref[...]).astype(BF16)
+
+
+def middle(attended, x, target, usable, w_out, w_up, w_down, vectors, u_b):
+    rows, width = x.shape
+    wide = w_up.shape[1]
+    row = pl.BlockSpec((TILE, width), lambda i: (i, 0))
+    long = pl.BlockSpec((TILE, wide), lambda i: (i, 0))
+    whole = lambda shape: pl.BlockSpec(shape, lambda i: (0, 0), pipeline_mode=pl.Buffered(1))
+    still = lambda shape: pl.BlockSpec(shape, lambda i: (0, 0))
+    shape = jax.ShapeDtypeStruct
+    return pl.pallas_call(
+        middle_kernel,
+        grid=(rows // TILE,),
+        in_specs=[
+            row, row, row, pl.BlockSpec((TILE, 1), lambda i: (i, 0)),
+            whole(w_out.shape), whole(w_up.shape), whole(w_down.shape), whole(vectors.shape), whole(u_b.shape),
+        ],
+        out_specs=[row, row, long, row, long, row, row, row, still((8, width)), still((8, wide))],
+        out_shape=(
+            shape((rows, width), BF16), shape((rows, width), BF16), shape((rows, wide), BF16),
+            shape((rows, width), BF16), shape((rows, wide), BF16), shape((rows, width), F32),
+            shape((rows, width), BF16), shape((rows, width), BF16), shape((8, width), F32), shape((8, wide), F32),
+        ),
+        scratch_shapes=[pltpu.VMEM((TILE, wide), BF16)],
+        compiler_params=pltpu.CompilerParams(vmem_limit_bytes=58 << 20),
+        cost_estimate=pl.CostEstimate(
+            flops=2 * rows * width * (2 * width + 4 * wide),
+            transcendentals=2 * rows * wide,
+            bytes_accessed=rows * (width * 20 + wide * 4) + 4 * wide * width,
+        ),
+        name="middle",
+    )(attended, x, target, usable, w_out, w_up, w_down, vectors, u_b)
 
 
 def slot_positions(targets, rows_dev, slot_rows, device_count):
@@ -298,54 +383,31 @@
     keys = matmul(x, w_k).astype(BF16)
     values = (matmul(x, w_v) + v_b).astype(BF16)
     attended, lse = attend(queries, keys, values, asked, barred)
-    pre_first = x + (matmul(attended, w_out) + o_b)
-    n1, r1 = norm_stats(pre_first)
-    hidden = n1 * g1 + s1
-    hidden_low = hidden.astype(BF16)
-    pre_act = matmul(hidden_low, w_up) + u_b
-    cdf = 0.5 * (1.0 + lax.erf(pre_act * (2.0 ** -0.5)))
-    act_low = (pre_act * cdf).astype(BF16)
-    slope = (cdf + pre_act * (jnp.exp(-0.5 * pre_act * pre_act) * 0.3989422804014327)).astype(BF16)
-    pre_second = hidden + (matmul(act_low, w_down) + d_b)
-    n2, r2 = norm_stats(pre_second)
-    layer_out = n2 * g2 + s2
-    misfit = jnp.where(usable[:, None], layer_out - target.astype(F32), 0.0)
-    states_routed = layer_out.astype(BF16)
-    squares = jnp.sum(misfit * misfit)
+    scale = rows_dev * device_count * 2.0 / valid_count
+    vectors = jnp.stack([o_b, g1, s1, d_b, g2, s2, jnp.full((width,), scale, F32), jnp.zeros((width,), F32)])
+    (
+        states_routed, hidden_low, act_low, down_grad, up_grad, grad_pre_first, out_grad, attended_grad, sums, up_sums,
+    ) = middle(attended, x, target, usable.astype(F32)[:, None], w_out, w_up, w_down, vectors, u_b[None])
+    grad_s2, grad_g2, grad_d_b, grad_s1, grad_g1, grad_o_b = (sums[i] for i in range(6))
+    squares = jnp.sum(sums[6])
+    grad_u_b = up_sums[0]
     states_out = states_routed[back_order]
-
-    grad_out = misfit * (rows_dev * device_count * 2.0 / valid_count)
-    grad_s2 = column_sum(grad_out)
-    grad_g2 = column_sum(grad_out * n2)
-    grad_pre_second = norm_back(grad_out, n2, r2, g2)
-    down_grad, states_out = lax.optimization_barrier((grad_pre_second.astype(BF16), states_out))
     states = exchange(states_out, device_count)[outgoing]
     grad_w_down = cross_rows(act_low, down_grad).astype(BF16)
-    grad_d_b = column_sum(down_grad)
-    up_grad = (slope * contract_last(down_grad, w_down)).astype(BF16)
     grad_w_up = cross_rows(hidden_low, up_grad).astype(BF16)
-    grad_u_b = column_sum(up_grad)
     up_own = up_weight.shape[0]
     down_own = down_weight.shape[0]
     chunks = up_weight.shape[1] // width
     blocks = [grad_w_down.reshape(device_count, down_own, width)] + [
         grad_w_up[:, c * width:(c + 1) * width].reshape(device_count, up_own, width) for c in range(chunks)
     ]
-    up_grad, block = lax.optimization_barrier((up_grad, jnp.concatenate(blocks, axis=1)))
+    attended_grad, block = lax.optimization_barrier((attended_grad, jnp.concatenate(blocks, axis=1)))
     share_ffn = scatter_sum(block)
     share_down = share_ffn[:down_own]
     share_up = jnp.concatenate(
         [share_ffn[down_own + c * up_own:down_own + (c + 1) * up_own] for c in range(chunks)], axis=1
     )
-    back_up = contract_last(up_grad, w_up)
-    grad_hidden = grad_pre_second + back_up
-    grad_s1 = column_sum(grad_hidden)
-    grad_g1 = column_sum(grad_hidden * n1)
-    grad_pre_first = norm_back(grad_hidden, n1, r1, g1)
-    out_grad = grad_pre_first.astype(BF16)
     grad_w_out = cross_rows(attended, out_grad).astype(BF16)
-    grad_o_b = column_sum(out_grad)
-    attended_grad = contract_last(out_grad, w_out).astype(BF16)
     dq, dk, dv = attend_back(queries, keys, values, attended_grad, lse, asked, barred)
     dq = dq * jnp.asarray(0.125, BF16)
     grad_q_b = column_sum(dq)

time: 890 us -> 848 us (0.953)
  matrix products: 162 us -> 73.6 us
  Pallas kernels: 132 us -> 202 us
  other arithmetic: 47.6 us -> 22.3 us
  waiting for transfers between devices: 342 us -> 359 us
  local copies, waits for them, and re-layouts: 151 us -> 139 us
  blocking collectives: 11.5 us -> 0 us
    pallas_call x0 -> x1, Pallas kernels: none -> 70.8 us  [middle(): pl.pallas_call(middle_kernel, grid=(rows // TILE,), in_specs=[row, row, r...]
    all_to_all x4, waiting for transfers between devices: 266 us -> 317 us  [exchange(): slots = lax.all_to_all(slots, 'dp', split_axis=0, concat_axis=0, tiled=True)]
    dot_general x6 -> x3, matrix products: 56.4 us -> 11.9 us  [matmul(): return jnp.dot(left, right, preferred_element_type=F32)]
    dot_general x6 -> x3, matrix products: 66.2 us -> 23.4 us  [contract_last(): lax.dot_general(left, right, (((1,), (1,)), ((), ())), preferred_element_...]
    reduce_scatter x2, waiting for transfers between devices: 74.2 us -> 40.3 us  [scatter_sum(): return lax.psum_scatter(value, 'dp', scatter_dimension=0, tiled=False)]
    all_to_all x1 -> x0, blocking collectives: 11.5 us -> none  [layer_step(): lax.all_to_all(grad_packed, 'dp', split_axis=0, concat_axis=0, tiled=True)]
    reduce_sum x3 -> x1, other arithmetic: 11.7 us -> 0.65 us  [layer_step(): squares = jnp.sum(sums[6])]
    gather x3 -> x2, local copies, waits for them, and re-layouts: 27.9 us -> 24.7 us  [layer_step(): target = exchange(teacher[send_order], device_count)[incoming]]
  transfers between devices with their start and end apart: 9 -> 10, of which waited for: 5 -> 5; matrix products, arithmetic and copies ran while one was open for 21% -> 20% of each run, Pallas kernels for 6% -> 6%
where the time goes in v4:
time: 848 us; the launch traced here: 842 us
  waiting for transfers between devices  359 us (42%)
  Pallas kernels  202 us (24%)
  local copies, waits for them, and re-layouts  139 us (16%)
  matrix products  73.6 us (9%)
  starting transfers between devices  25.3 us (3%)
  other arithmetic  22.3 us (3%)
  between operations  20.6 us (2%)
    all_to_all x4, waiting for transfers between devices, exchange(): slots = lax.all_to_all(slots, 'dp', split_axis=0, concat_axis=0, tiled=True)  317 us
    pallas_call x1, Pallas kernels, attend_back(): pl.pallas_call(attend_back_kernel, grid=(micro, PAIRS), in_specs=[wide, w...  79.2 us
    pallas_call x1, Pallas kernels, middle(): pl.pallas_call(middle_kernel, grid=(rows // TILE,), in_specs=[row, row, r...  70.8 us
    pallas_call x1, Pallas kernels, attend(): pl.pallas_call(attend_kernel, grid=(micro, PAIRS), in_specs=[wide, wide,...  52.3 us
    reduce_scatter x2, waiting for transfers between devices, scatter_sum(): return lax.psum_scatter(value, 'dp', scatter_dimension=0, tiled=False)  40.3 us
    dot_general x6, matrix products, cross_rows(): lax.dot_general(left, right, (((0,), (0,)), ((), ())), preferred_element_...  37.9 us
    gather x2, local copies, waits for them, and re-layouts, layer_step(): target = exchange(teacher[send_order], device_count)[incoming]  24.7 us
    dot_general x3, matrix products, contract_last(): lax.dot_general(left, right, (((1,), (1,)), ((), ())), preferred_element_...  23.4 us
  transfers between devices with their start and end apart: 10, of which 5 were waited for; matrix products, arithmetic and copies ran while one was open for 20% of the time, Pallas kernels for 6%

profile of v4, /device:TPU:0, one launch (start us, length us, event | category | flops | bytes accessed | tf_op | source)
XLA Modules:
  0.0 842.2 jit_solution(1821487582333825420)
XLA Ops:
  14.4 6.1 concatenate.26
  25.3 8.0 scatter_custom_fusion
  33.4 9.4 %gather_fusion = bf16[2048,768]{1,0:T(8,128)(2,1)} fusion(bf16[2048,768]{1,0:T(8,128)(2,1)S(1)} %copy-done, s32[2048]{0:T(1024)S(1)} %fusion.20), kind=kCustom, calls=%fused_computation | custom fusion | bytes 6299648 | tf_op jit(solution)/shard_map/gather | solution.py:378
  43.0 8.6 %scatter_custom_fusion.1 = s32[2048]{0:T(1024)} fusion(s32[2048]{0:T(1024)S(1)} %get-tuple-element.77, s32[2048]{0:T(1024)S(1)} %iota.69, s32[]{:T(128)} %constant.69.clone.1), kind=kCustom, calls=%fused_computation.109 | custom fusion | bytes 8196 | tf_op jit(solution)/shard_map/scatter | solution.py:301
  51.6 7.3 all-to-all-start
  59.0 12.4 %gather_fusion.2 = bf16[2048,768]{1,0:T(8,128)(2,1)} fusion(bf16[2048,768]{1,0:T(8,128)(2,1)} %param.21, s32[2048]{0:T(1024)S(1)} %fusion.20), kind=kCustom, calls=%fused_computation.2 | custom fusion | bytes 6299648 | tf_op jit(solution)/shard_map/gather | solution.py:380
  71.3 78.2 %all-to-all-done = bf16[32,64,768]{2,1,0:T(8,128)(2,1)S(1)} async-done(((bf16[32,64,768]{2,1,0:T(8,128)(2,1)}), bf16[32,64,768]{2,1,0:T(8,128)(2,1)S(1)}, u32[]{:S(2)}, u32[]{:S(2)}) %all-to-all-start) | async-done | bytes 3145760 | tf_op jit(solution)/shard_map/all_to_all | solution.py:316
  162.1 9.4 %gather_fusion.1 = bf16[2048,768]{1,0:T(8,128)(2,1)} fusion(bf16[2048,768]{1,0:T(8,128)(2,1)S(1)} %bitcast.107, s32[2048]{0:T(1024)S(1)} %fusion.21), kind=kCustom, calls=%fused_computation.1 | custom fusion | bytes 6299648 | tf_op jit(solution)/shard_map/gather | solution.py:379
  171.5 76.2 %all-to-all-done.1 = bf16[32,64,768]{2,1,0:T(8,128)(2,1)} async-done(((bf16[32,64,768]{2,1,0:T(8,128)(2,1)}), bf16[32,64,768]{2,1,0:T(8,128)(2,1)}, u32[]{:S(2)}, u32[]{:S(2)}) %all-to-all-start.1) | async-done | bytes 3145760 | tf_op jit(solution)/shard_map/all_to_all | solution.py:316
  247.6 12.3 %gather_fusion.3 = bf16[2048,768]{1,0:T(8,128)(2,1)} fusion(bf16[2048,768]{1,0:T(8,128)(2,1)} %bitcast.18, s32[2048]{0:T(1024)S(1)} %fusion.21), kind=kCustom, calls=%fused_computation.3 | custom fusion | bytes 6299648 | tf_op jit(solution)/shard_map/gather | solution.py:380
  280.4 52.3 %attend.1 = (bf16[2048,768]{1,0:T(8,128)(2,1)}, f32[2,6,16,1024]{3,2,1,0:T(8,128)}) custom-call(bf16[2048,768]{1,0:T(8,128)(2,1)} %multiply_convert_fusion.q_ref, bf16[2048,768]{1,0:T(8,128)(2,1)} %convolution_convert_fusion.2.k_ref, bf16[2048,768]{1,0:T(8,128)(2,1)} %add_convert_fusion.1.v_ref, bf16[2048,128]{1,0:T(8,128)(2,1)} %bitcast.133, ...), custom_call_target="tpu_custom_call" | custom-call | flops 6442450944 | bytes 12582912 | tf_op jit(solution)/shard_map/attend/pallas_call | solution.py:101
  332.7 70.8 %middle.1 = (bf16[2048,768]{1,0:T(8,128)(2,1)}, bf16[2048,768]{1,0:T(8,128)(2,1)}, bf16[2048,3072]{1,0:T(8,128)(2,1)}, bf16[2048,768]{1,0:T(8,128)(2,1)}, bf16[2...) custom-call(bf16[2048,768]{1,0:T(8,128)(2,1)} %get-tuple-element.44., ...), custom_call_target="tpu_custom_call" | custom-call | flops 43486543872 | bytes 66060288 | tf_op jit(solution)/shard_map/middle/pallas_call | solution.py:260
  403.6 14.3 %convolution_convert_fusion = bf16[768,3072]{1,0:T(8,128)(2,1)S(1)} fusion(bf16[2048,768]{1,0:T(8,128)(2,1)} %get-tuple-element.50, bf16[2048,3072]{1,0:T(8,128)(2,1)} %get-tuple-element.51), kind=kOutput, calls=%fused_computation.15 | convolution fusion | flops 9666035712 | bytes 20447232 | tf_op jit(solution)/shard_map/dot_general | solution.py:32
  419.7 11.0 %convolution_convert_fusion.1 = bf16[3072,768]{1,0:T(8,128)(2,1)S(1)} fusion(bf16[2048,3072]{1,0:T(8,128)(2,1)S(1)} %copy-done.20, bf16[2048,768]{1,0:T(8,128)(2,1)S(1)} %copy-done.21), kind=kOutput, calls=%fused_computation.16 | convolution fusion | flops 9666035712 | bytes 20447232 | tf_op jit(solution)/shard_map/dot_general | solution.py:32
  437.7 79.2 %attend_back.1 = (bf16[2048,768]{1,0:T(8,128)(2,1)}, bf16[2048,768]{1,0:T(8,128)(2,1)}, bf16[2048,768]{1,0:T(8,128)(2,1)}) custom-call(bf16[2048,768]{1,0:T(8,128)(2,1)} %multiply_convert_fusion.q_ref, bf16[2048,768]{1,0:T(8,128)(2,1)} %convolution_convert_fusion.2.k_ref, bf16[2048,768]{1,0:T(8,128)(2,1)} %add_convert_fusion.1.v_ref, ...), custom_call_target="tpu_custom_call" | custom-call | flops 16106127360 | bytes 22020096 | tf_op jit(solution)/shard_map/attend_back/pallas_call | solution.py:166
  546.6 7.8 fusion.36
  559.0 11.1 %add_convert_fusion = bf16[2048,768]{1,0:T(8,128)(2,1)S(1)} fusion(f32[2048,768]{1,0:T(8,128)} %fusion.37, f32[2048,768]{1,0:T(8,128)} %get-tuple-element.58, f32[2048,768]{1,0:T(8,128)} %fusion.36, bf16[2048,768]{1,0:T(8,128)(2,1)} %get-tuple-element.63, bf16[768,768]{1,0:T(8,128)(2,1)} %bitcast.114), kind=kOutput, calls=%fused_computation.10 | convolution fusion | flops 2422210560 | bytes 26345472 | tf_op jit(solution)/shard_map/dot_general | solution.py:28
  570.1 9.4 %gather_fusion.6 = bf16[2048,768]{1,0:T(8,128)(2,1)} fusion(bf16[2048,768]{1,0:T(8,128)(2,1)S(1)} %add_convert_fusion, s32[2048]{0:T(1024)S(1)} %fusion.22), kind=kCustom, calls=%fused_computation.6 | custom fusion | bytes 6299648 | tf_op jit(solution)/shard_map/gather | solution.py:420
  585.3 12.4 %gather_fusion.4 = bf16[2048,768]{1,0:T(8,128)(2,1)} fusion(bf16[2048,768]{1,0:T(8,128)(2,1)} %get-tuple-element.45, s32[2048]{0:T(1024)S(1)} %fusion.22), kind=kCustom, calls=%fused_computation.4 | custom fusion | bytes 6299648 | tf_op jit(solution)/shard_map/gather | solution.py:394
  597.7 78.4 %all-to-all-done.4 = bf16[32,64,768]{2,1,0:T(8,128)(2,1)S(1)} async-done(((bf16[32,64,768]{2,1,0:T(8,128)(2,1)}), bf16[32,64,768]{2,1,0:T(8,128)(2,1)S(1)}, u32[]{:S(2)}, u32[]{:S(2)}) %all-to-all-start.4) | async-done | bytes 3145760 | tf_op jit(solution)/shard_map/all_to_all | solution.py:316
  683.0 9.4 %gather_fusion.7 = bf16[2048,768]{1,0:T(8,128)(2,1)} fusion(bf16[2048,768]{1,0:T(8,128)(2,1)S(1)} %bitcast.108, s32[2048]{0:T(1024)S(1)} %copy-done.11), kind=kCustom, calls=%fused_computation.7 | custom fusion | bytes 6299648 | tf_op jit(solution)/shard_map/gather | solution.py:420
  692.4 84.0 %all-to-all-done.2 = bf16[32,64,768]{2,1,0:T(8,128)(2,1)} async-done(((bf16[32,64,768]{2,1,0:T(8,128)(2,1)}), bf16[32,64,768]{2,1,0:T(8,128)(2,1)}, u32[]{:S(2)}, u32[]{:S(2)}) %all-to-all-start.2) | async-done | bytes 3145760 | tf_op jit(solution)/shard_map/all_to_all | solution.py:316
  776.4 12.5 %gather_fusion.5 = bf16[2048,768]{1,0:T(8,128)(2,1)} fusion(bf16[2048,768]{1,0:T(8,128)(2,1)} %bitcast.21, s32[2048]{0:T(1024)S(1)} %copy-done.11), kind=kCustom, calls=%fused_computation.5 | custom fusion | bytes 6299648 | tf_op jit(solution)/shard_map/gather | solution.py:395
  790.6 40.3 %reduce-scatter.5.cloned.1.call-done = bf16[1,192,768]{2,1,0:T(8,128)(2,1)} async-done(((bf16[32,192,768]{2,1,0:T(8,128)(2,1)}), bf16[1,192,768]{2,1,0:T(8,128)(2,1)}) %reduce-scatter.5.cloned.1.call-update) | async-done | bytes 294928 | tf_op jit(solution)/shard_map/reduce_scatter | solution.py:310
  (158 shorter events, 100.8 us)
Async XLA Ops:
  7.2 26.2 %copy-start = (bf16[2048,768]{1,0:T(8,128)(2,1)S(1)}, bf16[2048,768]{1,0:T(8,128)(2,1)}, u32[]{:S(2)}) copy-start(bf16[2048,768]{1,0:T(8,128)(2,1)} %param.20) | copy-start | bytes 9437188
  7.2 252.8 %all-gather.10.cloned.1.call-start = ((), (), s32[]{:S(2)}) async-start(), calls=%async_computation.11 | async-start | bytes 5271552 | tf_op jit(solution)/shard_map/all_gather | solution.py:306
  21.2 311.5 %all-gather.6.cloned.1.call-start = ((), (), s32[]{:S(2)}) async-start(), calls=%async_computation.7 | async-start | bytes 4866048 | tf_op jit(solution)/shard_map/all_gather | solution.py:306
  33.4 9.6 %copy-start.13 = (s32[2048]{0:T(1024)S(1)}, s32[2048]{0:T(1024)}, u32[]{:S(2)}) copy-start(s32[2048]{0:T(1024)} %param.23) | copy-start | bytes 24580
  51.6 97.9 %all-to-all-start = ((bf16[32,64,768]{2,1,0:T(8,128)(2,1)}), bf16[32,64,768]{2,1,0:T(8,128)(2,1)S(1)}, u32[]{:S(2)}, u32[]{:S(2)}) async-start(bf16[32,64,768]{2,1,0:T(8,128)(2,1)} %bitcast.111), calls=%async_computation | async-start | bytes 6291456 | tf_op jit(solution)/shard_map/all_to_all | solution.py:316
  149.5 5.6 copy-start.15
  149.5 98.1 %all-to-all-start.1 = ((bf16[32,64,768]{2,1,0:T(8,128)(2,1)}), bf16[32,64,768]{2,1,0:T(8,128)(2,1)}, u32[]{:S(2)}, u32[]{:S(2)}) async-start(bf16[32,64,768]{2,1,0:T(8,128)(2,1)} %bitcast.109), calls=%async_computation.1 | async-start | bytes 6291456 | tf_op jit(solution)/shard_map/all_to_all | solution.py:316
  154.1 178.6 %all-gather.8.cloned.1.call-start = ((), (), s32[]{:S(2)}) async-start(), calls=%async_computation.8 | async-start | bytes 4866048 | tf_op jit(solution)/shard_map/all_gather | solution.py:306
  154.9 634.0 %reduce-scatter.3.cloned.1.call-start = ((), (), s32[]{:S(2)}) async-start(), calls=%async_computation.9 | async-start | bytes 4866048 | tf_op jit(solution)/shard_map/reduce_scatter | solution.py:310
  264.7 3.8 copy-start.5
  268.5 4.0 copy-start.7
  268.5 4.0 copy-start.4
  268.5 7.9 copy-start.9
  403.5 14.6 %copy-start.20 = (bf16[2048,3072]{1,0:T(8,128)(2,1)S(1)}, bf16[2048,3072]{1,0:T(8,128)(2,1)}, u32[]{:S(2)}) copy-start(bf16[2048,3072]{1,0:T(8,128)(2,1)} %get-tuple-element.48) | copy-start | bytes 37748740
  437.7 79.2 %copy-start.6 = (bf16[2048,768]{1,0:T(8,128)(2,1)S(1)}, bf16[2048,768]{1,0:T(8,128)(2,1)}, u32[]{:S(2)}) copy-start(bf16[2048,768]{1,0:T(8,128)(2,1)} %gather_fusion.1) | copy-start | bytes 9437188
  516.9 4.7 copy-start.3
  543.1 36.4 %all-to-all-start.3 = ((f32[32,1,384]{2,1,0:T(1,128)}), f32[32,1,384]{2,1,0:T(1,128)S(1)}, u32[]{:S(2)}, u32[]{:S(2)}) async-start(f32[32,1,384]{2,1,0:T(1,128)} %all_to_all.21), calls=%async_computation.3 | async-start | bytes 98304 | tf_op jit(solution)/shard_map/all_to_all | solution.py:428
  546.6 7.9 copy-start.8
  546.6 284.3 %reduce-scatter.5.cloned.1.call-start = ((), (), s32[]{:S(2)}) async-start(), calls=%async_computation.10 | async-start | bytes 9732096 | tf_op jit(solution)/shard_map/reduce_scatter | solution.py:310
  546.6 7.8 copy-start.17
  579.5 96.6 %all-to-all-start.4 = ((bf16[32,64,768]{2,1,0:T(8,128)(2,1)}), bf16[32,64,768]{2,1,0:T(8,128)(2,1)S(1)}, u32[]{:S(2)}, u32[]{:S(2)}) async-start(bf16[32,64,768]{2,1,0:T(8,128)(2,1)} %bitcast.112), calls=%async_computation.4 | async-start | bytes 6291456 | tf_op jit(solution)/shard_map/all_to_all | solution.py:316
  676.1 6.9 copy-start.11
  676.1 100.3 %all-to-all-start.2 = ((bf16[32,64,768]{2,1,0:T(8,128)(2,1)}), bf16[32,64,768]{2,1,0:T(8,128)(2,1)}, u32[]{:S(2)}, u32[]{:S(2)}) async-start(bf16[32,64,768]{2,1,0:T(8,128)(2,1)} %bitcast.110), calls=%async_computation.2 | async-start | bytes 6291456 | tf_op jit(solution)/shard_map/all_to_all | solution.py:316
  776.4 57.7 %copy-start.1 = (bf16[2048,768]{1,0:T(8,128)(2,1)S(1)}, bf16[2048,768]{1,0:T(8,128)(2,1)}, u32[]{:S(2)}) copy-start(bf16[2048,768]{1,0:T(8,128)(2,1)} %param.20) | copy-start | bytes 9437188
  (8 other events, 17.8 us)
Sparse Core Ops, SparseCore 0:
  21.3 90.4 all-gather.9
  114.7 85.1 all-gather.5
  202.8 67.4 all-gather.7
  535.6 138.8 reduce-scatter.2
  680.3 150.5 reduce-scatter.4

commit v5 on v4

--- a/solution.py
+++ b/solution.py
@@ -296,10 +296,38 @@
     return owner_dev * slot_rows + rank.reshape(rows_dev).astype(jnp.int32)
 
 
-def invert(positions):
-    return (
-        jnp.zeros_like(positions).at[positions].set(jnp.arange(positions.shape[0], dtype=jnp.int32))
-    )
+def place_kernel(pos_ref, rows_ref, out_ref):
+    count = rows_ref.shape[0]
+    first = pl.program_id(0) * TILE
+    wanted = lax.broadcasted_iota(jnp.int32, (TILE, count), 0) + first
+    chosen = jnp.where(wanted == pos_ref[0:1, :], 1.0, 0.0).astype(BF16)
+    out_ref[...] = matmul(chosen, rows_ref[...]).astype(BF16)
+
+
+def pick_kernel(pos_ref, rows_ref, out_ref):
+    count = rows_ref.shape[0]
+    column = jnp.broadcast_to(pos_ref[0:1, :].astype(F32), (BLOCK, TILE)).T[:, 0:1].astype(jnp.int32)
+    chosen = jnp.where(lax.broadcasted_iota(jnp.int32, (TILE, count), 1) == column, 1.0, 0.0).astype(BF16)
+    out_ref[...] = matmul(chosen, rows_ref[...]).astype(BF16)
+
+
+def permute(positions, rows, pick):
+    count, width = rows.shape
+    if pick:
+        pos_spec = pl.BlockSpec((1, TILE), lambda i: (0, i))
+    else:
+        pos_spec = pl.BlockSpec((1, count), lambda i: (0, 0))
+    return pl.pallas_call(
+        pick_kernel if pick else place_kernel,
+        grid=(count // TILE,),
+        in_specs=[pos_spec, pl.BlockSpec((count, width), lambda i: (0, 0), pipeline_mode=pl.Buffered(1))],
+        out_specs=pl.BlockSpec((TILE, width), lambda i: (i, 0)),
+        out_shape=jax.ShapeDtypeStruct((count, width), BF16),
+        cost_estimate=pl.CostEstimate(
+            flops=2 * count * count * width, transcendentals=0, bytes_accessed=4 * count * width
+        ),
+        name="pick" if pick else "place",
+    )(positions.reshape(1, count), rows)
 
 
 def gather(value, tiled=True):
@@ -361,8 +389,6 @@
         together[:, i * own:(i + 1) * own].reshape(device_count * own, width) for i in range(4)
     )
     gathered = together[:, 4 * own:].reshape(device_count, extra * width).astype(F32)
-    w_up = gather(up_weight)
-    w_down = gather(down_weight)
     full_vectors = []
     place = 0
     for size in sizes:
@@ -370,14 +396,23 @@
         place += size
     q_b, v_b, o_b, g1, s1, d_b, g2, s2, u_b = full_vectors
     valid_count = jnp.sum(gathered[:, place] * 64.0 + gathered[:, place + 1])
+    up_own = up_weight.shape[0]
+    down_own = down_weight.shape[0]
+    chunks = up_weight.shape[1] // width
+    ffn = gather(
+        jnp.concatenate([down_weight] + [up_weight[:, c * width:(c + 1) * width] for c in range(chunks)], axis=0), False
+    )
+    w_down = ffn[:, :down_own].reshape(device_count * down_own, width)
+    w_up = jnp.concatenate(
+        [ffn[:, down_own + c * up_own:down_own + (c + 1) * up_own] for c in range(chunks)], axis=2
+    ).reshape(device_count * up_own, chunks * width)
 
     outgoing = slot_positions(route_to, rows_dev, slot_rows, device_count)
     incoming = slot_positions(anchor, rows_dev, slot_rows, device_count)
-    send_order = invert(outgoing)
-    back_order = invert(incoming)
-    tokens_out, incoming, back_order = lax.optimization_barrier((tokens[send_order], incoming, back_order))
-    x = exchange(tokens_out, device_count)[incoming]
-    target = exchange(teacher[send_order], device_count)[incoming]
+    tokens_out, incoming = lax.optimization_barrier((permute(outgoing, tokens, False), incoming))
+    x = permute(incoming, exchange(tokens_out, device_count), True)
+    teacher_out = permute(outgoing, teacher, False)
+    target = permute(incoming, exchange(teacher_out, device_count), True)
 
     queries = ((matmul(x, w_q) + q_b) * 0.125).astype(BF16)
     keys = matmul(x, w_k).astype(BF16)
@@ -391,8 +426,7 @@
     grad_s2, grad_g2, grad_d_b, grad_s1, grad_g1, grad_o_b = (sums[i] for i in range(6))
     squares = jnp.sum(sums[6])
     grad_u_b = up_sums[0]
-    states_out = states_routed[back_order]
-    states = exchange(states_out, device_count)[outgoing]
+    states = permute(outgoing, exchange(permute(incoming, states_routed, False), device_count), True)
     grad_w_down = cross_rows(act_low, down_grad).astype(BF16)
     grad_w_up = cross_rows(hidden_low, up_grad).astype(BF16)
     up_own = up_weight.shape[0]
@@ -417,7 +451,7 @@
     dq, dk, dv, block = lax.optimization_barrier((dq, dk, dv, block))
     share_att = scatter_sum(block).astype(F32)
     rows_grad = (grad_pre_first + contract_last(dq, w_q) + contract_last(dk, w_k) + contract_last(dv, w_v)).astype(BF16)
-    token_grad = exchange(rows_grad[back_order], device_count)[outgoing]
+    token_grad = permute(outgoing, exchange(permute(incoming, rows_grad, False), device_count), True)
     grad_vectors = (grad_q_b, grad_v_b, grad_o_b, grad_g1, grad_s1, grad_d_b, grad_g2, grad_s2, grad_u_b)
     total_block = jnp.broadcast_to(squares.reshape(1, 1), (device_count, 1))
     grad_used = sum(sizes) + 1

time: 848 us -> 866 us (1.021)
  Pallas kernels: 202 us -> 295 us
  local copies, waits for them, and re-layouts: 139 us -> 49.8 us
  waiting for transfers between devices: 359 us -> 380 us
    pallas_call x0 -> x8, Pallas kernels: none -> 92.6 us  [permute(): pl.pallas_call(pick_kernel if pick else place_kernel, grid=(count // TILE...]
    gather x8 -> x0, local copies, waits for them, and re-layouts: 87.2 us -> none  [the longest x2 24.7 us: layer_step(): target = exchange(teacher[send_order], device_count)[incoming]]
    all_to_all x4, waiting for transfers between devices: 317 us -> 338 us  [exchange(): slots = lax.all_to_all(slots, 'dp', split_axis=0, concat_axis=0, tiled=True)]
    scatter x2 -> x0, local copies, waits for them, and re-layouts: 16.7 us -> none  [invert(): jnp.zeros_like(positions).at[positions]]
    unnamed x55 -> x63, local copies, waits for them, and re-layouts: 14.5 us -> 23.4 us
  transfers between devices with their start and end apart: 10 -> 9, of which waited for: 5 -> 5; matrix products, arithmetic and copies ran while one was open for 20% -> 7% of each run, Pallas kernels for 6% -> 17%
where the time goes in v5:
time: 866 us; the launch traced here: 860 us
  waiting for transfers between devices  380 us (44%)
  Pallas kernels  295 us (34%)
  matrix products  66.5 us (8%)
  local copies, waits for them, and re-layouts  49.8 us (6%)
  other arithmetic  24.7 us (3%)
  starting transfers between devices  24 us (3%)
  between operations  20.6 us (2%)
    all_to_all x4, waiting for transfers between devices, exchange(): slots = lax.all_to_all(slots, 'dp', split_axis=0, concat_axis=0, tiled=True)  338 us
    pallas_call x8, Pallas kernels, permute(): pl.pallas_call(pick_kernel if pick else place_kernel, grid=(count // TILE...  92.6 us
    pallas_call x1, Pallas kernels, attend_back(): pl.pallas_call(attend_back_kernel, grid=(micro, PAIRS), in_specs=[wide, w...  79.2 us
    pallas_call x1, Pallas kernels, middle(): pl.pallas_call(middle_kernel, grid=(rows // TILE,), in_specs=[row, row, r...  70.8 us
    pallas_call x1, Pallas kernels, attend(): pl.pallas_call(attend_kernel, grid=(micro, PAIRS), in_specs=[wide, wide,...  52.3 us
    reduce_scatter x2, waiting for transfers between devices, scatter_sum(): return lax.psum_scatter(value, 'dp', scatter_dimension=0, tiled=False)  41.2 us
    dot_general x6, matrix products, cross_rows(): lax.dot_general(left, right, (((0,), (0,)), ((), ())), preferred_element_...  38 us
    unnamed x63, local copies, waits for them, and re-layouts  23.4 us
  transfers between devices with their start and end apart: 9, of which 5 were waited for; matrix products, arithmetic and copies ran while one was open for 7% of the time, Pallas kernels for 17%

profile of v5, /device:TPU:0, one launch (start us, length us, event | category | flops | bytes accessed | tf_op | source)
XLA Modules:
  0.0 860.3 jit_solution(17680925958836571401)
XLA Ops:
  14.2 6.1 concatenate.32
  30.7 10.7 %place.4 = bf16[2048,768]{1,0:T(8,128)(2,1)} custom-call(s32[1,2048]{1,0:T(1,128)} %bitcast.146, bf16[2048,768]{1,0:T(8,128)(2,1)} %rows_ref.2), custom_call_target="tpu_custom_call" | custom-call | flops 6442450944 | bytes 6291456 | tf_op jit(solution)/shard_map/place/pallas_call | solution.py:320
  41.4 7.3 all-to-all-start
  48.7 10.7 %place.5 = bf16[2048,768]{1,0:T(8,128)(2,1)} custom-call(s32[1,2048]{1,0:T(1,128)} %bitcast.147, bf16[2048,768]{1,0:T(8,128)(2,1)} %rows_ref.3), custom_call_target="tpu_custom_call" | custom-call | flops 6442450944 | bytes 6291456 | tf_op jit(solution)/shard_map/place/pallas_call | solution.py:320
  59.4 87.3 %all-to-all-done = bf16[32,64,768]{2,1,0:T(8,128)(2,1)S(1)} async-done(((bf16[32,64,768]{2,1,0:T(8,128)(2,1)}), bf16[32,64,768]{2,1,0:T(8,128)(2,1)S(1)}, u32[]{:S(2)}, u32[]{:S(2)}) %all-to-all-start) | async-done | bytes 3145760 | tf_op jit(solution)/shard_map/all_to_all | solution.py:344
  157.0 12.6 %pick.4.x_ref = bf16[2048,768]{1,0:T(8,128)(2,1)} custom-call(s32[1,2048]{1,0:T(1,128)} %bitcast.150, bf16[2048,768]{1,0:T(8,128)(2,1)} %bitcast.121), custom_call_target="tpu_custom_call" | custom-call | flops 6442450944 | bytes 6291456 | tf_op jit(solution)/shard_map/pick/pallas_call | solution.py:320
  169.6 87.9 %all-to-all-done.1 = bf16[32,64,768]{2,1,0:T(8,128)(2,1)} async-done(((bf16[32,64,768]{2,1,0:T(8,128)(2,1)}), bf16[32,64,768]{2,1,0:T(8,128)(2,1)}, u32[]{:S(2)}, u32[]{:S(2)}) %all-to-all-start.1) | async-done | bytes 3145760 | tf_op jit(solution)/shard_map/all_to_all | solution.py:344
  257.5 12.4 %pick.5.target_ref = bf16[2048,768]{1,0:T(8,128)(2,1)} custom-call(s32[1,2048]{1,0:T(1,128)} %bitcast.151, bf16[2048,768]{1,0:T(8,128)(2,1)} %bitcast.20.rows_ref), custom_call_target="tpu_custom_call" | custom-call | flops 6442450944 | bytes 6291456 | tf_op jit(solution)/shard_map/pick/pallas_call | solution.py:320
  290.3 52.3 %attend.1 = (bf16[2048,768]{1,0:T(8,128)(2,1)}, f32[2,6,16,1024]{3,2,1,0:T(8,128)}) custom-call(bf16[2048,768]{1,0:T(8,128)(2,1)} %multiply_convert_fusion.q_ref, bf16[2048,768]{1,0:T(8,128)(2,1)} %convolution_convert_fusion.2.k_ref, bf16[2048,768]{1,0:T(8,128)(2,1)} %add_convert_fusion.1.v_ref, bf16[2048,128]{1,0:T(8,128)(2,1)} %bitcast.140, ...), custom_call_target="tpu_custom_call" | custom-call | flops 6442450944 | bytes 12582912 | tf_op jit(solution)/shard_map/attend/pallas_call | solution.py:101
  352.7 70.8 %middle.1 = (bf16[2048,768]{1,0:T(8,128)(2,1)}, bf16[2048,768]{1,0:T(8,128)(2,1)}, bf16[2048,3072]{1,0:T(8,128)(2,1)}, bf16[2048,768]{1,0:T(8,128)(2,1)}, bf16[2...) custom-call(bf16[2048,768]{1,0:T(8,128)(2,1)} %get-tuple-element.43., ...), custom_call_target="tpu_custom_call" | custom-call | flops 43486543872 | bytes 66060288 | tf_op jit(solution)/shard_map/middle/pallas_call | solution.py:260
  423.5 14.3 %convolution_convert_fusion = bf16[768,3072]{1,0:T(8,128)(2,1)S(1)} fusion(bf16[2048,768]{1,0:T(8,128)(2,1)} %get-tuple-element.48, bf16[2048,3072]{1,0:T(8,128)(2,1)} %get-tuple-element.49), kind=kOutput, calls=%fused_computation.5 | convolution fusion | flops 9666035712 | bytes 20447232 | tf_op jit(solution)/shard_map/dot_general | solution.py:32
  439.7 11.0 %convolution_convert_fusion.1 = bf16[3072,768]{1,0:T(8,128)(2,1)S(1)} fusion(bf16[2048,3072]{1,0:T(8,128)(2,1)S(1)} %copy-done.20, bf16[2048,768]{1,0:T(8,128)(2,1)S(1)} %copy-done.21), kind=kOutput, calls=%fused_computation.6 | convolution fusion | flops 9666035712 | bytes 20447232 | tf_op jit(solution)/shard_map/dot_general | solution.py:32
  457.6 79.2 %attend_back.1 = (bf16[2048,768]{1,0:T(8,128)(2,1)}, bf16[2048,768]{1,0:T(8,128)(2,1)}, bf16[2048,768]{1,0:T(8,128)(2,1)}) custom-call(bf16[2048,768]{1,0:T(8,128)(2,1)} %multiply_convert_fusion.q_ref, bf16[2048,768]{1,0:T(8,128)(2,1)} %convolution_convert_fusion.2.k_ref, bf16[2048,768]{1,0:T(8,128)(2,1)} %add_convert_fusion.1.v_ref, ...), custom_call_target="tpu_custom_call" | custom-call | flops 16106127360 | bytes 22020096 | tf_op jit(solution)/shard_map/attend_back/pallas_call | solution.py:166
  536.8 4.7 convolution_convert_fusion.6
  565.9 5.3 fusion.30
  575.8 6.4 add_convert_fusion.rows_ref
  582.2 10.7 %place.7 = bf16[2048,768]{1,0:T(8,128)(2,1)} custom-call(s32[1,2048]{1,0:T(1,128)} %bitcast.152, bf16[2048,768]{1,0:T(8,128)(2,1)} %add_convert_fusion.rows_ref), custom_call_target="tpu_custom_call" | custom-call | flops 6442450944 | bytes 6291456 | tf_op jit(solution)/shard_map/place/pallas_call | solution.py:320
  592.9 5.8 all-to-all-start.4
  599.3 10.6 %place.6 = bf16[2048,768]{1,0:T(8,128)(2,1)} custom-call(s32[1,2048]{1,0:T(1,128)} %bitcast.153, bf16[2048,768]{1,0:T(8,128)(2,1)} %get-tuple-element.44.rows_ref), custom_call_target="tpu_custom_call" | custom-call | flops 6442450944 | bytes 6291456 | tf_op jit(solution)/shard_map/place/pallas_call | solution.py:320
  609.9 81.9 %all-to-all-done.4 = bf16[32,64,768]{2,1,0:T(8,128)(2,1)S(1)} async-done(((bf16[32,64,768]{2,1,0:T(8,128)(2,1)}), bf16[32,64,768]{2,1,0:T(8,128)(2,1)S(1)}, u32[]{:S(2)}, u32[]{:S(2)}) %all-to-all-start.4) | async-done | bytes 3145760 | tf_op jit(solution)/shard_map/all_to_all | solution.py:344
  700.2 12.4 %pick.7 = bf16[2048,768]{1,0:T(8,128)(2,1)} custom-call(s32[1,2048]{1,0:T(1,128)} %bitcast.148, bf16[2048,768]{1,0:T(8,128)(2,1)} %bitcast.123), custom_call_target="tpu_custom_call" | custom-call | flops 6442450944 | bytes 6291456 | tf_op jit(solution)/shard_map/pick/pallas_call | solution.py:320
  712.6 81.1 %all-to-all-done.2 = bf16[32,64,768]{2,1,0:T(8,128)(2,1)} async-done(((bf16[32,64,768]{2,1,0:T(8,128)(2,1)}), bf16[32,64,768]{2,1,0:T(8,128)(2,1)}, u32[]{:S(2)}, u32[]{:S(2)}) %all-to-all-start.2) | async-done | bytes 3145760 | tf_op jit(solution)/shard_map/all_to_all | solution.py:344
  793.7 12.4 %pick.6 = bf16[2048,768]{1,0:T(8,128)(2,1)} custom-call(s32[1,2048]{1,0:T(1,128)} %bitcast.149, bf16[2048,768]{1,0:T(8,128)(2,1)} %bitcast.26.rows_ref), custom_call_target="tpu_custom_call" | custom-call | flops 6442450944 | bytes 6291456 | tf_op jit(solution)/shard_map/pick/pallas_call | solution.py:320
  807.8 41.2 %reduce-scatter.5.cloned.1.call-done = bf16[1,192,768]{2,1,0:T(8,128)(2,1)} async-done(((bf16[32,192,768]{2,1,0:T(8,128)(2,1)}), bf16[1,192,768]{2,1,0:T(8,128)(2,1)}) %reduce-scatter.5.cloned.1.call-update) | async-done | bytes 294928 | tf_op jit(solution)/shard_map/reduce_scatter | solution.py:338
  (161 shorter events, 104.7 us)
Async XLA Ops:
  7.2 262.7 %all-gather.8.cloned.1.call-start = ((), (), s32[]{:S(2)}) async-start(), calls=%async_computation.10 | async-start | bytes 5271552 | tf_op jit(solution)/shard_map/all_gather | solution.py:334
  21.0 321.6 %all-gather.6.cloned.1.call-start = ((), (), s32[]{:S(2)}) async-start(), calls=%async_computation.9 | async-start | bytes 9732096 | tf_op jit(solution)/shard_map/all_gather | solution.py:334
  41.4 105.3 %all-to-all-start = ((bf16[32,64,768]{2,1,0:T(8,128)(2,1)}), bf16[32,64,768]{2,1,0:T(8,128)(2,1)S(1)}, u32[]{:S(2)}, u32[]{:S(2)}) async-start(bf16[32,64,768]{2,1,0:T(8,128)(2,1)} %bitcast.126), calls=%async_computation | async-start | bytes 6291456 | tf_op jit(solution)/shard_map/all_to_all | solution.py:344
  146.7 5.4 copy-start.13
  148.3 109.1 %all-to-all-start.1 = ((bf16[32,64,768]{2,1,0:T(8,128)(2,1)}), bf16[32,64,768]{2,1,0:T(8,128)(2,1)}, u32[]{:S(2)}, u32[]{:S(2)}) async-start(bf16[32,64,768]{2,1,0:T(8,128)(2,1)} %bitcast.122), calls=%async_computation.1 | async-start | bytes 6291456 | tf_op jit(solution)/shard_map/all_to_all | solution.py:344
  152.0 654.1 %reduce-scatter.3.cloned.1.call-start = ((), (), s32[]{:S(2)}) async-start(), calls=%async_computation.7 | async-start | bytes 4866048 | tf_op jit(solution)/shard_map/reduce_scatter | solution.py:338
  274.6 3.8 copy-start.14
  278.4 4.0 copy-start.7
  278.4 4.0 copy-start.3
  278.4 7.9 copy-start.9
  342.6 5.1 copy-start.2
  423.5 14.6 %copy-start.20 = (bf16[2048,3072]{1,0:T(8,128)(2,1)S(1)}, bf16[2048,3072]{1,0:T(8,128)(2,1)}, u32[]{:S(2)}) copy-start(bf16[2048,3072]{1,0:T(8,128)(2,1)} %get-tuple-element.46) | copy-start | bytes 37748740
  457.6 79.2 %copy-start.15 = (bf16[2048,768]{1,0:T(8,128)(2,1)S(1)}, bf16[2048,768]{1,0:T(8,128)(2,1)}, u32[]{:S(2)}) copy-start(bf16[2048,768]{1,0:T(8,128)(2,1)} %pick.4.x_ref) | copy-start | bytes 9437188
  536.8 4.7 copy-start.1
  555.5 3.3 copy-start.12
  562.4 30.5 %all-to-all-start.3 = ((f32[32,1,384]{2,1,0:T(1,128)}), f32[32,1,384]{2,1,0:T(1,128)S(1)}, u32[]{:S(2)}, u32[]{:S(2)}) async-start(f32[32,1,384]{2,1,0:T(1,128)} %all_to_all.21), calls=%async_computation.3 | async-start | bytes 98304 | tf_op jit(solution)/shard_map/all_to_all | solution.py:462
  565.9 5.3 copy-start.8
  565.9 5.3 copy-start.17
  565.9 9.9 %slice-start = ((s8[6291456]{0:T(1024)(128)(4,1)}), s8[4194304]{0:T(1024)(128)(4,1)S(1)}, s32[]{:S(2)}) async-start(s8[6291456]{0:T(1024)(128)(4,1)} %bitcast.110), calls=%async_computation.11 | async-start | bytes 8388608
  571.2 4.6 slice-start.1
  571.2 4.6 copy-start.4
  592.9 98.9 %all-to-all-start.4 = ((bf16[32,64,768]{2,1,0:T(8,128)(2,1)}), bf16[32,64,768]{2,1,0:T(8,128)(2,1)S(1)}, u32[]{:S(2)}, u32[]{:S(2)}) async-start(bf16[32,64,768]{2,1,0:T(8,128)(2,1)} %bitcast.125), calls=%async_computation.4 | async-start | bytes 6291456 | tf_op jit(solution)/shard_map/all_to_all | solution.py:344
  598.7 250.3 %reduce-scatter.5.cloned.1.call-start = ((), (), s32[]{:S(2)}) async-start(), calls=%async_computation.8 | async-start | bytes 9732096 | tf_op jit(solution)/shard_map/reduce_scatter | solution.py:338
  693.5 100.3 %all-to-all-start.2 = ((bf16[32,64,768]{2,1,0:T(8,128)(2,1)}), bf16[32,64,768]{2,1,0:T(8,128)(2,1)}, u32[]{:S(2)}, u32[]{:S(2)}) async-start(bf16[32,64,768]{2,1,0:T(8,128)(2,1)} %bitcast.124), calls=%async_computation.2 | async-start | bytes 6291456 | tf_op jit(solution)/shard_map/all_to_all | solution.py:344
  (9 other events, 17.8 us)
Sparse Core Ops, SparseCore 0:
  21.2 97.2 all-gather.7
  122.0 127.4 all-gather.5
  555.6 139.1 reduce-scatter.2
  700.5 148.4 reduce-scatter.4

commit v6 on v5

--- a/solution.py
+++ b/solution.py
@@ -184,24 +184,19 @@
     return jnp.sum(value, axis=-1, keepdims=True) * (1.0 / value.shape[-1])
 
 
-def middle_kernel(
-    att_ref, x_ref, target_ref, usable_ref, w_out_ref, w_up_ref, w_down_ref, vec_ref, ub_ref,
-    states_ref, hidden_ref, act_ref, down_ref, up_ref, first_ref, out_ref, attg_ref, sums_ref, ubsum_ref,
-    slope_ref,
+def ahead_kernel(
+    att_ref, x_ref, w_out_ref, w_up_ref, w_down_ref, vec_ref, ub_ref,
+    states_ref, hidden_ref, act_ref, slope_ref, n1_ref, r1_ref, n2_ref, r2_ref,
 ):
     width = x_ref.shape[1]
     chunks = w_up_ref.shape[1] // width
-    o_b, g1, s1, d_b, g2, s2, scale = (vec_ref[i:i + 1, :] for i in range(7))
-
-    @pl.when(pl.program_id(0) == 0)
-    def _():
-        sums_ref[...] = jnp.zeros_like(sums_ref)
-        ubsum_ref[...] = jnp.zeros_like(ubsum_ref)
-
+    o_b, g1, s1, d_b, g2, s2 = (vec_ref[i:i + 1, :] for i in range(6))
     pre_first = x_ref[...].astype(F32) + (matmul(att_ref[...], w_out_ref[...]) + o_b)
     center = pre_first - row_mean(pre_first)
     r1 = lax.rsqrt(row_mean(center * center) + EPSILON)
     n1 = center * r1
+    r1_ref[...] = r1
+    n1_ref[...] = n1
     hidden = n1 * g1 + s1
     hidden_low = hidden.astype(BF16)
     hidden_ref[...] = hidden_low
@@ -218,9 +213,26 @@
     center = total - row_mean(total)
     r2 = lax.rsqrt(row_mean(center * center) + EPSILON)
     n2 = center * r2
-    layer_out = n2 * g2 + s2
-    states_ref[...] = layer_out.astype(BF16)
-    misfit = jnp.where(usable_ref[...] > 0.5, layer_out - target_ref[...].astype(F32), 0.0)
+    r2_ref[...] = r2
+    n2_ref[...] = n2
+    states_ref[...] = (n2 * g2 + s2).astype(BF16)
+
+
+def return_kernel(
+    target_ref, usable_ref, slope_ref, n1_ref, r1_ref, n2_ref, r2_ref, w_out_ref, w_up_ref, w_down_ref, vec_ref,
+    down_ref, up_ref, first_ref, out_ref, attg_ref, sums_ref, ubsum_ref,
+):
+    width = target_ref.shape[1]
+    chunks = w_up_ref.shape[1] // width
+    _, g1, _, _, g2, s2, scale = (vec_ref[i:i + 1, :] for i in range(7))
+
+    @pl.when(pl.program_id(0) == 0)
+    def _():
+        sums_ref[...] = jnp.zeros_like(sums_ref)
+        ubsum_ref[...] = jnp.zeros_like(ubsum_ref)
+
+    n1, r1, n2, r2 = n1_ref[...], r1_ref[...], n2_ref[...], r2_ref[...]
+    misfit = jnp.where(usable_ref[...] > 0.5, n2 * g2 + s2 - target_ref[...].astype(F32), 0.0)
     grad_out = misfit * scale
     u = grad_out * g2
     grad_second = r2 * (u - row_mean(u) - n2 * row_mean(u * n2))
@@ -249,36 +261,62 @@
     attg_ref[...] = contract_last(out_grad, w_out_ref[...]).astype(BF16)
 
 
-def middle(attended, x, target, usable, w_out, w_up, w_down, vectors, u_b):
+def row_specs(width, wide):
+    row = pl.BlockSpec((TILE, width), lambda i: (i, 0))
+    long = pl.BlockSpec((TILE, wide), lambda i: (i, 0))
+    thin = pl.BlockSpec((TILE, 1), lambda i: (i, 0))
+    whole = lambda array: pl.BlockSpec(array.shape, lambda i: (0, 0), pipeline_mode=pl.Buffered(1))
+    return row, long, thin, whole
+
+
+def middle_ahead(attended, x, w_out, w_up, w_down, vectors, u_b):
     rows, width = x.shape
     wide = w_up.shape[1]
-    row = pl.BlockSpec((TILE, width), lambda i: (i, 0))
-    long = pl.BlockSpec((TILE, wide), lambda i: (i, 0))
-    whole = lambda shape: pl.BlockSpec(shape, lambda i: (0, 0), pipeline_mode=pl.Buffered(1))
-    still = lambda shape: pl.BlockSpec(shape, lambda i: (0, 0))
+    row, long, thin, whole = row_specs(width, wide)
     shape = jax.ShapeDtypeStruct
     return pl.pallas_call(
-        middle_kernel,
+        ahead_kernel,
         grid=(rows // TILE,),
-        in_specs=[
-            row, row, row, pl.BlockSpec((TILE, 1), lambda i: (i, 0)),
-            whole(w_out.shape), whole(w_up.shape), whole(w_down.shape), whole(vectors.shape), whole(u_b.shape),
-        ],
-        out_specs=[row, row, long, row, long, row, row, row, still((8, width)), still((8, wide))],
+        in_specs=[row, row, whole(w_out), whole(w_up), whole(w_down), whole(vectors), whole(u_b)],
+        out_specs=[row, row, long, long, row, thin, row, thin],
         out_shape=(
             shape((rows, width), BF16), shape((rows, width), BF16), shape((rows, wide), BF16),
+            shape((rows, wide), BF16), shape((rows, width), F32), shape((rows, 1), F32),
+            shape((rows, width), F32), shape((rows, 1), F32),
+        ),
+        compiler_params=pltpu.CompilerParams(vmem_limit_bytes=58 << 20),
+        cost_estimate=pl.CostEstimate(
+            flops=2 * rows * width * (width + 2 * wide),
+            transcendentals=2 * rows * wide,
+            bytes_accessed=rows * (width * 16 + wide * 4) + 4 * wide * width,
+        ),
+        name="middle_ahead",
+    )(attended, x, w_out, w_up, w_down, vectors, u_b)
+
+
+def middle_back(target, usable, slope, n1, r1, n2, r2, w_out, w_up, w_down, vectors):
+    rows, width = target.shape
+    wide = w_up.shape[1]
+    row, long, thin, whole = row_specs(width, wide)
+    still = lambda dims: pl.BlockSpec(dims, lambda i: (0, 0))
+    shape = jax.ShapeDtypeStruct
+    return pl.pallas_call(
+        return_kernel,
+        grid=(rows // TILE,),
+        in_specs=[row, thin, long, row, thin, row, thin, whole(w_out), whole(w_up), whole(w_down), whole(vectors)],
+        out_specs=[row, long, row, row, row, still((8, width)), still((8, wide))],
+        out_shape=(
             shape((rows, width), BF16), shape((rows, wide), BF16), shape((rows, width), F32),
             shape((rows, width), BF16), shape((rows, width), BF16), shape((8, width), F32), shape((8, wide), F32),
         ),
-        scratch_shapes=[pltpu.VMEM((TILE, wide), BF16)],
         compiler_params=pltpu.CompilerParams(vmem_limit_bytes=58 << 20),
         cost_estimate=pl.CostEstimate(
-            flops=2 * rows * width * (2 * width + 4 * wide),
-            transcendentals=2 * rows * wide,
+            flops=2 * rows * width * (width + 2 * wide),
+            transcendentals=0,
             bytes_accessed=rows * (width * 20 + wide * 4) + 4 * wide * width,
         ),
-        name="middle",
-    )(attended, x, target, usable, w_out, w_up, w_down, vectors, u_b)
+        name="middle_back",
+    )(target, usable, slope, n1, r1, n2, r2, w_out, w_up, w_down, vectors)
 
 
 def slot_positions(targets, rows_dev, slot_rows, device_count):
@@ -420,9 +458,12 @@
     attended, lse = attend(queries, keys, values, asked, barred)
     scale = rows_dev * device_count * 2.0 / valid_count
     vectors = jnp.stack([o_b, g1, s1, d_b, g2, s2, jnp.full((width,), scale, F32), jnp.zeros((width,), F32)])
-    (
-        states_routed, hidden_low, act_low, down_grad, up_grad, grad_pre_first, out_grad, attended_grad, sums, up_sums,
-    ) = middle(attended, x, target, usable.astype(F32)[:, None], w_out, w_up, w_down, vectors, u_b[None])
+    states_routed, hidden_low, act_low, slope, n1, r1, n2, r2 = middle_ahead(
+        attended, x, w_out, w_up, w_down, vectors, u_b[None]
+    )
+    down_grad, up_grad, grad_pre_first, out_grad, attended_grad, sums, up_sums = middle_back(
+        target, usable.astype(F32)[:, None], slope, n1, r1, n2, r2, w_out, w_up, w_down, vectors
+    )
     grad_s2, grad_g2, grad_d_b, grad_s1, grad_g1, grad_o_b = (sums[i] for i in range(6))
     squares = jnp.sum(sums[6])
     grad_u_b = up_sums[0]
@@ -446,9 +487,8 @@
     dq = dq * jnp.asarray(0.125, BF16)
     grad_q_b = column_sum(dq)
     grad_v_b = column_sum(dv)
-    blocks = [cross_rows(x, dq).astype(BF16), cross_rows(x, dk).astype(BF16), cross_rows(x, dv).astype(BF16), grad_w_out]
+    blocks = [cross_rows(x, grad).astype(BF16) for grad in (dq, dk, dv)] + [grad_w_out]
     block = jnp.concatenate([g.reshape(device_count, own, width) for g in blocks], axis=1)
-    dq, dk, dv, block = lax.optimization_barrier((dq, dk, dv, block))
     share_att = scatter_sum(block).astype(F32)
     rows_grad = (grad_pre_first + contract_last(dq, w_q) + contract_last(dk, w_k) + contract_last(dv, w_v)).astype(BF16)
     token_grad = permute(outgoing, exchange(permute(incoming, rows_grad, False), device_count), True)

time: 866 us -> 868 us (level)
    pallas_call x1 -> x2, Pallas kernels: 70.8 us -> 78.6 us  [the longest x1 39.3 us: middle_ahead(): pl.pallas_call(ahead_kernel, grid=(rows // TILE,), in_specs=[row, row, wh...]
    unnamed x63 -> x59, local copies, waits for them, and re-layouts: 23.4 us -> 22.3 us
where the time goes in v6:
time: 868 us; the launch traced here: 862 us
  waiting for transfers between devices  379 us (44%)
  Pallas kernels  303 us (35%)
  matrix products  63.7 us (7%)
  local copies, waits for them, and re-layouts  48.8 us (6%)
  starting transfers between devices  24 us (3%)
  other arithmetic  22.9 us (3%)
  between operations  20.6 us (2%)
    all_to_all x4, waiting for transfers between devices, exchange(): slots = lax.all_to_all(slots, 'dp', split_axis=0, concat_axis=0, tiled=True)  338 us
    pallas_call x8, Pallas kernels, permute(): pl.pallas_call(pick_kernel if pick else place_kernel, grid=(count // TILE...  92.7 us
    pallas_call x1, Pallas kernels, attend_back(): pl.pallas_call(attend_back_kernel, grid=(micro, PAIRS), in_specs=[wide, w...  79.2 us
    pallas_call x1, Pallas kernels, attend(): pl.pallas_call(attend_kernel, grid=(micro, PAIRS), in_specs=[wide, wide,...  52.3 us
    reduce_scatter x2, waiting for transfers between devices, scatter_sum(): return lax.psum_scatter(value, 'dp', scatter_dimension=0, tiled=False)  40.9 us
    pallas_call x1, Pallas kernels, middle_ahead(): pl.pallas_call(ahead_kernel, grid=(rows // TILE,), in_specs=[row, row, wh...  39.3 us
    pallas_call x1, Pallas kernels, middle_back(): pl.pallas_call(return_kernel, grid=(rows // TILE,), in_specs=[row, thin,...  39.3 us
    dot_general x6, matrix products, cross_rows(): lax.dot_general(left, right, (((0,), (0,)), ((), ())), preferred_element_...  37.1 us
  transfers between devices with their start and end apart: 9, of which 5 were waited for; matrix products, arithmetic and copies ran while one was open for 7% of the time, Pallas kernels for 17%

profile of v6, /device:TPU:0, one launch (start us, length us, event | category | flops | bytes accessed | tf_op | source)
XLA Modules:
  0.0 862.3 jit_solution(17222271015663903381)
XLA Ops:
  14.2 6.1 concatenate.32
  30.7 10.7 %place.4 = bf16[2048,768]{1,0:T(8,128)(2,1)} custom-call(s32[1,2048]{1,0:T(1,128)} %bitcast.146, bf16[2048,768]{1,0:T(8,128)(2,1)} %rows_ref.2), custom_call_target="tpu_custom_call" | custom-call | flops 6442450944 | bytes 6291456 | tf_op jit(solution)/shard_map/place/pallas_call | solution.py:358
  41.4 7.3 all-to-all-start
  48.7 10.7 %place.6 = bf16[2048,768]{1,0:T(8,128)(2,1)} custom-call(s32[1,2048]{1,0:T(1,128)} %bitcast.147, bf16[2048,768]{1,0:T(8,128)(2,1)} %rows_ref.3), custom_call_target="tpu_custom_call" | custom-call | flops 6442450944 | bytes 6291456 | tf_op jit(solution)/shard_map/place/pallas_call | solution.py:358
  59.4 87.3 %all-to-all-done = bf16[32,64,768]{2,1,0:T(8,128)(2,1)S(1)} async-done(((bf16[32,64,768]{2,1,0:T(8,128)(2,1)}), bf16[32,64,768]{2,1,0:T(8,128)(2,1)S(1)}, u32[]{:S(2)}, u32[]{:S(2)}) %all-to-all-start) | async-done | bytes 3145760 | tf_op jit(solution)/shard_map/all_to_all | solution.py:382
  157.0 12.6 %pick.4.x_ref = bf16[2048,768]{1,0:T(8,128)(2,1)} custom-call(s32[1,2048]{1,0:T(1,128)} %bitcast.150, bf16[2048,768]{1,0:T(8,128)(2,1)} %bitcast.120), custom_call_target="tpu_custom_call" | custom-call | flops 6442450944 | bytes 6291456 | tf_op jit(solution)/shard_map/pick/pallas_call | solution.py:358
  169.6 87.9 %all-to-all-done.2 = bf16[32,64,768]{2,1,0:T(8,128)(2,1)} async-done(((bf16[32,64,768]{2,1,0:T(8,128)(2,1)}), bf16[32,64,768]{2,1,0:T(8,128)(2,1)}, u32[]{:S(2)}, u32[]{:S(2)}) %all-to-all-start.2) | async-done | bytes 3145760 | tf_op jit(solution)/shard_map/all_to_all | solution.py:382
  257.5 12.4 %pick.6.target_ref = bf16[2048,768]{1,0:T(8,128)(2,1)} custom-call(s32[1,2048]{1,0:T(1,128)} %bitcast.151, bf16[2048,768]{1,0:T(8,128)(2,1)} %bitcast.26.rows_ref), custom_call_target="tpu_custom_call" | custom-call | flops 6442450944 | bytes 6291456 | tf_op jit(solution)/shard_map/pick/pallas_call | solution.py:358
  290.3 52.3 %attend.1 = (bf16[2048,768]{1,0:T(8,128)(2,1)}, f32[2,6,16,1024]{3,2,1,0:T(8,128)}) custom-call(bf16[2048,768]{1,0:T(8,128)(2,1)} %multiply_convert_fusion.q_ref, bf16[2048,768]{1,0:T(8,128)(2,1)} %convolution_convert_fusion.2.k_ref, bf16[2048,768]{1,0:T(8,128)(2,1)} %add_convert_fusion.1.v_ref, bf16[2048,128]{1,0:T(8,128)(2,1)} %bitcast.140, ...), custom_call_target="tpu_custom_call" | custom-call | flops 6442450944 | bytes 12582912 | tf_op jit(solution)/shard_map/attend/pallas_call | solution.py:101
  352.8 39.3 %middle_ahead.1 = (bf16[2048,768]{1,0:T(8,128)(2,1)}, bf16[2048,768]{1,0:T(8,128)(2,1)}, bf16[2048,3072]{1,0:T(8,128)(2,1)}, bf16[2048,3072]{1,0:T(8,128)(2,1)},...) custom-call(bf16[2048,768]{1,0:T(8,128)(2,1)} %get-tuple-element.44.att_ref, ...), custom_call_target="tpu_custom_call" | custom-call | flops 21743271936 | bytes 59768832 | tf_op jit(solution)/shard_map/middle_ahead/pallas_call | solution.py:277
  392.1 39.3 %middle_back.1 = (bf16[2048,768]{1,0:T(8,128)(2,1)}, bf16[2048,3072]{1,0:T(8,128)(2,1)}, f32[2048,768]{1,0:T(8,128)}, bf16[2048,768]{1,0:T(8,128)(2,1)}, bf16[20...) custom-call(bf16[2048,768]{1,0:T(8,128)(2,1)} %pick.6.target_ref, f32[2048,1]{1,0:T(8,128)} %bitcast.136, ...), custom_call_target="tpu_custom_call" | custom-call | flops 21743271936 | bytes 66060288 | tf_op jit(solution)/shard_map/middle_back/pallas_call | solution.py:303
  431.4 13.3 %convolution_convert_fusion = bf16[768,3072]{1,0:T(8,128)(2,1)S(1)} fusion(bf16[2048,768]{1,0:T(8,128)(2,1)S(1)} %copy-done.19, bf16[2048,3072]{1,0:T(8,128)(2,1)} %get-tuple-element.55), kind=kOutput, calls=%fused_computation.5 | convolution fusion | flops 9666035712 | bytes 20447232 | tf_op jit(solution)/shard_map/dot_general | solution.py:32
  446.7 11.0 %convolution_convert_fusion.1 = bf16[3072,768]{1,0:T(8,128)(2,1)S(1)} fusion(bf16[2048,3072]{1,0:T(8,128)(2,1)S(1)} %copy-done.20, bf16[2048,768]{1,0:T(8,128)(2,1)S(1)} %copy-done.21), kind=kOutput, calls=%fused_computation.6 | convolution fusion | flops 9666035712 | bytes 20447232 | tf_op jit(solution)/shard_map/dot_general | solution.py:32
  464.6 79.2 %attend_back.1 = (bf16[2048,768]{1,0:T(8,128)(2,1)}, bf16[2048,768]{1,0:T(8,128)(2,1)}, bf16[2048,768]{1,0:T(8,128)(2,1)}) custom-call(bf16[2048,768]{1,0:T(8,128)(2,1)} %multiply_convert_fusion.q_ref, bf16[2048,768]{1,0:T(8,128)(2,1)} %convolution_convert_fusion.2.k_ref, bf16[2048,768]{1,0:T(8,128)(2,1)} %add_convert_fusion.1.v_ref, ...), custom_call_target="tpu_custom_call" | custom-call | flops 16106127360 | bytes 22020096 | tf_op jit(solution)/shard_map/attend_back/pallas_call | solution.py:166
  570.1 5.2 fusion.2
  578.2 6.4 add_convert_fusion.rows_ref
  584.6 10.7 %place.7 = bf16[2048,768]{1,0:T(8,128)(2,1)} custom-call(s32[1,2048]{1,0:T(1,128)} %bitcast.152, bf16[2048,768]{1,0:T(8,128)(2,1)} %add_convert_fusion.rows_ref), custom_call_target="tpu_custom_call" | custom-call | flops 6442450944 | bytes 6291456 | tf_op jit(solution)/shard_map/place/pallas_call | solution.py:358
  595.2 5.9 all-to-all-start.4
  601.7 10.6 %place.5 = bf16[2048,768]{1,0:T(8,128)(2,1)} custom-call(s32[1,2048]{1,0:T(1,128)} %bitcast.153, bf16[2048,768]{1,0:T(8,128)(2,1)} %get-tuple-element.45.rows_ref), custom_call_target="tpu_custom_call" | custom-call | flops 6442450944 | bytes 6291456 | tf_op jit(solution)/shard_map/place/pallas_call | solution.py:358
  612.3 81.7 %all-to-all-done.4 = bf16[32,64,768]{2,1,0:T(8,128)(2,1)S(1)} async-done(((bf16[32,64,768]{2,1,0:T(8,128)(2,1)}), bf16[32,64,768]{2,1,0:T(8,128)(2,1)S(1)}, u32[]{:S(2)}, u32[]{:S(2)}) %all-to-all-start.4) | async-done | bytes 3145760 | tf_op jit(solution)/shard_map/all_to_all | solution.py:382
  702.4 12.4 %pick.7 = bf16[2048,768]{1,0:T(8,128)(2,1)} custom-call(s32[1,2048]{1,0:T(1,128)} %bitcast.148, bf16[2048,768]{1,0:T(8,128)(2,1)} %bitcast.122), custom_call_target="tpu_custom_call" | custom-call | flops 6442450944 | bytes 6291456 | tf_op jit(solution)/shard_map/pick/pallas_call | solution.py:358
  714.8 81.1 %all-to-all-done.1 = bf16[32,64,768]{2,1,0:T(8,128)(2,1)} async-done(((bf16[32,64,768]{2,1,0:T(8,128)(2,1)}), bf16[32,64,768]{2,1,0:T(8,128)(2,1)}, u32[]{:S(2)}, u32[]{:S(2)}) %all-to-all-start.1) | async-done | bytes 3145760 | tf_op jit(solution)/shard_map/all_to_all | solution.py:382
  795.9 12.5 %pick.5 = bf16[2048,768]{1,0:T(8,128)(2,1)} custom-call(s32[1,2048]{1,0:T(1,128)} %bitcast.149, bf16[2048,768]{1,0:T(8,128)(2,1)} %bitcast.24.rows_ref), custom_call_target="tpu_custom_call" | custom-call | flops 6442450944 | bytes 6291456 | tf_op jit(solution)/shard_map/pick/pallas_call | solution.py:358
  810.1 40.9 %reduce-scatter.5.cloned.1.call-done = bf16[1,192,768]{2,1,0:T(8,128)(2,1)} async-done(((bf16[32,192,768]{2,1,0:T(8,128)(2,1)}), bf16[1,192,768]{2,1,0:T(8,128)(2,1)}) %reduce-scatter.5.cloned.1.call-update) | async-done | bytes 294928 | tf_op jit(solution)/shard_map/reduce_scatter | solution.py:376
  (156 shorter events, 104.9 us)
Async XLA Ops:
  7.2 262.7 %all-gather.8.cloned.1.call-start = ((), (), s32[]{:S(2)}) async-start(), calls=%async_computation.10 | async-start | bytes 5271552 | tf_op jit(solution)/shard_map/all_gather | solution.py:372
  21.0 321.6 %all-gather.6.cloned.1.call-start = ((), (), s32[]{:S(2)}) async-start(), calls=%async_computation.9 | async-start | bytes 9732096 | tf_op jit(solution)/shard_map/all_gather | solution.py:372
  41.4 105.3 %all-to-all-start = ((bf16[32,64,768]{2,1,0:T(8,128)(2,1)}), bf16[32,64,768]{2,1,0:T(8,128)(2,1)S(1)}, u32[]{:S(2)}, u32[]{:S(2)}) async-start(bf16[32,64,768]{2,1,0:T(8,128)(2,1)} %bitcast.125), calls=%async_computation | async-start | bytes 6291456 | tf_op jit(solution)/shard_map/all_to_all | solution.py:382
  146.7 5.4 copy-start.12
  148.3 109.1 %all-to-all-start.2 = ((bf16[32,64,768]{2,1,0:T(8,128)(2,1)}), bf16[32,64,768]{2,1,0:T(8,128)(2,1)}, u32[]{:S(2)}, u32[]{:S(2)}) async-start(bf16[32,64,768]{2,1,0:T(8,128)(2,1)} %bitcast.121), calls=%async_computation.2 | async-start | bytes 6291456 | tf_op jit(solution)/shard_map/all_to_all | solution.py:382
  152.0 656.4 %reduce-scatter.3.cloned.1.call-start = ((), (), s32[]{:S(2)}) async-start(), calls=%async_computation.7 | async-start | bytes 4866048 | tf_op jit(solution)/shard_map/reduce_scatter | solution.py:376
  274.6 3.9 copy-start.13
  278.4 4.0 copy-start.6
  278.4 4.0 copy-start.2
  278.4 7.9 copy-start.8
  342.6 5.1 copy-start.1
  392.1 39.3 %copy-start.19 = (bf16[2048,768]{1,0:T(8,128)(2,1)S(1)}, bf16[2048,768]{1,0:T(8,128)(2,1)}, u32[]{:S(2)}) copy-start(bf16[2048,768]{1,0:T(8,128)(2,1)} %get-tuple-element.54) | copy-start | bytes 9437188
  431.4 13.7 %copy-start.20 = (bf16[2048,3072]{1,0:T(8,128)(2,1)S(1)}, bf16[2048,3072]{1,0:T(8,128)(2,1)}, u32[]{:S(2)}) copy-start(bf16[2048,3072]{1,0:T(8,128)(2,1)} %get-tuple-element.52) | copy-start | bytes 37748740
  464.6 79.3 %copy-start.14 = (bf16[2048,768]{1,0:T(8,128)(2,1)S(1)}, bf16[2048,768]{1,0:T(8,128)(2,1)}, u32[]{:S(2)}) copy-start(bf16[2048,768]{1,0:T(8,128)(2,1)} %pick.4.x_ref) | copy-start | bytes 9437188
  543.9 4.7 copy-start.16
  551.3 2.8 copy-start.18
  559.7 3.3 copy-start.11
  566.6 28.7 %all-to-all-start.3 = ((f32[32,1,384]{2,1,0:T(1,128)}), f32[32,1,384]{2,1,0:T(1,128)S(1)}, u32[]{:S(2)}, u32[]{:S(2)}) async-start(f32[32,1,384]{2,1,0:T(1,128)} %all_to_all.21), calls=%async_computation.3 | async-start | bytes 98304 | tf_op jit(solution)/shard_map/all_to_all | solution.py:502
  570.1 5.2 copy-start.7
  570.1 5.2 copy-start.17
  575.4 2.8 copy-start.3
  595.2 98.8 %all-to-all-start.4 = ((bf16[32,64,768]{2,1,0:T(8,128)(2,1)}), bf16[32,64,768]{2,1,0:T(8,128)(2,1)S(1)}, u32[]{:S(2)}, u32[]{:S(2)}) async-start(bf16[32,64,768]{2,1,0:T(8,128)(2,1)} %bitcast.124), calls=%async_computation.4 | async-start | bytes 6291456 | tf_op jit(solution)/shard_map/all_to_all | solution.py:382
  601.1 249.9 %reduce-scatter.5.cloned.1.call-start = ((), (), s32[]{:S(2)}) async-start(), calls=%async_computation.8 | async-start | bytes 9732096 | tf_op jit(solution)/shard_map/reduce_scatter | solution.py:376
  695.7 100.2 %all-to-all-start.1 = ((bf16[32,64,768]{2,1,0:T(8,128)(2,1)}), bf16[32,64,768]{2,1,0:T(8,128)(2,1)}, u32[]{:S(2)}, u32[]{:S(2)}) async-start(bf16[32,64,768]{2,1,0:T(8,128)(2,1)} %bitcast.123), calls=%async_computation.1 | async-start | bytes 6291456 | tf_op jit(solution)/shard_map/all_to_all | solution.py:382
  (7 other events, 12.0 us)
Sparse Core Ops, SparseCore 0:
  21.2 97.2 all-gather.7
  122.0 126.2 all-gather.5
  559.8 137.2 reduce-scatter.2
  702.8 148.1 reduce-scatter.4
